TPU v7x, 32 devices: a whole 2x2x4 slice. The times are simulated.
32 devices in a mesh: dp: 8 (over z, x), tensor: 4 (over y, core).
Axes of the slice: x: 2, y: 2, z: 4, core: 2. Of those that a mesh axis runs over, the one named last changes fastest.
Arguments:
- incoming_signals: bfloat16 [4096, 2048], P(('dp', 'tensor')), may hold values from -6 to 6
- loss_sensitivity: bfloat16 [4096, 2048], P(('dp', 'tensor')), may hold values from -6 to 6
- token_counts_per_slot: int32 [8], P('dp'), may hold values from 1 to 512, as said below
- leading_norm_multiplier: bfloat16 [2048], P('dp'), may hold values from 0.099609375 to 1.8984375
- leading_norm_offset: bfloat16 [2048], P('dp'), may hold values from -1.5 to 1.5
- question_projection: bfloat16 [2048, 2048], P('dp', 'tensor'), may hold values from -0.125 to 0.125
- lookup_projection: bfloat16 [2048, 2048], P('dp', 'tensor'), may hold values from -0.125 to 0.125
- content_projection: bfloat16 [2048, 4096], P('dp', 'tensor'), may hold values from -0.125 to 0.125
- silu_switch_projection: bfloat16 [2048, 4096], P('dp', 'tensor'), may hold values from -0.125 to 0.125
- retention_result_projection: bfloat16 [4096, 2048], P('tensor', 'dp'), may hold values from -0.09375 to 0.09375
- trailing_norm_multiplier: bfloat16 [2048], P('dp'), may hold values from 0.099609375 to 1.8984375
- trailing_norm_offset: bfloat16 [2048], P('dp'), may hold values from -1.5 to 1.5
- feedforward_switch_projection: bfloat16 [2048, 4096], P('dp', 'tensor'), may hold values from -0.125 to 0.125
- expanding_projection: bfloat16 [2048, 4096], P('dp', 'tensor'), may hold values from -0.125 to 0.125
- contracting_projection: bfloat16 [4096, 2048], P('tensor', 'dp'), may hold values from -0.09375 to 0.09375
Outputs:
- layer_output: bfloat16 [4096, 2048], P(('dp', 'tensor'))
- input_delta: float32 [4096, 2048], P(('dp', 'tensor'))
- before_scale_gradient: float32 [2048], P('dp')
- before_bias_gradient: float32 [2048], P('dp')
- query_gradient: float32 [2048, 2048], P('dp', 'tensor')
- key_gradient: float32 [2048, 2048], P('dp', 'tensor')
- value_gradient: float32 [2048, 4096], P('dp', 'tensor')
- swish_gradient: float32 [2048, 4096], P('dp', 'tensor')
- output_gradient: float32 [4096, 2048], P('tensor', 'dp')
- after_scale_gradient: float32 [2048], P('dp')
- after_bias_gradient: float32 [2048], P('dp')
- gate_gradient: float32 [2048, 4096], P('dp', 'tensor')
- up_gradient: float32 [2048, 4096], P('dp', 'tensor')
- down_gradient: float32 [4096, 2048], P('tensor', 'dp')
Inputs may be any that keep to these rules, and one draw needn't show every extreme that they name: token_counts_per_slot[s] counts the valid leading rows of slot s, the slot being 512 consecutive rows; at least one sequence fills its slot.
All inputs are finite; a program needn't handle non-finite values.
Results may differ from a plain program's by a relative error of at most 0.024.
Values may be sent and summed in bfloat16 or wider, within the bound.
A program may use at most 192 MiB of HBM per device.

v0:
```python
import jax
import jax.numpy as jnp
from jax import lax
from jax.sharding import PartitionSpec as P

KEY_DIM = 256
VAL_DIM = 512
SEQ_LEN = 512


EPSILON = 1e-05
GROUP_EPSILON = 0.1


def normalize(values, epsilon):
    centre = values - jnp.mean(values, axis=-1, keepdims=True)
    inverse = lax.rsqrt(jnp.mean(centre * centre, axis=-1, keepdims=True) + epsilon)
    return (centre * inverse, inverse)


def normalize_back(upstream, normed, inverse):
    return inverse * (
        upstream
        - jnp.mean(upstream, axis=-1, keepdims=True)
        - normed * jnp.mean(upstream * normed, axis=-1, keepdims=True)
    )


def rotate_half(values):
    middle = values.shape[-1] // 2
    return jnp.concatenate([-values[..., middle:], values[..., :middle]], axis=-1)


def rotary_tables(span, columns):
    middle = columns // 2
    places = jnp.arange(span, dtype=jnp.int32).astype(jnp.float32)
    spectrum = 10000.0 ** (-jnp.arange(middle, dtype=jnp.int32).astype(jnp.float32) / middle)
    angles = places[:, None] * spectrum[None, :]
    angles = jnp.concatenate([angles, angles], axis=1)
    return (jnp.cos(angles)[None, :, None, :], jnp.sin(angles)[None, :, None, :])


def decay_table(span, head_ids):
    log_rates = jnp.log(1.0 - jnp.exp2(-5.0 - head_ids.astype(jnp.float32)))
    places = jnp.arange(span, dtype=jnp.int32)
    offsets = places[:, None] - places[None, :]
    decayed = jnp.exp(jnp.maximum(offsets, 0).astype(jnp.float32)[None] * log_rates[:, None, None])
    return jnp.where(offsets[None] >= 0, decayed, 0.0)


def gelu_tanh(values):
    return jax.nn.gelu(values, approximate=True)


def matmul(left, right):
    return jnp.dot(left, right, preferred_element_type=jnp.float32)


def per_device(
    incoming_signals,
    loss_sensitivity,
    token_counts_per_slot,
    leading_norm_multiplier,
    leading_norm_offset,
    question_projection,
    lookup_projection,
    content_projection,
    silu_switch_projection,
    retention_result_projection,
    trailing_norm_multiplier,
    trailing_norm_offset,
    feedforward_switch_projection,
    expanding_projection,
    contracting_projection,
):
    local_rows = incoming_signals.shape[0]
    heads_here = question_projection.shape[1] // KEY_DIM
    slots_here = token_counts_per_slot.shape[0]
    tensor_rank = lax.axis_index("tensor")
    row_ids = tensor_rank * local_rows + jnp.arange(local_rows, dtype=jnp.int32)
    slot_match = (row_ids // SEQ_LEN)[:, None] == jnp.arange(slots_here, dtype=jnp.int32)[None, :]
    row_lengths = jnp.sum(jnp.where(slot_match, token_counts_per_slot[None, :], 0), axis=1)
    valid_rows = (row_ids % SEQ_LEN < row_lengths)[:, None]
    pre_scale, pre_shift, query_full, key_full, value_full, swish_full, output_full = (
        lax.all_gather(leading_norm_multiplier, "dp", axis=0, tiled=True),
        lax.all_gather(leading_norm_offset, "dp", axis=0, tiled=True),
        lax.all_gather(question_projection, "dp", axis=0, tiled=True),
        lax.all_gather(lookup_projection, "dp", axis=0, tiled=True),
        lax.all_gather(content_projection, "dp", axis=0, tiled=True),
        lax.all_gather(silu_switch_projection, "dp", axis=0, tiled=True),
        lax.all_gather(retention_result_projection, "dp", axis=1, tiled=True),
    )
    post_scale, post_shift, gate_full, up_full, down_full = (
        lax.all_gather(trailing_norm_multiplier, "dp", axis=0, tiled=True),
        lax.all_gather(trailing_norm_offset, "dp", axis=0, tiled=True),
        lax.all_gather(feedforward_switch_projection, "dp", axis=0, tiled=True),
        lax.all_gather(expanding_projection, "dp", axis=0, tiled=True),
        lax.all_gather(contracting_projection, "dp", axis=1, tiled=True),
    )
    pre_scale = pre_scale.astype(jnp.float32)
    post_scale = post_scale.astype(jnp.float32)
    input_rows = incoming_signals.astype(jnp.float32)
    initial_demeaned, first_inverse = normalize(input_rows, EPSILON)
    initial_standardized = (initial_demeaned * pre_scale + pre_shift.astype(jnp.float32)).astype(
        jnp.bfloat16
    )
    normed_all = lax.all_gather(initial_standardized, "tensor", axis=0, tiled=True)
    total_rows = normed_all.shape[0]
    slot_count = total_rows // SEQ_LEN
    shape_key = (slot_count, SEQ_LEN, heads_here, KEY_DIM)
    shape_value = (slot_count, SEQ_LEN, heads_here, VAL_DIM)
    query_proj = matmul(normed_all, query_full).reshape(shape_key)
    key_proj = matmul(normed_all, key_full).reshape(shape_key)
    value_proj = matmul(normed_all, value_full)
    swish_heads = matmul(normed_all, swish_full).reshape(shape_value)
    cosines, sines = rotary_tables(SEQ_LEN, KEY_DIM)
    head_ids = tensor_rank * heads_here + jnp.arange(heads_here, dtype=jnp.int32)
    decays = decay_table(SEQ_LEN, head_ids)
    query_rot = (query_proj * cosines + rotate_half(query_proj) * sines).astype(jnp.bfloat16)
    key_rot = ((key_proj * cosines + rotate_half(key_proj) * sines) * KEY_DIM ** (-0.5)).astype(
        jnp.bfloat16
    )
    value_heads = value_proj.reshape(shape_value).astype(jnp.bfloat16)
    scores = (
        jnp.einsum("snhk,smhk->shnm", query_rot, key_rot, preferred_element_type=jnp.float32)
        * decays[None]
    ).astype(jnp.bfloat16)
    retained = jnp.einsum(
        "shnm,smhv->snhv", scores, value_heads, preferred_element_type=jnp.float32
    )
    group_hat, group_inverse = normalize(retained, GROUP_EPSILON)
    sigmoid_gate = jax.nn.sigmoid(swish_heads)
    gated = (
        (swish_heads * sigmoid_gate * group_hat)
        .reshape(total_rows, heads_here * VAL_DIM)
        .astype(jnp.bfloat16)
    )
    retention_part = matmul(gated, output_full)
    retention_rows = lax.psum_scatter(
        retention_part.astype(jnp.bfloat16), "tensor", scatter_dimension=0, tiled=True
    ).astype(jnp.float32)
    middle_rows = input_rows + retention_rows
    second_hat, second_inverse = normalize(middle_rows, EPSILON)
    second_normed = (second_hat * post_scale + post_shift.astype(jnp.float32)).astype(jnp.bfloat16)
    mixer_all = lax.all_gather(second_normed, "tensor", axis=0, tiled=True)
    gate_proj = matmul(mixer_all, gate_full)
    up_proj = matmul(mixer_all, up_full)
    gelu_gate, gelu_back = jax.vjp(gelu_tanh, gate_proj)
    hidden = (gelu_gate * up_proj).astype(jnp.bfloat16)
    mixer_part = matmul(hidden, down_full)
    mixer_total = lax.psum_scatter(
        mixer_part.astype(jnp.bfloat16), "tensor", scatter_dimension=0, tiled=True
    ).astype(jnp.float32)
    final_rows = middle_rows + mixer_total
    layer_output = jnp.where(valid_rows, final_rows, 0.0).astype(jnp.bfloat16)
    out_back = jnp.where(valid_rows, loss_sensitivity.astype(jnp.float32), 0.0)
    out_all = lax.all_gather(out_back.astype(jnp.bfloat16), "tensor", axis=0, tiled=True)
    down_gradient = matmul(hidden.T, out_all)
    hidden_back = matmul(out_all, down_full.T)
    gate_back = gelu_back(hidden_back * up_proj)[0].astype(jnp.bfloat16)
    up_back = (hidden_back * gelu_gate).astype(jnp.bfloat16)
    gate_gradient = matmul(mixer_all.T, gate_back)
    up_gradient = matmul(mixer_all.T, up_back)
    mixer_input_part = matmul(gate_back, gate_full.T) + matmul(up_back, up_full.T)
    mixer_input = lax.psum_scatter(
        mixer_input_part.astype(jnp.bfloat16), "tensor", scatter_dimension=0, tiled=True
    ).astype(jnp.float32)
    after_scale_piece = jnp.sum(mixer_input * second_hat, axis=0)
    after_bias_piece = jnp.sum(mixer_input, axis=0)
    middle_back = out_back + normalize_back(mixer_input * post_scale, second_hat, second_inverse)
    middle_all = lax.all_gather(middle_back.astype(jnp.bfloat16), "tensor", axis=0, tiled=True)
    output_gradient = matmul(gated.T, middle_all)
    gated_back = matmul(middle_all, output_full.T).reshape(shape_value)
    swish_back = (
        (gated_back * group_hat * sigmoid_gate * (1.0 + swish_heads * (1.0 - sigmoid_gate)))
        .reshape(total_rows, heads_here * VAL_DIM)
        .astype(jnp.bfloat16)
    )
    retained_back = normalize_back(
        gated_back * swish_heads * sigmoid_gate, group_hat, group_inverse
    ).astype(jnp.bfloat16)
    score_back = (
        jnp.einsum(
            "snhv,smhv->shnm", retained_back, value_heads, preferred_element_type=jnp.float32
        )
        * decays[None]
    ).astype(jnp.bfloat16)
    query_rot_back = jnp.einsum(
        "shnm,smhk->snhk", score_back, key_rot, preferred_element_type=jnp.float32
    )
    key_rot_back = jnp.einsum(
        "shnm,snhk->smhk", score_back, query_rot, preferred_element_type=jnp.float32
    )
    value_back = jnp.einsum(
        "shnm,snhv->smhv", scores, retained_back, preferred_element_type=jnp.float32
    )
    query_back = (
        (query_rot_back * cosines - rotate_half(query_rot_back) * sines)
        .reshape(total_rows, heads_here * KEY_DIM)
        .astype(jnp.bfloat16)
    )
    key_back = (
        ((key_rot_back * cosines - rotate_half(key_rot_back) * sines) * KEY_DIM ** (-0.5))
        .reshape(total_rows, heads_here * KEY_DIM)
        .astype(jnp.bfloat16)
    )
    value_low = value_back.reshape(total_rows, heads_here * VAL_DIM).astype(jnp.bfloat16)
    query_gradient = matmul(normed_all.T, query_back)
    key_gradient = matmul(normed_all.T, key_back)
    value_gradient = matmul(normed_all.T, value_low)
    swish_gradient = matmul(normed_all.T, swish_back)
    first_part = (
        matmul(query_back, query_full.T)
        + matmul(key_back, key_full.T)
        + matmul(value_low, value_full.T)
        + matmul(swish_back, swish_full.T)
    )
    first_layer_input = lax.psum_scatter(
        first_part.astype(jnp.bfloat16), "tensor", scatter_dimension=0, tiled=True
    ).astype(jnp.float32)
    before_scale_piece = jnp.sum(first_layer_input * initial_demeaned, axis=0)
    before_bias_piece = jnp.sum(first_layer_input, axis=0)
    input_delta = middle_back + normalize_back(
        first_layer_input * pre_scale, initial_demeaned, first_inverse
    )
    gain_pieces = (
        lax.psum(before_scale_piece.astype(jnp.bfloat16), "tensor").astype(jnp.float32),
        lax.psum(before_bias_piece.astype(jnp.bfloat16), "tensor").astype(jnp.float32),
        lax.psum(after_scale_piece.astype(jnp.bfloat16), "tensor").astype(jnp.float32),
        lax.psum(after_bias_piece.astype(jnp.bfloat16), "tensor").astype(jnp.float32),
    )
    (
        before_scale_gradient,
        before_bias_gradient,
        query_owned,
        key_owned,
        value_owned,
        swish_owned,
        output_owned,
        after_scale_gradient,
        after_bias_gradient,
        gate_owned,
        up_owned,
        down_owned,
    ) = (
        lax.psum_scatter(
            gain_pieces[0].astype(jnp.bfloat16), "dp", scatter_dimension=0, tiled=True
        ).astype(jnp.float32),
        lax.psum_scatter(
            gain_pieces[1].astype(jnp.bfloat16), "dp", scatter_dimension=0, tiled=True
        ).astype(jnp.float32),
        lax.psum_scatter(
            query_gradient.astype(jnp.bfloat16), "dp", scatter_dimension=0, tiled=True
        ).astype(jnp.float32),
        lax.psum_scatter(
            key_gradient.astype(jnp.bfloat16), "dp", scatter_dimension=0, tiled=True
        ).astype(jnp.float32),
        lax.psum_scatter(
            value_gradient.astype(jnp.bfloat16), "dp", scatter_dimension=0, tiled=True
        ).astype(jnp.float32),
        lax.psum_scatter(
            swish_gradient.astype(jnp.bfloat16), "dp", scatter_dimension=0, tiled=True
        ).astype(jnp.float32),
        lax.psum_scatter(
            output_gradient.astype(jnp.bfloat16), "dp", scatter_dimension=1, tiled=True
        ).astype(jnp.float32),
        lax.psum_scatter(
            gain_pieces[2].astype(jnp.bfloat16), "dp", scatter_dimension=0, tiled=True
        ).astype(jnp.float32),
        lax.psum_scatter(
            gain_pieces[3].astype(jnp.bfloat16), "dp", scatter_dimension=0, tiled=True
        ).astype(jnp.float32),
        lax.psum_scatter(
            gate_gradient.astype(jnp.bfloat16), "dp", scatter_dimension=0, tiled=True
        ).astype(jnp.float32),
        lax.psum_scatter(
            up_gradient.astype(jnp.bfloat16), "dp", scatter_dimension=0, tiled=True
        ).astype(jnp.float32),
        lax.psum_scatter(
            down_gradient.astype(jnp.bfloat16), "dp", scatter_dimension=1, tiled=True
        ).astype(jnp.float32),
    )
    return (
        layer_output,
        input_delta,
        before_scale_gradient,
        before_bias_gradient,
        query_owned,
        key_owned,
        value_owned,
        swish_owned,
        output_owned,
        after_scale_gradient,
        after_bias_gradient,
        gate_owned,
        up_owned,
        down_owned,
    )


def solution(mesh):
    placed = (
        P(("dp", "tensor"), None),
        P(("dp", "tensor"), None),
        P("dp"),
        P("dp"),
        P("dp"),
        P("dp", "tensor"),
        P("dp", "tensor"),
        P("dp", "tensor"),
        P("dp", "tensor"),
        P("tensor", "dp"),
        P("dp"),
        P("dp"),
        P("dp", "tensor"),
        P("dp", "tensor"),
        P("tensor", "dp"),
    )
    return jax.shard_map(
        per_device,
        mesh=mesh,
        in_specs=placed,
        out_specs=(
            P(("dp", "tensor"), None),
            P(("dp", "tensor"), None),
            P("dp"),
            P("dp"),
            P("dp", "tensor"),
            P("dp", "tensor"),
            P("dp", "tensor"),
            P("dp", "tensor"),
            P("tensor", "dp"),
            P("dp"),
            P("dp"),
            P("dp", "tensor"),
            P("dp", "tensor"),
            P("tensor", "dp"),
        ),
        check_vma=False,
    )
```

profile of v0, /device:TPU:8, one launch (start us, length us, event | category | flops | bytes accessed | tf_op | source)
XLA Modules:
  0.0 1544.2 jit_solution(5240154103597735115)
XLA Ops:
  10.4 18.0 %all-gather = bf16[8,1,256]{2,1,0:T(2,128)(2,1)S(1)} all-gather(bf16[1,1,256]{2,1,0:T(2,128)(2,1)S(1)} %reshape.528), channel_id=1, replica_groups=mesh['dp'=8,'tensor'=4] {'dp'}, dimensions={0}, use_global_device_ids=true | all-gather | bytes 4608 | tf_op jit(solution)/shard_map/all_gather | solution.py:85
  29.1 16.3 %all-gather.1 = bf16[8,1,256]{2,1,0:T(2,128)(2,1)S(1)} all-gather(bf16[1,1,256]{2,1,0:T(2,128)(2,1)S(1)} %reshape.530), channel_id=1, replica_groups=mesh['dp'=8,'tensor'=4] {'dp'}, dimensions={0}, use_global_device_ids=true | all-gather | bytes 4608 | tf_op jit(solution)/shard_map/all_gather | solution.py:86
  54.4 17.4 %all-gather.17.cloned.1.call-done = bf16[512,2048]{1,0:T(8,128)(2,1)} async-done(((bf16[128,2048]{1,0:T(8,128)(2,1)}), bf16[512,2048]{1,0:T(8,128)(2,1)}) %all-gather.17.cloned.1.call-update) | async-done | bytes 2097168 | tf_op jit(solution)/shard_map/all_gather | solution.py:107
  71.8 51.3 %all-gather.25.cloned.1.call-done = bf16[2048,512]{1,0:T(8,128)(2,1)} async-done(((bf16[256,512]{1,0:T(8,128)(2,1)}), bf16[2048,512]{1,0:T(8,128)(2,1)}) %all-gather.25.cloned.1.call-update) | async-done | bytes 2097168 | tf_op jit(solution)/shard_map/all_gather | solution.py:88
  126.7 46.2 %all-gather.23.cloned.1.call-done = bf16[2048,512]{1,0:T(8,128)(2,1)} async-done(((bf16[256,512]{1,0:T(8,128)(2,1)}), bf16[2048,512]{1,0:T(8,128)(2,1)}) %all-gather.23.cloned.1.call-update) | async-done | bytes 2097168 | tf_op jit(solution)/shard_map/all_gather | solution.py:87
  180.0 65.9 %all-gather.21.cloned.1.call-done = bf16[2048,1024]{1,0:T(8,128)(2,1)} async-done(((bf16[256,1024]{1,0:T(8,128)(2,1)}), bf16[2048,1024]{1,0:T(8,128)(2,1)}) %all-gather.21.cloned.1.call-update) | async-done | bytes 4194320 | tf_op jit(solution)/shard_map/all_gather | solution.py:89
  251.7 67.5 %all-gather.19.cloned.1.call-done = bf16[2048,1024]{1,0:T(8,128)(2,1)} async-done(((bf16[256,1024]{1,0:T(8,128)(2,1)}), bf16[2048,1024]{1,0:T(8,128)(2,1)}) %all-gather.19.cloned.1.call-update) | async-done | bytes 4194320 | tf_op jit(solution)/shard_map/all_gather | solution.py:90
  327.3 65.4 %all-gather.27.cloned.1.call-done = bf16[1024,2048]{1,0:T(8,128)(2,1)} async-done(((bf16[1024,256]{1,0:T(8,128)(2,1)}), bf16[1024,2048]{1,0:T(8,128)(2,1)}) %all-gather.27.cloned.1.call-update) | async-done | bytes 4194320 | tf_op jit(solution)/shard_map/all_gather | solution.py:91
  392.8 6.8 convolution_convert_fusion.7
  400.4 16.9 %all-gather.2 = bf16[8,1,256]{2,1,0:T(2,128)(2,1)S(1)} all-gather(bf16[1,1,256]{2,1,0:T(2,128)(2,1)S(1)} %reshape.532), channel_id=1, replica_groups=mesh['dp'=8,'tensor'=4] {'dp'}, dimensions={0}, use_global_device_ids=true | all-gather | bytes 4608 | tf_op jit(solution)/shard_map/all_gather | solution.py:94
  417.3 16.9 %all-gather.3 = bf16[8,1,256]{2,1,0:T(2,128)(2,1)S(1)} all-gather(bf16[1,1,256]{2,1,0:T(2,128)(2,1)S(1)} %reshape.534), channel_id=1, replica_groups=mesh['dp'=8,'tensor'=4] {'dp'}, dimensions={0}, use_global_device_ids=true | all-gather | bytes 4608 | tf_op jit(solution)/shard_map/all_gather | solution.py:95
  442.0 63.6 %all-gather.31.cloned.1.call-done = bf16[2048,1024]{1,0:T(8,128)(2,1)} async-done(((bf16[256,1024]{1,0:T(8,128)(2,1)}), bf16[2048,1024]{1,0:T(8,128)(2,1)}) %all-gather.31.cloned.1.call-update) | async-done | bytes 4194320 | tf_op jit(solution)/shard_map/all_gather | solution.py:96
  505.6 23.6 %all-gather.29.cloned.1.call-done = bf16[512,2048]{1,0:T(8,128)(2,1)} async-done(((bf16[128,2048]{1,0:T(8,128)(2,1)}), bf16[512,2048]{1,0:T(8,128)(2,1)}) %all-gather.29.cloned.1.call-update) | async-done | bytes 2097168 | tf_op jit(solution)/shard_map/all_gather | solution.py:145
  529.2 6.5 fusion.61
  535.6 68.0 %all-gather.33.cloned.1.call-done = bf16[2048,1024]{1,0:T(8,128)(2,1)} async-done(((bf16[256,1024]{1,0:T(8,128)(2,1)}), bf16[2048,1024]{1,0:T(8,128)(2,1)}) %all-gather.33.cloned.1.call-update) | async-done | bytes 4194320 | tf_op jit(solution)/shard_map/all_gather | solution.py:97
  603.6 6.5 fusion.62
  610.2 17.0 %all-gather.37.cloned.1.call-done = bf16[512,2048]{1,0:T(8,128)(2,1)} async-done(((bf16[128,2048]{1,0:T(8,128)(2,1)}), bf16[512,2048]{1,0:T(8,128)(2,1)}) %all-gather.37.cloned.1.call-update) | async-done | bytes 2097168 | tf_op jit(solution)/shard_map/all_gather | solution.py:157
  627.2 74.7 %all-gather.35.cloned.1.call-done = bf16[1024,2048]{1,0:T(8,128)(2,1)} async-done(((bf16[1024,256]{1,0:T(8,128)(2,1)}), bf16[1024,2048]{1,0:T(8,128)(2,1)}) %all-gather.35.cloned.1.call-update) | async-done | bytes 4194320 | tf_op jit(solution)/shard_map/all_gather | solution.py:98
  701.9 8.9 multiply_convert_fusion.3
  724.0 24.9 %reduce-scatter.17.cloned.1.call-done = bf16[128,2048]{1,0:T(8,128)(2,1)} async-done(((bf16[512,2048]{1,0:T(8,128)(2,1)}), bf16[128,2048]{1,0:T(8,128)(2,1)}) %reduce-scatter.17.cloned.1.call-update) | async-done | bytes 524304 | tf_op jit(solution)/shard_map/reduce_scatter | solution.py:165
  750.5 32.0 %reduce-scatter.15.cloned.1.call-done = bf16[128,2048]{1,0:T(8,128)(2,1)} async-done(((bf16[512,2048]{1,0:T(8,128)(2,1)}), bf16[128,2048]{1,0:T(8,128)(2,1)}) %reduce-scatter.15.cloned.1.call-update) | async-done | bytes 524304 | tf_op jit(solution)/shard_map/reduce_scatter | solution.py:151
  792.3 6.4 convolution_convert_fusion.1
  866.7 34.1 %reduce-scatter.31.cloned.1.call-done = bf16[256,1024]{1,0:T(8,128)(2,1)} async-done(((bf16[2048,1024]{1,0:T(8,128)(2,1)}), bf16[256,1024]{1,0:T(8,128)(2,1)}) %reduce-scatter.31.cloned.1.call-update) | async-done | bytes 524304 | tf_op jit(solution)/shard_map/reduce_scatter | solution.py:273
  902.9 89.3 %reduce-scatter.33.cloned.1.call-done = bf16[256,1024]{1,0:T(8,128)(2,1)} async-done(((bf16[2048,1024]{1,0:T(8,128)(2,1)}), bf16[256,1024]{1,0:T(8,128)(2,1)}) %reduce-scatter.33.cloned.1.call-update) | async-done | bytes 524304 | tf_op jit(solution)/shard_map/reduce_scatter | solution.py:276
  994.3 89.8 %reduce-scatter.35.cloned.1.call-done = bf16[1024,256]{1,0:T(8,128)(2,1)} async-done(((bf16[1024,2048]{1,0:T(8,128)(2,1)}), bf16[1024,256]{1,0:T(8,128)(2,1)}) %reduce-scatter.35.cloned.1.call-update) | async-done | bytes 524304 | tf_op jit(solution)/shard_map/reduce_scatter | solution.py:279
  1086.2 31.1 %reduce-scatter.19.cloned.1.call-done = bf16[128,2048]{1,0:T(8,128)(2,1)} async-done(((bf16[512,2048]{1,0:T(8,128)(2,1)}), bf16[128,2048]{1,0:T(8,128)(2,1)}) %reduce-scatter.19.cloned.1.call-update) | async-done | bytes 524304 | tf_op jit(solution)/shard_map/reduce_scatter | solution.py:218
  1120.0 34.8 %all-reduce.4 = (bf16[2048]{0:T(1024)(128)(2,1)S(1)}, bf16[2048]{0:T(1024)(128)(2,1)S(1)}, bf16[2048]{0:T(1024)(128)(2,1)S(1)}, bf16[2048]{0:T(1024)(128)(2,1)S(1)}) all-reduce(bf16[2048]{0:T(1024)(128)(2,1)S(1)} %get-tuple-element.18, bf16[2048]{0:T(1024)(128)(2,1)S(1)} %reduce_sum.167, ...), channel_id=6, replica_groups=mesh['dp'=8,'tensor'=4] {'dp'}, use_global_device_ids=true, to_apply=%region_18.19.clone | all-reduce | flops 8192 | bytes 32768
  1162.9 25.9 %reduce-scatter.21.cloned.1.call-done = bf16[256,512]{1,0:T(8,128)(2,1)} async-done(((bf16[2048,512]{1,0:T(8,128)(2,1)}), bf16[256,512]{1,0:T(8,128)(2,1)}) %reduce-scatter.21.cloned.1.call-update) | async-done | bytes 262160 | tf_op jit(solution)/shard_map/reduce_scatter | solution.py:252
  1190.7 69.1 %reduce-scatter.23.cloned.1.call-done = bf16[256,512]{1,0:T(8,128)(2,1)} async-done(((bf16[2048,512]{1,0:T(8,128)(2,1)}), bf16[256,512]{1,0:T(8,128)(2,1)}) %reduce-scatter.23.cloned.1.call-update) | async-done | bytes 262160 | tf_op jit(solution)/shard_map/reduce_scatter | solution.py:255
  1263.0 88.9 %reduce-scatter.29.cloned.1.call-done = bf16[1024,256]{1,0:T(8,128)(2,1)} async-done(((bf16[1024,2048]{1,0:T(8,128)(2,1)}), bf16[1024,256]{1,0:T(8,128)(2,1)}) %reduce-scatter.29.cloned.1.call-update) | async-done | bytes 524304 | tf_op jit(solution)/shard_map/reduce_scatter | solution.py:264
  1354.0 89.5 %reduce-scatter.25.cloned.1.call-done = bf16[256,1024]{1,0:T(8,128)(2,1)} async-done(((bf16[2048,1024]{1,0:T(8,128)(2,1)}), bf16[256,1024]{1,0:T(8,128)(2,1)}) %reduce-scatter.25.cloned.1.call-update) | async-done | bytes 524304 | tf_op jit(solution)/shard_map/reduce_scatter | solution.py:258
  1445.7 89.4 %reduce-scatter.27.cloned.1.call-done = bf16[256,1024]{1,0:T(8,128)(2,1)} async-done(((bf16[2048,1024]{1,0:T(8,128)(2,1)}), bf16[256,1024]{1,0:T(8,128)(2,1)}) %reduce-scatter.27.cloned.1.call-update) | async-done | bytes 524304 | tf_op jit(solution)/shard_map/reduce_scatter | solution.py:261
  (219 shorter events, 165.3 us)
Async XLA Ops:
  7.2 64.7 %all-gather.17.cloned.1.call-start = ((), (), s32[]{:S(2)}) async-start(), calls=%async_computation.12 | async-start | bytes 2621440 | tf_op jit(solution)/shard_map/all_gather | solution.py:107
  47.7 75.5 %all-gather.25.cloned.1.call-start = ((), (), s32[]{:S(2)}) async-start(), calls=%async_computation.16 | async-start | bytes 2359296 | tf_op jit(solution)/shard_map/all_gather | solution.py:88
  48.4 124.5 %all-gather.23.cloned.1.call-start = ((), (), s32[]{:S(2)}) async-start(), calls=%async_computation.15 | async-start | bytes 2359296 | tf_op jit(solution)/shard_map/all_gather | solution.py:87
  49.1 196.7 %all-gather.21.cloned.1.call-start = ((), (), s32[]{:S(2)}) async-start(), calls=%async_computation.14 | async-start | bytes 4718592 | tf_op jit(solution)/shard_map/all_gather | solution.py:89
  49.7 269.5 %all-gather.19.cloned.1.call-start = ((), (), s32[]{:S(2)}) async-start(), calls=%async_computation.13 | async-start | bytes 4718592 | tf_op jit(solution)/shard_map/all_gather | solution.py:90
  50.3 342.5 %all-gather.27.cloned.1.call-start = ((), (), s32[]{:S(2)}) async-start(), calls=%async_computation.17 | async-start | bytes 4718592 | tf_op jit(solution)/shard_map/all_gather | solution.py:91
  50.9 383.3 %reduce-scatter.13.cloned.1.call-start = ((), (), s32[]{:S(2)}) async-start(), calls=%async_computation.18 | async-start | bytes 2621440 | tf_op jit(solution)/shard_map/reduce_scatter | solution.py:139
  54.4 122.1 %copy-start.4 = (f32[512,256]{0,1:T(8,128)}, f32[512,256]{0,1:T(8,128)S(1)}, u32[]{:S(2)}) copy-start(f32[512,256]{0,1:T(8,128)S(1)} %get-tuple-element.50) | copy-start | bytes 1572868
  54.4 122.1 %copy-start.6 = (f32[512,256]{0,1:T(8,128)}, f32[512,256]{0,1:T(8,128)S(1)}, u32[]{:S(2)}) copy-start(f32[512,256]{0,1:T(8,128)S(1)} %get-tuple-element.51) | copy-start | bytes 1572868
  178.2 67.7 %copy-start.30 = (bf16[512,2048]{1,0:T(8,128)(2,1)S(1)}, bf16[512,2048]{1,0:T(8,128)(2,1)}, u32[]{:S(2)}) copy-start(bf16[512,2048]{1,0:T(8,128)(2,1)} %all-gather.17.cloned.1.call-done) | copy-start | bytes 6291460
  399.5 17.7 %copy-start.33 = (bf16[256]{0:T(256)(128)(2,1)S(1)}, bf16[256]{0:T(256)(128)(2,1)}, u32[]{:S(2)}) copy-start(bf16[256]{0:T(256)(128)(2,1)} %param.26) | copy-start | bytes 1540
  399.6 34.6 %copy-start = (bf16[128,2048]{1,0:T(8,128)(2,1)S(1)}, bf16[128,2048]{1,0:T(8,128)(2,1)}, u32[]{:S(2)}) copy-start(bf16[128,2048]{1,0:T(8,128)(2,1)} %param.15) | copy-start | bytes 1572868
  399.6 106.0 %all-gather.31.cloned.1.call-start = ((), (), s32[]{:S(2)}) async-start(), calls=%async_computation.20 | async-start | bytes 4718592 | tf_op jit(solution)/shard_map/all_gather | solution.py:96
  400.3 128.8 %all-gather.29.cloned.1.call-start = ((), (), s32[]{:S(2)}) async-start(), calls=%async_computation.19 | async-start | bytes 2621440 | tf_op jit(solution)/shard_map/all_gather | solution.py:145
  438.0 165.6 %all-gather.33.cloned.1.call-start = ((), (), s32[]{:S(2)}) async-start(), calls=%async_computation.21 | async-start | bytes 4718592 | tf_op jit(solution)/shard_map/all_gather | solution.py:97
  438.6 188.6 %all-gather.37.cloned.1.call-start = ((), (), s32[]{:S(2)}) async-start(), calls=%async_computation.24 | async-start | bytes 2621440 | tf_op jit(solution)/shard_map/all_gather | solution.py:157
  441.4 260.6 %all-gather.35.cloned.1.call-start = ((), (), s32[]{:S(2)}) async-start(), calls=%async_computation.22 | async-start | bytes 4718592 | tf_op jit(solution)/shard_map/all_gather | solution.py:98
  441.9 307.0 %reduce-scatter.17.cloned.1.call-start = ((), (), s32[]{:S(2)}) async-start(), calls=%async_computation.25 | async-start | bytes 2621440 | tf_op jit(solution)/shard_map/reduce_scatter | solution.py:165
  717.5 65.0 %reduce-scatter.15.cloned.1.call-start = ((), (), s32[]{:S(2)}) async-start(), calls=%async_computation.23 | async-start | bytes 2621440 | tf_op jit(solution)/shard_map/reduce_scatter | solution.py:151
  724.0 84.8 %all-gather.39.cloned.1.call-start = ((), (), s32[]{:S(2)}) async-start(), calls=%async_computation.26 | async-start | bytes 2621440 | tf_op jit(solution)/shard_map/all_gather | solution.py:171
  786.0 114.7 %reduce-scatter.31.cloned.1.call-start = ((), (), s32[]{:S(2)}) async-start(), calls=%async_computation.33 | async-start | bytes 4718592 | tf_op jit(solution)/shard_map/reduce_scatter | solution.py:273
  792.3 199.9 %reduce-scatter.33.cloned.1.call-start = ((), (), s32[]{:S(2)}) async-start(), calls=%async_computation.34 | async-start | bytes 4718592 | tf_op jit(solution)/shard_map/reduce_scatter | solution.py:276
  798.7 285.4 %reduce-scatter.35.cloned.1.call-start = ((), (), s32[]{:S(2)}) async-start(), calls=%async_computation.35 | async-start | bytes 4718592 | tf_op jit(solution)/shard_map/reduce_scatter | solution.py:279
  805.2 312.1 %reduce-scatter.19.cloned.1.call-start = ((), (), s32[]{:S(2)}) async-start(), calls=%async_computation.27 | async-start | bytes 2621440 | tf_op jit(solution)/shard_map/reduce_scatter | solution.py:218
  815.4 13.2 copy-start.22
  834.4 354.5 %reduce-scatter.21.cloned.1.call-start = ((), (), s32[]{:S(2)}) async-start(), calls=%async_computation.28 | async-start | bytes 2359296 | tf_op jit(solution)/shard_map/reduce_scatter | solution.py:252
  838.7 421.1 %reduce-scatter.23.cloned.1.call-start = ((), (), s32[]{:S(2)}) async-start(), calls=%async_computation.29 | async-start | bytes 2359296 | tf_op jit(solution)/shard_map/reduce_scatter | solution.py:255
  843.0 508.9 %reduce-scatter.29.cloned.1.call-start = ((), (), s32[]{:S(2)}) async-start(), calls=%async_computation.32 | async-start | bytes 4718592 | tf_op jit(solution)/shard_map/reduce_scatter | solution.py:264
  850.2 593.4 %reduce-scatter.25.cloned.1.call-start = ((), (), s32[]{:S(2)}) async-start(), calls=%async_computation.30 | async-start | bytes 4718592 | tf_op jit(solution)/shard_map/reduce_scatter | solution.py:258
  857.5 677.6 %reduce-scatter.27.cloned.1.call-start = ((), (), s32[]{:S(2)}) async-start(), calls=%async_computation.31 | async-start | bytes 4718592 | tf_op jit(solution)/shard_map/reduce_scatter | solution.py:261
  994.3 267.3 %copy-start.10 = (f32[128,2048]{1,0:T(8,128)S(1)}, f32[128,2048]{1,0:T(8,128)}, u32[]{:S(2)}) copy-start(f32[128,2048]{1,0:T(8,128)} %get-tuple-element.32) | copy-start | bytes 3145732
  1117.2 144.4 %copy-start.9 = (bf16[128,2048]{1,0:T(8,128)(2,1)S(1)}, bf16[128,2048]{1,0:T(8,128)(2,1)}, u32[]{:S(2)}) copy-start(bf16[128,2048]{1,0:T(8,128)(2,1)} %reduce-scatter.19.cloned.1.call-done) | copy-start | bytes 1572868
  (30 other events, 64.2 us)
Sparse Core Ops, SparseCore 0:
  47.8 24.0 all-gather.16
  74.0 49.1 all-gather.24
  125.2 47.6 all-gather.22
  174.9 70.9 all-gather.20
  247.9 71.3 all-gather.18
  321.1 71.6 all-gather.26
  399.7 31.1 reduce-scatter.12
  433.1 72.4 all-gather.30
  507.7 21.3 all-gather.28
  531.1 72.4 all-gather.32
  605.8 21.3 all-gather.36
  629.1 72.7 all-gather.34
  717.7 31.1 reduce-scatter.16
  751.3 31.1 reduce-scatter.14
  786.1 22.5 all-gather.38
  812.2 88.4 reduce-scatter.30
  904.2 87.9 reduce-scatter.32
  995.7 88.3 reduce-scatter.34
  1086.6 30.5 reduce-scatter.18
  1120.6 68.1 reduce-scatter.20
  1192.4 67.3 reduce-scatter.22
  1263.4 88.4 reduce-scatter.28
  1355.6 87.9 reduce-scatter.24
  1447.1 87.9 reduce-scatter.26
where the time goes:
time: 1550 us; the launch traced here: 1540 us
  waiting for transfers between devices  1230 us (79%)
  matrix products  123 us (8%)
  blocking collectives  108 us (7%)
  other arithmetic  47.5 us (3%)
  between operations  16.5 us (1%)
    dot_general x23, matrix products, matmul(): return jnp.dot(left, right, preferred_element_type=jnp.float32)  112 us
    reduce_scatter x1, waiting for transfers between devices, per_device(): lax.psum_scatter(down_gradient.astype(jnp.bfloat16), 'dp', scatter_dimens...  89.8 us
    reduce_scatter x1, waiting for transfers between devices, per_device(): lax.psum_scatter(value_gradient.astype(jnp.bfloat16), 'dp', scatter_dimen...  89.5 us
    reduce_scatter x1, waiting for transfers between devices, per_device(): lax.psum_scatter(swish_gradient.astype(jnp.bfloat16), 'dp', scatter_dimen...  89.4 us
    reduce_scatter x1, waiting for transfers between devices, per_device(): lax.psum_scatter(up_gradient.astype(jnp.bfloat16), 'dp', scatter_dimensio...  89.3 us
    reduce_scatter x1, waiting for transfers between devices, per_device(): lax.psum_scatter(output_gradient.astype(jnp.bfloat16), 'dp', scatter_dime...  88.9 us
    all_gather x1, waiting for transfers between devices, per_device(): lax.all_gather(contracting_projection, 'dp', axis=1, tiled=True)  74.7 us
    reduce_scatter x1, waiting for transfers between devices, per_device(): lax.psum_scatter(key_gradient.astype(jnp.bfloat16), 'dp', scatter_dimensi...  69.1 us
  transfers between devices with their start and end apart: 24, of which 23 were waited for; matrix products, arithmetic and copies ran while one was open for 9% of the time, Pallas kernels for 0%

commit v1 on v0

v1 whole, which is shorter than its diff:
```python
import functools

import jax
import jax.numpy as jnp
from jax import lax
from jax.experimental import pallas as pl
from jax.experimental.pallas import tpu as pltpu
from jax.sharding import PartitionSpec as P

KEY_DIM = 256
VAL_DIM = 512
SEQ_LEN = 512

EPSILON = 1e-05
GROUP_EPSILON = 0.1

MESH = pl.DeviceIdType.MESH
F32 = jnp.float32
BF16 = jnp.bfloat16
CHUNK = 16


def normalize(values, epsilon):
    centre = values - jnp.mean(values, axis=-1, keepdims=True)
    inverse = lax.rsqrt(jnp.mean(centre * centre, axis=-1, keepdims=True) + epsilon)
    return (centre * inverse, inverse)


def normalize_back(upstream, normed, inverse):
    return inverse * (
        upstream
        - jnp.mean(upstream, axis=-1, keepdims=True)
        - normed * jnp.mean(upstream * normed, axis=-1, keepdims=True)
    )


def rotate_half(values):
    middle = values.shape[-1] // 2
    return jnp.concatenate([-values[..., middle:], values[..., :middle]], axis=-1)


def rotary_tables(span, columns):
    middle = columns // 2
    places = jnp.arange(span, dtype=jnp.int32).astype(jnp.float32)
    spectrum = 10000.0 ** (-jnp.arange(middle, dtype=jnp.int32).astype(jnp.float32) / middle)
    angles = places[:, None] * spectrum[None, :]
    angles = jnp.concatenate([angles, angles], axis=1)
    return (jnp.cos(angles)[None], jnp.sin(angles)[None])


def decay_table(span, head_id):
    log_rate = jnp.log(1.0 - jnp.exp2(-5.0 - head_id.astype(jnp.float32)))
    places = jnp.arange(span, dtype=jnp.int32)
    offsets = places[:, None] - places[None, :]
    decayed = jnp.exp(jnp.maximum(offsets, 0).astype(jnp.float32) * log_rate)
    return jnp.where(offsets >= 0, decayed, 0.0)


def gelu_tanh(values):
    return jax.nn.gelu(values, approximate=True)


def matmul(left, right):
    return jnp.dot(left, right, preferred_element_type=jnp.float32)


class Place:
    def __init__(self):
        d, t = lax.axis_index("dp"), lax.axis_index("tensor")
        self.x, self.y, self.c = lax.rem(d, 2), t // 2, lax.rem(t, 2)
        dx, ty = d + 1 - 2 * self.x, (1 - self.y) * 2 + self.c
        self.sib = (d, t + 1 - 2 * self.c)
        self.xn = (dx, t)
        self.yn = (d, ty)

    def block(self, j, other_core=0):
        x = 1 - self.x if j in (1, 3) else self.x
        y = 1 - self.y if j in (2, 3) else self.y
        c = 1 - self.c if other_core else self.c
        return x * 4 + y * 2 + c


def greet(place):
    barrier = pltpu.get_barrier_semaphore()
    for partner in (place.sib, place.xn, place.yn):
        pl.semaphore_signal(barrier, inc=1, device_id=partner, device_id_type=MESH)
    pl.semaphore_wait(barrier, 3)


def rows_of(index, rows):
    return pl.ds(pl.multiple_of(index * rows, rows), rows)


class Gather:
    @staticmethod
    def scratch():
        return [pltpu.SemaphoreType.DMA((13,)), pltpu.SemaphoreType.DMA((13,))]

    def __init__(self, place, src, out, send, recv):
        rows = src.shape[0]
        half = rows // 2
        p = place

        def remote(k, source, j, lo, n, target, core=0):
            where = pl.ds(pl.multiple_of(p.block(j, core) * rows + lo, 8), n)
            source = source.at[pl.ds(lo, n)] if source is src else source.at[where]
            return pltpu.make_async_remote_copy(
                src_ref=source,
                dst_ref=out.at[where],
                send_sem=send.at[k],
                recv_sem=recv.at[k],
                device_id=target,
                device_id_type=MESH,
            )

        self.p, self.rows, self.half = p, rows, half
        self.local = pltpu.make_async_copy(src, out.at[rows_of(p.block(0), rows)], send.at[12])
        h = half
        self.xa = remote(0, src, 0, 0, h, p.xn)
        self.xb = remote(1, src, 0, h, h, p.xn)
        self.ya = remote(2, src, 0, 0, h, p.yn)
        self.yb = remote(3, src, 0, h, h, p.yn)
        self.s0 = remote(4, src, 0, 0, rows, p.sib)
        self.da = remote(5, out, 1, 0, h, p.yn)
        self.db = remote(6, out, 2, h, h, p.xn)
        self.s1 = remote(7, out, 1, 0, rows, p.sib)
        self.s2 = remote(8, out, 2, 0, rows, p.sib)
        self.s3a = remote(9, out, 3, 0, h, p.sib)
        self.s3b = remote(10, out, 3, h, h, p.sib)

    def start(self):
        for copy in (self.xa, self.yb, self.xb, self.ya, self.s0, self.local):
            copy.start()

    def forward(self):
        self.xa.wait_recv()
        self.da.start()
        self.yb.wait_recv()
        self.db.start()
        self.xb.wait_recv()
        self.s1.start()
        self.ya.wait_recv()
        self.s2.start()

    def finish(self):
        self.da.wait_recv()
        self.s3a.start()
        self.db.wait_recv()
        self.s3b.start()
        self.local.wait()
        for copy in (self.s0, self.s1, self.s2, self.s3a, self.s3b):
            copy.wait()
        for copy in (self.xa, self.xb, self.ya, self.yb, self.da, self.db):
            copy.wait_send()


class Reduce:
    @staticmethod
    def scratch(rows, columns):
        return [
            pltpu.VMEM((4, rows, columns), BF16),
            pltpu.VMEM((4, rows, columns), BF16),
            pltpu.VMEM((2, rows, columns), BF16),
            pltpu.VMEM((2, rows // 2, columns), BF16),
            pltpu.SemaphoreType.DMA((14,)),
            pltpu.SemaphoreType.DMA((10,)),
        ]

    def __init__(self, place, part, mine, theirs, got, across, send, recv):
        p = place
        rows = mine.shape[1]
        h = rows // 2
        self.rows, self.half = rows, h
        self.mine, self.theirs, self.got, self.across = mine, theirs, got, across

        def remote(k, source, target_ref, target):
            return pltpu.make_async_remote_copy(
                src_ref=source,
                dst_ref=target_ref,
                send_sem=send.at[k],
                recv_sem=recv.at[k],
                device_id=target,
                device_id_type=MESH,
            )

        a, b = pl.ds(0, h), pl.ds(h, h)
        self.load = [
            pltpu.make_async_copy(part.at[rows_of(p.block(j), rows)], mine.at[j], send.at[10 + j])
            for j in range(4)
        ]
        self.swap = [
            remote(j, part.at[rows_of(p.block(j, 1), rows)], theirs.at[j], p.sib) for j in range(4)
        ]
        self.da = remote(4, mine.at[3, a], across.at[0], p.xn)
        self.db = remote(5, mine.at[3, b], across.at[1], p.yn)
        self.xa = remote(6, mine.at[1, a], got.at[0, a], p.xn)
        self.xb = remote(7, mine.at[1, b], got.at[0, b], p.xn)
        self.ya = remote(8, mine.at[2, a], got.at[1, a], p.yn)
        self.yb = remote(9, mine.at[2, b], got.at[1, b], p.yn)

    def add(self, j, lo, n, other, other_lo):
        def body(i, carry):
            r = pl.ds(pl.multiple_of(lo + i * CHUNK, CHUNK), CHUNK)
            q = pl.ds(pl.multiple_of(other_lo + i * CHUNK, CHUNK), CHUNK)
            self.mine[j, r] = (self.mine[j, r].astype(F32) + other[q].astype(F32)).astype(BF16)
            return carry

        lax.fori_loop(0, n // CHUNK, body, 0)

    def start(self):
        for j in (3, 1, 2, 0):
            self.swap[j].start()
            self.load[j].start()

    def run(self):
        rows, h = self.rows, self.half
        for j, copies in ((3, (self.da, self.db)), (1, (self.xa,)), (2, (self.yb,))):
            self.load[j].wait()
            self.swap[j].wait_recv()
            self.add(j, 0, rows, self.theirs.at[j], 0)
            for copy in copies:
                copy.start()
        self.db.wait_recv()
        self.add(1, h, h, self.across.at[1], 0)
        self.xb.start()
        self.da.wait_recv()
        self.add(2, 0, h, self.across.at[0], 0)
        self.ya.start()
        self.load[0].wait()
        self.swap[0].wait_recv()
        for copy in (self.xa, self.yb, self.xb, self.ya):
            copy.wait_recv()

    def total(self, r):
        pieces = (self.mine[0, r], self.theirs[0, r], self.got[0, r], self.got[1, r])
        one, two, three, four = (piece.astype(F32) for piece in pieces)
        return (one + two) + (three + four)

    def finish(self):
        for copy in (*self.swap, self.da, self.db, self.xa, self.xb, self.ya, self.yb):
            copy.wait_send()


def chunks(rows, body):
    def step(i, carry):
        body(pl.ds(pl.multiple_of(i * CHUNK, CHUNK), CHUNK))
        return carry

    lax.fori_loop(0, rows // CHUNK, step, 0)


def first_kernel(x_ref, cot_ref, gains_ref, out_x, out_cot, normed, *sems):
    place = Place()
    greet(place)
    gain, shift = gains_ref[0:1, :], gains_ref[1:2, :]

    def body(r):
        hat, _ = normalize(x_ref[r].astype(F32), EPSILON)
        normed[r] = (hat * gain + shift).astype(BF16)

    chunks(x_ref.shape[0], body)
    one = Gather(place, normed, out_x, *sems[:2])
    two = Gather(place, cot_ref, out_cot, *sems[2:])
    one.start()
    two.start()
    one.forward()
    two.forward()
    one.finish()
    two.finish()


def second_kernel(part_ref, x_ref, gains_ref, out_all, middle_ref, normed, *scratch):
    place = Place()
    greet(place)
    reduce = Reduce(place, part_ref, *scratch[:6])
    reduce.start()
    reduce.run()
    gain, shift = gains_ref[2:3, :], gains_ref[3:4, :]

    def body(r):
        middle = x_ref[r].astype(F32) + reduce.total(r)
        middle_ref[r] = middle
        hat, _ = normalize(middle, EPSILON)
        normed[r] = (hat * gain + shift).astype(BF16)

    chunks(x_ref.shape[0], body)
    gather = Gather(place, normed, out_all, *scratch[6:])
    gather.start()
    gather.forward()
    gather.finish()
    reduce.finish()


def third_kernel(
    part_ref, middle_ref, cot_ref, gains_ref, out_all, back_ref, pieces_ref, low, *scratch
):
    place = Place()
    greet(place)
    reduce = Reduce(place, part_ref, *scratch[:6])
    reduce.start()
    pieces_ref[...] = jnp.zeros_like(pieces_ref)
    reduce.run()
    gain = gains_ref[2:3, :]

    def body(r):
        upstream = reduce.total(r)
        hat, inverse = normalize(middle_ref[r], EPSILON)
        scaled = upstream * hat
        pieces_ref[0] += scaled[0:8] + scaled[8:16]
        pieces_ref[1] += upstream[0:8] + upstream[8:16]
        back = cot_ref[r].astype(F32) + normalize_back(upstream * gain, hat, inverse)
        back_ref[r] = back
        low[r] = back.astype(BF16)

    chunks(middle_ref.shape[0], body)
    gather = Gather(place, low, out_all, *scratch[6:])
    gather.start()
    gather.forward()
    gather.finish()
    reduce.finish()


def fourth_kernel(
    first_ref, mixer_ref, x_ref, middle_ref, gains_ref, delta_ref, final_ref, pieces_ref, *scratch
):
    place = Place()
    greet(place)
    one = Reduce(place, first_ref, *scratch[:6])
    two = Reduce(place, mixer_ref, *scratch[6:])
    one.start()
    two.start()
    pieces_ref[...] = jnp.zeros_like(pieces_ref)
    one.run()
    two.run()
    gain = gains_ref[0:1, :]

    def body(r):
        upstream = one.total(r)
        hat, inverse = normalize(x_ref[r].astype(F32), EPSILON)
        scaled = upstream * hat
        pieces_ref[0] += scaled[0:8] + scaled[8:16]
        pieces_ref[1] += upstream[0:8] + upstream[8:16]
        delta_ref[r] = normalize_back(upstream * gain, hat, inverse)
        final_ref[r] = middle_ref[r] + two.total(r)

    chunks(x_ref.shape[0], body)
    one.finish()
    two.finish()


ANY = pl.BlockSpec(memory_space=pl.ANY)
VM = pl.BlockSpec(memory_space=pltpu.VMEM)


def call(kernel, ident, args, specs, outs, out_specs, scratch, nbytes):
    return pl.pallas_call(
        kernel,
        out_shape=outs,
        in_specs=specs,
        out_specs=out_specs,
        scratch_shapes=scratch,
        compiler_params=pltpu.CompilerParams(
            collective_id=ident, has_side_effects=True, vmem_limit_bytes=32 << 20
        ),
        cost_estimate=pl.CostEstimate(flops=0, bytes_accessed=nbytes, transcendentals=0),
        name=kernel.__name__,
    )(*args)


def per_device(
    groups,
    swap,
    incoming_signals,
    loss_sensitivity,
    token_counts_per_slot,
    leading_norm_multiplier,
    leading_norm_offset,
    question_projection,
    lookup_projection,
    content_projection,
    silu_switch_projection,
    retention_result_projection,
    trailing_norm_multiplier,
    trailing_norm_offset,
    feedforward_switch_projection,
    expanding_projection,
    contracting_projection,
):
    local_rows, hidden_size = incoming_signals.shape
    total_rows = 8 * local_rows
    slots_here = token_counts_per_slot.shape[0]
    dp_rank, tensor_rank = lax.axis_index("dp"), lax.axis_index("tensor")
    side = lax.rem(dp_rank, 2)
    row_ids = tensor_rank * local_rows + jnp.arange(local_rows, dtype=jnp.int32)
    slot_match = (row_ids // SEQ_LEN)[:, None] == jnp.arange(slots_here, dtype=jnp.int32)[None, :]
    row_lengths = jnp.sum(jnp.where(slot_match, token_counts_per_slot[None, :], 0), axis=1)
    valid_rows = (row_ids % SEQ_LEN < row_lengths)[:, None]

    def exchange(weight, axis, join):
        half = weight.shape[axis] // 2
        keep = lax.dynamic_slice_in_dim(weight, side * half, half, axis)
        give = lax.dynamic_slice_in_dim(weight, (1 - side) * half, half, axis)
        take = lax.ppermute(give, "dp", swap)
        return jnp.where(
            side == 0,
            jnp.concatenate([keep, take], axis=join),
            jnp.concatenate([take, keep], axis=join),
        )

    def spread(block, axis):
        return lax.all_gather(block, "dp", axis=axis, tiled=True, axis_index_groups=groups)

    query_half = exchange(question_projection, 1, 0)
    key_half = exchange(lookup_projection, 1, 0)
    query_key = spread(jnp.concatenate([query_half, key_half], axis=1), 0)
    value_full = spread(exchange(content_projection, 1, 0), 0)
    swish_full = spread(exchange(silu_switch_projection, 1, 0), 0)
    output_full = spread(exchange(retention_result_projection, 0, 1), 1)
    gate_full = spread(exchange(feedforward_switch_projection, 1, 0), 0)
    up_full = spread(exchange(expanding_projection, 1, 0), 0)
    down_full = spread(exchange(contracting_projection, 0, 1), 1)

    gains = jnp.stack(
        [leading_norm_multiplier, leading_norm_offset, trailing_norm_multiplier, trailing_norm_offset]
    )
    gains = lax.all_gather(gains, "dp", axis=1, tiled=True).astype(F32)
    gains = jnp.concatenate([gains, gains], axis=0)

    all_rows = jax.ShapeDtypeStruct((total_rows, hidden_size), BF16)
    own_rows = jax.ShapeDtypeStruct((local_rows, hidden_size), F32)
    pieces = jax.ShapeDtypeStruct((2, 8, hidden_size), F32)
    row_low = pltpu.VMEM((local_rows, hidden_size), BF16)
    reduce_scratch = Reduce.scratch(local_rows, hidden_size)
    moved = total_rows * hidden_size * 2

    out_low = jnp.where(valid_rows, loss_sensitivity, 0)
    normed_all, out_all = call(
        first_kernel,
        0,
        (incoming_signals, out_low, gains),
        [VM, VM, VM],
        (all_rows, all_rows),
        (ANY, ANY),
        [row_low, *Gather.scratch(), *Gather.scratch()],
        24 * moved,
    )

    slot_count = total_rows // SEQ_LEN
    shape_key = (slot_count, SEQ_LEN, KEY_DIM)
    shape_value = (slot_count, SEQ_LEN, VAL_DIM)
    query_key_proj = matmul(normed_all, query_key)
    query_proj = query_key_proj[:, :KEY_DIM].reshape(shape_key)
    key_proj = query_key_proj[:, KEY_DIM:].reshape(shape_key)
    value_heads = matmul(normed_all, value_full).reshape(shape_value).astype(BF16)
    swish_heads = matmul(normed_all, swish_full).reshape(shape_value)
    cosines, sines = rotary_tables(SEQ_LEN, KEY_DIM)
    decays = decay_table(SEQ_LEN, tensor_rank * 2 + side)
    query_rot = (query_proj * cosines + rotate_half(query_proj) * sines).astype(BF16)
    key_rot = ((key_proj * cosines + rotate_half(key_proj) * sines) * KEY_DIM ** (-0.5)).astype(BF16)
    scores = (
        jnp.einsum("snk,smk->snm", query_rot, key_rot, preferred_element_type=F32) * decays[None]
    ).astype(BF16)
    retained = jnp.einsum("snm,smv->snv", scores, value_heads, preferred_element_type=F32)
    group_hat, group_inverse = normalize(retained, GROUP_EPSILON)
    sigmoid_gate = jax.nn.sigmoid(swish_heads)
    gated = (swish_heads * sigmoid_gate * group_hat).reshape(total_rows, VAL_DIM).astype(BF16)
    retention_part = matmul(gated, output_full).astype(BF16)

    mixer_all, middle_rows = call(
        second_kernel,
        1,
        (retention_part, incoming_signals, gains),
        [ANY, VM, VM],
        (all_rows, own_rows),
        (ANY, VM),
        [row_low, *reduce_scratch, *Gather.scratch()],
        24 * moved,
    )

    gate_proj = matmul(mixer_all, gate_full)
    up_proj = matmul(mixer_all, up_full)
    gelu_gate, gelu_back = jax.vjp(gelu_tanh, gate_proj)
    hidden = (gelu_gate * up_proj).astype(BF16)
    down_gradient = matmul(hidden.T, out_all).astype(BF16)
    hidden_back = matmul(out_all, down_full.T)
    gate_back = gelu_back(hidden_back * up_proj)[0].astype(BF16)
    up_back = (hidden_back * gelu_gate).astype(BF16)
    gate_gradient = matmul(mixer_all.T, gate_back).astype(BF16)
    up_gradient = matmul(mixer_all.T, up_back).astype(BF16)
    mixer_input_part = (matmul(gate_back, gate_full.T) + matmul(up_back, up_full.T)).astype(BF16)
    mixer_part = matmul(hidden, down_full).astype(BF16)

    middle_all, middle_back, after_pieces = call(
        third_kernel,
        2,
        (mixer_input_part, middle_rows, out_low, gains),
        [ANY, VM, VM, VM],
        (all_rows, own_rows, pieces),
        (ANY, VM, VM),
        [row_low, *reduce_scratch, *Gather.scratch()],
        24 * moved,
    )

    output_gradient = matmul(gated.T, middle_all).astype(BF16)
    gated_back = matmul(middle_all, output_full.T).reshape(shape_value)
    swish_back = (
        (gated_back * group_hat * sigmoid_gate * (1.0 + swish_heads * (1.0 - sigmoid_gate)))
        .reshape(total_rows, VAL_DIM)
        .astype(BF16)
    )
    retained_back = normalize_back(
        gated_back * swish_heads * sigmoid_gate, group_hat, group_inverse
    ).astype(BF16)
    score_back = (
        jnp.einsum("snv,smv->snm", retained_back, value_heads, preferred_element_type=F32)
        * decays[None]
    ).astype(BF16)
    query_rot_back = jnp.einsum("snm,smk->snk", score_back, key_rot, preferred_element_type=F32)
    key_rot_back = jnp.einsum("snm,snk->smk", score_back, query_rot, preferred_element_type=F32)
    value_back = jnp.einsum("snm,snv->smv", scores, retained_back, preferred_element_type=F32)
    query_back = (
        (query_rot_back * cosines - rotate_half(query_rot_back) * sines)
        .reshape(total_rows, KEY_DIM)
        .astype(BF16)
    )
    key_back = (
        ((key_rot_back * cosines - rotate_half(key_rot_back) * sines) * KEY_DIM ** (-0.5))
        .reshape(total_rows, KEY_DIM)
        .astype(BF16)
    )
    value_low = value_back.reshape(total_rows, VAL_DIM).astype(BF16)
    swish_gradient = matmul(normed_all.T, swish_back).astype(BF16)
    value_gradient = matmul(normed_all.T, value_low).astype(BF16)
    query_key_back = jnp.concatenate([query_back, key_back], axis=1)
    query_key_gradient = matmul(normed_all.T, query_key_back).astype(BF16)
    first_part = (
        matmul(query_key_back, query_key.T)
        + matmul(value_low, value_full.T)
        + matmul(swish_back, swish_full.T)
    ).astype(BF16)

    delta, final_rows, before_pieces = call(
        fourth_kernel,
        3,
        (first_part, mixer_part, incoming_signals, middle_rows, gains),
        [ANY, ANY, VM, VM, VM],
        (own_rows, own_rows, pieces),
        (VM, VM, VM),
        [*reduce_scratch, *reduce_scratch],
        24 * moved,
    )
    layer_output = jnp.where(valid_rows, final_rows, 0.0).astype(BF16)
    input_delta = middle_back + delta

    gain_pieces = jnp.concatenate(
        [jnp.sum(before_pieces, axis=1), jnp.sum(after_pieces, axis=1)], axis=0
    )
    gain_sums = lax.psum(gain_pieces, ("dp", "tensor"))
    width = leading_norm_multiplier.shape[0]
    gain_sums = lax.dynamic_slice_in_dim(gain_sums, dp_rank * width, width, 1)

    def collect(gradient, axis):
        return lax.psum_scatter(
            gradient, "dp", scatter_dimension=axis, tiled=True, axis_index_groups=groups
        )

    def restore(block, axis, join):
        half = block.shape[axis] // 2
        keep = lax.dynamic_slice_in_dim(block, side * half, half, axis)
        give = lax.dynamic_slice_in_dim(block, (1 - side) * half, half, axis)
        take = lax.ppermute(give, "dp", swap)
        return jnp.where(
            side == 0,
            jnp.concatenate([keep, take], axis=join),
            jnp.concatenate([take, keep], axis=join),
        ).astype(F32)

    down_owned = restore(collect(down_gradient, 1), 1, 0)
    gate_owned = restore(collect(gate_gradient, 0), 0, 1)
    up_owned = restore(collect(up_gradient, 0), 0, 1)
    output_owned = restore(collect(output_gradient, 1), 1, 0)
    swish_owned = restore(collect(swish_gradient, 0), 0, 1)
    value_owned = restore(collect(value_gradient, 0), 0, 1)
    query_key_owned = collect(query_key_gradient, 0)
    query_owned = restore(query_key_owned[:, :KEY_DIM], 0, 1)
    key_owned = restore(query_key_owned[:, KEY_DIM:], 0, 1)
    return (
        layer_output,
        input_delta,
        gain_sums[0],
        gain_sums[1],
        query_owned,
        key_owned,
        value_owned,
        swish_owned,
        output_owned,
        gain_sums[2],
        gain_sums[3],
        gate_owned,
        up_owned,
        down_owned,
    )


def solution(mesh):
    ranks = mesh.shape["dp"]
    groups = [[2 * k + side for k in range(ranks // 2)] for side in range(2)]
    swap = [(rank, rank + 1 - 2 * (rank % 2)) for rank in range(ranks)]
    rows, gain, column, row = P(("dp", "tensor"), None), P("dp"), P("dp", "tensor"), P("tensor", "dp")
    weights = (gain, gain, column, column, column, column, row, gain, gain, column, column, row)
    return jax.shard_map(
        functools.partial(per_device, groups, swap),
        mesh=mesh,
        in_specs=(rows, rows, P("dp"), *weights),
        out_specs=(rows, rows, *weights),
        check_vma=False,
    )
```

time: 1550 us -> 704 us (0.45)
  waiting for transfers between devices: 1230 us -> 231 us
  Pallas kernels: 0 us -> 175 us
  blocking collectives: 108 us -> 68.6 us
  starting transfers between devices: 1.52 us -> 21.4 us
  local copies, waits for them, and re-layouts: 14.6 us -> 31.1 us
  other arithmetic: 47.5 us -> 31.8 us
    reduce_scatter x12 -> x7, waiting for transfers between devices: 664 us -> 74.1 us  [collect(): lax.psum_scatter(gradient, 'dp', scatter_dimension=axis, tiled=True, axis...]
    all_gather x12 -> x7, waiting for transfers between devices: 564 us -> 118 us  [spread(): lax.all_gather(block, 'dp', axis=axis, tiled=True, axis_index_groups=groups)]
    pallas_call x0 -> x4, Pallas kernels: none -> 175 us  [call(): pl.pallas_call(kernel, out_shape=outs, in_specs=specs, out_specs=out_spec...]
    all_gather x4 -> x1, blocking collectives: 68 us -> 25.2 us  [per_device(): gains = lax.all_gather(gains, 'dp', axis=1, tiled=True).astype(F32)]
    ppermute x0 -> x16, waiting for transfers between devices: none -> 39 us  [the longest x8 33.6 us: exchange(): take = lax.ppermute(give, 'dp', swap)]
    psum x1, blocking collectives: 5.64 us -> 43.3 us  [per_device(): gain_sums = lax.psum(gain_pieces, ('dp', 'tensor'))]
    unnamed x1 -> x0, blocking collectives: 34.8 us -> none
    ppermute x0 -> x16, starting transfers between devices: none -> 20.3 us  [the longest x8 10.2 us: exchange(): take = lax.ppermute(give, 'dp', swap)]
  transfers between devices with their start and end apart: 24 -> 30, of which waited for: 23 -> 15; matrix products, arithmetic and copies ran while one was open for 9% -> 22% of each run, Pallas kernels for 0% -> 25%
where the time goes in v1:
time: 704 us; the launch traced here: 697 us
  waiting for transfers between devices  231 us (33%)
  Pallas kernels  175 us (25%)
  matrix products  122 us (17%)
  blocking collectives  68.6 us (10%)
  other arithmetic  31.8 us (5%)
  local copies, waits for them, and re-layouts  31.1 us (4%)
  starting transfers between devices  21.4 us (3%)
  between operations  15.9 us (2%)
    pallas_call x4, Pallas kernels, call(): pl.pallas_call(kernel, out_shape=outs, in_specs=specs, out_specs=out_spec...  175 us
    all_gather x7, waiting for transfers between devices, spread(): lax.all_gather(block, 'dp', axis=axis, tiled=True, axis_index_groups=groups)  118 us
    dot_general x21, matrix products, matmul(): return jnp.dot(left, right, preferred_element_type=jnp.float32)  117 us
    reduce_scatter x7, waiting for transfers between devices, collect(): lax.psum_scatter(gradient, 'dp', scatter_dimension=axis, tiled=True, axis...  74.1 us
    psum x1, blocking collectives, per_device(): gain_sums = lax.psum(gain_pieces, ('dp', 'tensor'))  43.3 us
    ppermute x8, waiting for transfers between devices, exchange(): take = lax.ppermute(give, 'dp', swap)  33.6 us
    all_gather x1, blocking collectives, per_device(): gains = lax.all_gather(gains, 'dp', axis=1, tiled=True).astype(F32)  25.2 us
    unnamed x108, local copies, waits for them, and re-layouts  19.1 us
  transfers between devices with their start and end apart: 30, of which 15 were waited for; matrix products, arithmetic and copies ran while one was open for 22% of the time, Pallas kernels for 25%

profile of v1, /device:TPU:8, one launch (start us, length us, event | category | flops | bytes accessed | tf_op | source)
XLA Modules:
  0.0 696.6 jit_solution(13945638327803487939)
XLA Ops:
  19.1 6.0 collective-permute-done.2
  27.5 5.4 collective-permute-done.4
  35.0 5.4 collective-permute-done.5
  42.6 5.8 collective-permute-done.7
  50.9 6.3 collective-permute-done.3
  60.8 25.2 %all_gather.24 = bf16[4,2048]{1,0:T(4,128)(2,1)S(1)} all-gather(bf16[4,256]{1,0:T(4,128)(2,1)S(1)} %pad_maximum_fusion.6), channel_id=1, replica_groups=mesh['dp'=8,'tensor'=4] {'dp'}, dimensions={1}, use_global_device_ids=true | all-gather | bytes 18432 | tf_op jit(solution)/shard_map/all_gather | solution.py:426
  86.2 40.4 %first_kernel.1 = (bf16[1024,2048]{1,0:T(8,128)(2,1)S(1)}, bf16[1024,2048]{1,0:T(8,128)(2,1)S(1)}) custom-call(bf16[128,2048]{1,0:T(8,128)(2,1)S(1)} %copy-done, bf16[128,2048]{1,0:T(8,128)(2,1)S(1)} %broadcast_select_fusion.cot_ref, f32[8,2048]{1,0:T(8,128)S(1)} %maximum_convert_fusion.gains_ref), custom_call_target="tpu_custom_call" | custom-call | bytes 100663296 | tf_op jit(solution)/shard_map/first_kernel/pallas_call | solution.py:356
  135.0 5.2 fusion.36
  143.5 5.6 convolution_convert_fusion.10
  151.8 4.6 all-gather.14.cloned.1.call-done
  156.4 7.3 %multiply_convert_fusion.5 = (bf16[2,512,512]{2,1,0:T(8,128)(2,1)S(1)}, f32[1024,512]{1,0:T(8,128)}) fusion(f32[2,512,512]{2,1,0:T(8,128)} %copy-done.10, f32[2,512]{1,0:T(2,128)S(1)} %add_rsqrt_fusion, f32[2,512]{1,0:T(2,128)S(1)} %broadcast_multiply_fusion.3, bf16[1024,2048]{1,0:T(8,128)(2,1)} %copy-done.1, ...), kind=kOutput, calls=%fused_computation.28 | convolution fusion | flops 2151677952 | bytes 11542528 | tf_op jit(solution)/shard_map/dot_general | solution.py:64
  163.7 39.2 %all-gather.16.cloned.1.call-done = bf16[512,2048]{1,0:T(8,128)(2,1)} async-done(((bf16[512,512]{1,0:T(8,128)(2,1)}), bf16[512,2048]{1,0:T(8,128)(2,1)}) %all-gather.16.cloned.1.call-update) | async-done | bytes 2097168 | tf_op jit(solution)/shard_map/all_gather | solution.py:411
  206.9 45.0 %second_kernel.1 = (bf16[1024,2048]{1,0:T(8,128)(2,1)S(1)}, f32[128,2048]{1,0:T(8,128)S(1)}) custom-call(bf16[1024,2048]{1,0:T(8,128)(2,1)S(1)} %convolution_convert_fusion.1.part_ref, bf16[128,2048]{1,0:T(8,128)(2,1)S(1)} %copy-done, f32[8,2048]{1,0:T(8,128)S(1)} %maximum_convert_fusion.gains_ref), custom_call_target="tpu_custom_call" | custom-call | bytes 100663296 | tf_op jit(solution)/shard_map/second_kernel/pallas_call | solution.py:356
  254.0 6.5 fusion.38
  260.4 34.3 %all-gather.12.cloned.1.call-done = bf16[512,2048]{1,0:T(8,128)(2,1)} async-done(((bf16[512,512]{1,0:T(8,128)(2,1)}), bf16[512,2048]{1,0:T(8,128)(2,1)}) %all-gather.12.cloned.1.call-update) | async-done | bytes 2097168 | tf_op jit(solution)/shard_map/all_gather | solution.py:411
  294.8 6.6 fusion.37
  301.4 39.4 %all-gather.18.cloned.1.call-done = bf16[2048,512]{1,0:T(8,128)(2,1)} async-done(((bf16[512,512]{1,0:T(8,128)(2,1)}), bf16[2048,512]{1,0:T(8,128)(2,1)}) %all-gather.18.cloned.1.call-update) | async-done | bytes 2097168 | tf_op jit(solution)/shard_map/all_gather | solution.py:411
  340.8 8.9 %multiply_convert_fusion = (bf16[1024,512]{1,0:T(8,128)(2,1)}, bf16[1024,512]{1,0:T(8,128)(2,1)S(1)}, bf16[1024,512]{1,0:T(8,128)(2,1)S(1)}) fusion(f32[1024,512]{1,0:T(8,128)} %fusion.38, f32[1024,512]{1,0:T(8,128)} %fusion.37, bf16[1024,2048]{1,0:T(8,128)(2,1)} %copy-done.8, bf16[2048,512]{1,0:T(8,128)(2,1)} %all-gather.18.cloned.1.call-done), kind=kOutput, calls=%fused_computation.20 | convolution fusion | flops 2161115136 | bytes 13631488 | tf_op jit(solution)/shard_map/dot_general | solution.py:64
  354.6 5.9 convolution_convert_fusion.4
  360.7 6.4 convolution_convert_fusion.2
  367.1 4.4 fusion.39
  374.0 45.7 %third_kernel.1 = (bf16[1024,2048]{1,0:T(8,128)(2,1)S(1)}, f32[128,2048]{1,0:T(8,128)S(1)}, f32[2,8,2048]{2,1,0:T(8,128)S(1)}) custom-call(bf16[1024,2048]{1,0:T(8,128)(2,1)S(1)} %add_convert_fusion.1.part_ref, f32[128,2048]{1,0:T(8,128)S(1)} %get-tuple-element.27.middle_ref, bf16[128,2048]{1,0:T(8,128)(2,1)S(1)} %broadcast_select_fusion.cot_ref, ...), custom_call_target="tpu_custom_call" | custom-call | bytes 100663296 | tf_op jit(solution)/shard_map/third_kernel/pallas_call | solution.py:356
  440.6 6.3 convolution_convert_fusion.5
  447.0 6.2 convolution_convert_fusion.6
  456.7 5.9 convolution_convert_fusion.7
  463.7 7.6 %fusion.18 = f32[1024,2048]{1,0:T(8,128)} fusion(bf16[2048,512]{1,0:T(8,128)(2,1)} %all-gather.8.cloned.1.call-done, bf16[1024,256]{1,0:T(8,128)(2,1)} %bitcast.90, bf16[1024,256]{1,0:T(8,128)(2,1)S(1)} %bitcast.88), kind=kOutput, calls=%fused_computation.55 | convolution fusion | flops 2149580800 | bytes 11534336 | tf_op jit(solution)/shard_map/dot_general | solution.py:64
  473.7 5.7 fusion.42
  479.4 8.2 %add_convert_fusion.first_ref = bf16[1024,2048]{1,0:T(8,128)(2,1)S(1)} fusion(f32[1024,2048]{1,0:T(8,128)} %fusion.18, f32[1024,2048]{1,0:T(8,128)} %fusion.42, bf16[1024,512]{1,0:T(8,128)(2,1)S(1)} %bitcast.82, bf16[2048,512]{1,0:T(8,128)(2,1)S(1)} %copy-done.18), kind=kOutput, calls=%fused_computation | convolution fusion | flops 2153775104 | bytes 24117248 | tf_op jit(solution)/shard_map/dot_general | solution.py:64
  487.6 43.9 %fourth_kernel.1 = (f32[128,2048]{1,0:T(8,128)S(1)}, f32[128,2048]{1,0:T(8,128)S(1)}, f32[2,8,2048]{2,1,0:T(8,128)S(1)}) custom-call(bf16[1024,2048]{1,0:T(8,128)(2,1)S(1)} %add_convert_fusion.first_ref, bf16[1024,2048]{1,0:T(8,128)(2,1)S(1)} %convolution_convert_fusion.mixer_ref, bf16[128,2048]{1,0:T(8,128)(2,1)S(1)} %copy-done, ...), custom_call_target="tpu_custom_call" | custom-call | bytes 100663296 | tf_op jit(solution)/shard_map/fourth_kernel/pallas_call | solution.py:356
  535.9 43.3 %psum.7 = f32[4,2048]{1,0:T(4,128)S(1)} all-reduce(f32[4,2048]{1,0:T(4,128)S(1)} %pad_maximum_fusion.5), channel_id=1, replica_groups=mesh['dp'=8,'tensor'=4] {'dp','tensor'}, use_global_device_ids=true, to_apply=%region_6.7 | all-reduce | flops 8192 | bytes 65536 | tf_op jit(solution)/shard_map/psum | solution.py:558
  594.0 30.2 %reduce-scatter.12.cloned.1.call-done = bf16[512,512]{1,0:T(8,128)(2,1)} async-done(((bf16[2048,512]{1,0:T(8,128)(2,1)}), bf16[512,512]{1,0:T(8,128)(2,1)}) %reduce-scatter.12.cloned.1.call-update) | async-done | bytes 524304 | tf_op jit(solution)/shard_map/reduce_scatter | solution.py:563
  625.2 43.9 %reduce-scatter.10.cloned.1.call-done = bf16[512,512]{1,0:T(8,128)(2,1)} async-done(((bf16[2048,512]{1,0:T(8,128)(2,1)}), bf16[512,512]{1,0:T(8,128)(2,1)}) %reduce-scatter.10.cloned.1.call-update) | async-done | bytes 524304 | tf_op jit(solution)/shard_map/reduce_scatter | solution.py:563
  (250 shorter events, 120.1 us)
Async XLA Ops:
  7.2 127.8 %all-gather.8.cloned.1.call-start = ((), (), s32[]{:S(2)}) async-start(), calls=%async_computation.7 | async-start | bytes 2621440 | tf_op jit(solution)/shard_map/all_gather | solution.py:411
  8.3 5.8 collective-permute-start
  10.8 5.6 collective-permute-start.1
  17.4 126.1 %all-gather.10.cloned.1.call-start = ((), (), s32[]{:S(2)}) async-start(), calls=%async_computation.8 | async-start | bytes 2621440 | tf_op jit(solution)/shard_map/all_gather | solution.py:411
  17.5 7.5 %collective-permute-start.2 = (bf16[256,512]{1,0:T(8,128)(2,1)S(1)}, bf16[256,512]{1,0:T(8,128)(2,1)S(1)}, u32[]{:S(2)}, u32[]{:S(2)}) collective-permute-start(bf16[256,512]{1,0:T(8,128)(2,1)S(1)} %get-tuple-element.78), channel_id=1, source_target_pairs={{0,4},{4,0},{8,12},{12,8},{16,20},{20,16},{24,28},{28,24},{1,5},{5... | collective-permute-start | bytes 786440 | tf_op jit(solution)/shard_map/ppermute | solution.py:403
  26.0 130.4 %all-gather.14.cloned.1.call-start = ((), (), s32[]{:S(2)}) async-start(), calls=%async_computation.10 | async-start | bytes 2621440 | tf_op jit(solution)/shard_map/all_gather | solution.py:411
  26.2 6.7 collective-permute-start.4
  33.9 169.1 %all-gather.16.cloned.1.call-start = ((), (), s32[]{:S(2)}) async-start(), calls=%async_computation.11 | async-start | bytes 2621440 | tf_op jit(solution)/shard_map/all_gather | solution.py:411
  34.0 6.4 collective-permute-start.5
  41.4 212.6 %all-gather.20.cloned.1.call-start = ((), (), s32[]{:S(2)}) async-start(), calls=%async_computation.13 | async-start | bytes 2621440 | tf_op jit(solution)/shard_map/all_gather | solution.py:411
  41.5 6.9 collective-permute-start.7
  49.4 245.4 %all-gather.12.cloned.1.call-start = ((), (), s32[]{:S(2)}) async-start(), calls=%async_computation.9 | async-start | bytes 2621440 | tf_op jit(solution)/shard_map/all_gather | solution.py:411
  49.5 7.7 %collective-permute-start.3 = (bf16[512,256]{1,0:T(8,128)(2,1)S(1)}, bf16[512,256]{1,0:T(8,128)(2,1)S(1)}, u32[]{:S(2)}, u32[]{:S(2)}) collective-permute-start(bf16[512,256]{1,0:T(8,128)(2,1)S(1)} %get-tuple-element.74), channel_id=1, source_target_pairs={{0,4},{4,0},{8,12},{12,8},{16,20},{20,16},{24,28},{28,24},{1,5},{5... | collective-permute-start | bytes 786440 | tf_op jit(solution)/shard_map/ppermute | solution.py:403
  58.2 282.6 %all-gather.18.cloned.1.call-start = ((), (), s32[]{:S(2)}) async-start(), calls=%async_computation.12 | async-start | bytes 2621440 | tf_op jit(solution)/shard_map/all_gather | solution.py:411
  58.3 75.3 %collective-permute-start.6 = (bf16[256,512]{1,0:T(8,128)(2,1)S(1)}, bf16[256,512]{1,0:T(8,128)(2,1)S(1)}, u32[]{:S(2)}, u32[]{:S(2)}) collective-permute-start(bf16[256,512]{1,0:T(8,128)(2,1)S(1)} %get-tuple-element.68), channel_id=1, source_target_pairs={{0,4},{4,0},{8,12},{12,8},{16,20},{20,16},{24,28},{28,24},{1,5},{5... | collective-permute-start | bytes 786440 | tf_op jit(solution)/shard_map/ppermute | solution.py:403
  134.7 446.1 %reduce-scatter.18.cloned.1.call-start = ((), (), s32[]{:S(2)}) async-start(), calls=%async_computation.19 | async-start | bytes 2621440 | tf_op jit(solution)/shard_map/reduce_scatter | solution.py:563
  354.5 229.7 %reduce-scatter.16.cloned.1.call-start = ((), (), s32[]{:S(2)}) async-start(), calls=%async_computation.18 | async-start | bytes 2621440 | tf_op jit(solution)/shard_map/reduce_scatter | solution.py:563
  360.4 224.9 %reduce-scatter.20.cloned.1.call-start = ((), (), s32[]{:S(2)}) async-start(), calls=%async_computation.20 | async-start | bytes 2621440 | tf_op jit(solution)/shard_map/reduce_scatter | solution.py:563
  367.1 221.4 %reduce-scatter.8.cloned.1.call-start = ((), (), s32[]{:S(2)}) async-start(), calls=%async_computation.14 | async-start | bytes 2621440 | tf_op jit(solution)/shard_map/reduce_scatter | solution.py:563
  374.0 45.7 %copy-start.12 = (f32[1024,512]{1,0:T(8,128)S(1)}, f32[1024,512]{1,0:T(8,128)}, u32[]{:S(2)}) copy-start(f32[1024,512]{1,0:T(8,128)} %get-tuple-element.96) | copy-start | bytes 6291460
  440.6 152.4 %reduce-scatter.14.cloned.1.call-start = ((), (), s32[]{:S(2)}) async-start(), calls=%async_computation.17 | async-start | bytes 2621440 | tf_op jit(solution)/shard_map/reduce_scatter | solution.py:563
  446.9 177.3 %reduce-scatter.12.cloned.1.call-start = ((), (), s32[]{:S(2)}) async-start(), calls=%async_computation.16 | async-start | bytes 2621440 | tf_op jit(solution)/shard_map/reduce_scatter | solution.py:563
  453.1 216.0 %reduce-scatter.10.cloned.1.call-start = ((), (), s32[]{:S(2)}) async-start(), calls=%async_computation.15 | async-start | bytes 2621440 | tf_op jit(solution)/shard_map/reduce_scatter | solution.py:563
  533.4 46.5 %copy-start.5 = (f32[128,2048]{1,0:T(8,128)S(1)}, f32[128,2048]{1,0:T(8,128)}, u32[]{:S(2)}) copy-start(f32[128,2048]{1,0:T(8,128)} %copy-done.4) | copy-start | bytes 3145732
  581.9 93.2 %collective-permute-start.14 = (bf16[256,512]{1,0:T(8,128)(2,1)S(1)}, bf16[256,512]{1,0:T(8,128)(2,1)S(1)}, u32[]{:S(2)}, u32[]{:S(2)}) collective-permute-start(bf16[256,512]{1,0:T(8,128)(2,1)S(1)} %get-tuple-element.56), channel_id=1, source_target_pairs={{0,4},{4,0},{8,12},{12,8},{16,20},{20,16},{24,28},{28,24},{1,5},{5... | collective-permute-start | bytes 786440 | tf_op jit(solution)/shard_map/ppermute | solution.py:571
  585.3 92.4 %collective-permute-start.13 = (bf16[256,512]{1,0:T(8,128)(2,1)S(1)}, bf16[256,512]{1,0:T(8,128)(2,1)S(1)}, u32[]{:S(2)}, u32[]{:S(2)}) collective-permute-start(bf16[256,512]{1,0:T(8,128)(2,1)S(1)} %get-tuple-element.58), channel_id=1, source_target_pairs={{0,4},{4,0},{8,12},{12,8},{16,20},{20,16},{24,28},{28,24},{1,5},{5... | collective-permute-start | bytes 786440 | tf_op jit(solution)/shard_map/ppermute | solution.py:571
  586.4 92.4 %collective-permute-start.15 = (bf16[512,256]{1,0:T(8,128)(2,1)S(1)}, bf16[512,256]{1,0:T(8,128)(2,1)}, u32[]{:S(2)}, u32[]{:S(2)}) collective-permute-start(bf16[512,256]{1,0:T(8,128)(2,1)S(1)} %get-tuple-element.54), channel_id=1, source_target_pairs={{0,4},{4,0},{8,12},{12,8},{16,20},{20,16},{24,28},{28,24},{1,5},{5... | collective-permute-start | bytes 786440 | tf_op jit(solution)/shard_map/ppermute | solution.py:571
  590.2 80.0 %collective-permute-start.9 = (bf16[256,256]{1,0:T(8,128)(2,1)}, bf16[256,256]{1,0:T(8,128)(2,1)}, u32[]{:S(2)}, u32[]{:S(2)}) collective-permute-start(bf16[256,256]{1,0:T(8,128)(2,1)} %get-tuple-element.80), channel_id=1, source_target_pairs={{0,4},{4,0},{8,12},{12,8},{16,20},{20,16},{24,28},{28,24},{1,5},{5... | collective-permute-start | bytes 393224 | tf_op jit(solution)/shard_map/ppermute | solution.py:571
  591.1 82.6 %collective-permute-start.8 = (bf16[256,256]{1,0:T(8,128)(2,1)}, bf16[256,256]{1,0:T(8,128)(2,1)S(1)}, u32[]{:S(2)}, u32[]{:S(2)}) collective-permute-start(bf16[256,256]{1,0:T(8,128)(2,1)} %get-tuple-element.82), channel_id=1, source_target_pairs={{0,4},{4,0},{8,12},{12,8},{16,20},{20,16},{24,28},{28,24},{1,5},{5... | collective-permute-start | bytes 393224 | tf_op jit(solution)/shard_map/ppermute | solution.py:571
  670.3 10.7 %collective-permute-start.12 = (bf16[512,256]{1,0:T(8,128)(2,1)S(1)}, bf16[512,256]{1,0:T(8,128)(2,1)S(1)}, u32[]{:S(2)}, u32[]{:S(2)}) collective-permute-start(bf16[512,256]{1,0:T(8,128)(2,1)S(1)} %get-tuple-element.60), channel_id=1, source_target_pairs={{0,4},{4,0},{8,12},{12,8},{16,20},{20,16},{24,28},{28,24},{1,5},{5... | collective-permute-start | bytes 786440 | tf_op jit(solution)/shard_map/ppermute | solution.py:571
  673.6 11.5 %collective-permute-start.11 = (bf16[256,512]{1,0:T(8,128)(2,1)S(1)}, bf16[256,512]{1,0:T(8,128)(2,1)S(1)}, u32[]{:S(2)}, u32[]{:S(2)}) collective-permute-start(bf16[256,512]{1,0:T(8,128)(2,1)S(1)} %get-tuple-element.62), channel_id=1, source_target_pairs={{0,4},{4,0},{8,12},{12,8},{16,20},{20,16},{24,28},{28,24},{1,5},{5... | collective-permute-start | bytes 786440 | tf_op jit(solution)/shard_map/ppermute | solution.py:571
  675.1 13.4 %collective-permute-start.10 = (bf16[256,512]{1,0:T(8,128)(2,1)S(1)}, bf16[256,512]{1,0:T(8,128)(2,1)S(1)}, u32[]{:S(2)}, u32[]{:S(2)}) collective-permute-start(bf16[256,512]{1,0:T(8,128)(2,1)S(1)} %get-tuple-element.64), channel_id=1, source_target_pairs={{0,4},{4,0},{8,12},{12,8},{16,20},{20,16},{24,28},{28,24},{1,5},{5... | collective-permute-start | bytes 786440 | tf_op jit(solution)/shard_map/ppermute | solution.py:571
  (52 other events, 367.8 us)
Sparse Core Ops, SparseCore 0:
  17.5 45.4 all-gather.7
  65.2 44.4 all-gather.9
  111.9 44.5 all-gather.13
  158.4 44.4 all-gather.15
  204.3 44.4 all-gather.19
  250.3 44.4 all-gather.11
  296.3 44.4 all-gather.17
  354.6 42.8 reduce-scatter.17
  399.9 42.8 reduce-scatter.15
  444.9 42.8 reduce-scatter.19
  490.1 42.8 reduce-scatter.7
  535.1 43.8 reduce-scatter.13
  581.3 42.8 reduce-scatter.11
  626.3 42.8 reduce-scatter.9

commit v2 on v1

--- a/solution.py
+++ b/solution.py
@@ -2,6 +2,7 @@
 
 import jax
 import jax.numpy as jnp
+import numpy as np
 from jax import lax
 from jax.experimental import pallas as pl
 from jax.experimental.pallas import tpu as pltpu
@@ -602,14 +603,987 @@
     )
 
 
+PLANES = 4
+QK, VALUE, SWISH, OUTPUT, GATE, UP, DOWN = range(7)
+WIDE = 512
+TILE = 256
+
+
+def nt(left, right):
+    return lax.dot_general(left, right, (((1,), (1,)), ((), ())), preferred_element_type=F32)
+
+
+def loop(count, body):
+    def step(i, carry):
+        body(i)
+        return carry
+
+    lax.fori_loop(0, count, step, 0)
+
+
+def at(index, size):
+    return pl.ds(pl.multiple_of(index * size, size), size)
+
+
+def mega_scratch(rows, hidden):
+    total = 8 * rows
+    dma = pltpu.SemaphoreType.DMA
+    return dict(
+        w=pltpu.VMEM((7, hidden, WIDE), BF16),
+        xs=pltpu.VMEM((total, hidden), BF16),
+        xt=pltpu.VMEM((hidden, total), BF16),
+        outs=pltpu.VMEM((total, hidden), BF16),
+        part=pltpu.VMEM((total, hidden), BF16),
+        theirs=pltpu.VMEM((4, rows, hidden), BF16),
+        got=pltpu.VMEM((2, rows, hidden), BF16),
+        across=pltpu.VMEM((2, rows // 2, hidden), BF16),
+        q=pltpu.VMEM((total, KEY_DIM), BF16),
+        k=pltpu.VMEM((total, KEY_DIM), BF16),
+        v=pltpu.VMEM((total, VAL_DIM), BF16),
+        sc=pltpu.VMEM((total, SEQ_LEN), BF16),
+        swish=pltpu.VMEM((total, VAL_DIM), F32),
+        ghat=pltpu.VMEM((total, VAL_DIM), F32),
+        ginv=pltpu.VMEM((total, 128), F32),
+        gated=pltpu.VMEM((total, VAL_DIM), BF16),
+        hid=pltpu.VMEM((total, WIDE), BF16),
+        gate=pltpu.VMEM((total, WIDE), F32),
+        up=pltpu.VMEM((total, WIDE), F32),
+        gb=pltpu.VMEM((total, WIDE), BF16),
+        ub=pltpu.VMEM((total, WIDE), BF16),
+        sb=pltpu.VMEM((total, SEQ_LEN), BF16),
+        qkb=pltpu.VMEM((total, 2 * KEY_DIM), BF16),
+        turned=pltpu.VMEM((WIDE, total), BF16),
+        st=pltpu.VMEM((4, WIDE, WIDE), BF16),
+        decay=pltpu.VMEM((SEQ_LEN, SEQ_LEN), F32),
+        low=pltpu.VMEM((rows, hidden), BF16),
+        middle=pltpu.VMEM((rows, hidden), F32),
+        back=pltpu.VMEM((rows, hidden), F32),
+        pieces=pltpu.VMEM((4, 8, hidden), F32),
+        gparts=pltpu.VMEM((8, 8, 256), F32),
+        gain=pltpu.VMEM((8, hidden), F32),
+        gsend=pltpu.VMEM((8, 8, 256), F32),
+        gsum=pltpu.VMEM((4, 8, 256), F32),
+        ex_s=dma((8,)),
+        ex_r=dma((8,)),
+        ex_l=dma((8,)),
+        zs=dma((7, 5)),
+        zr=dma((7, 4)),
+        rs=dma((7, 4)),
+        rr=dma((7, 4)),
+        ra=dma((7,)),
+        stl=dma((4,)),
+        fl=dma((4,)),
+        fe_s=dma((8,)),
+        fe_r=dma((8,)),
+        gg_s=dma((8,)),
+        gg_r=dma((8,)),
+        gt_s=dma((4,)),
+        gt_r=dma((4,)),
+        ga_s=dma((13,)),
+        ga_r=dma((13,)),
+        gc_s=dma((13,)),
+        gc_r=dma((13,)),
+        re_s=dma((10,)),
+        re_r=dma((10,)),
+        ol=dma((4,)),
+        free=pltpu.SemaphoreType.REGULAR,
+    )
+
+
+class PlaneSum(Reduce):
+    def __init__(self, place, part, theirs, got, across, send, recv):
+        p = place
+        rows = theirs.shape[1]
+        h = rows // 2
+        self.rows, self.half, self.part = rows, h, part
+        self.theirs, self.got, self.across = theirs, got, across
+        self.base = [p.block(j) * rows for j in range(4)]
+
+        def remote(k, source, target_ref, target):
+            return pltpu.make_async_remote_copy(
+                src_ref=source,
+                dst_ref=target_ref,
+                send_sem=send.at[k],
+                recv_sem=recv.at[k],
+                device_id=target,
+                device_id_type=MESH,
+            )
+
+        def piece(j, lo):
+            return part.at[pl.ds(pl.multiple_of(self.base[j] + lo, 8), h)]
+
+        a, b = pl.ds(0, h), pl.ds(h, h)
+        self.swap = [
+            remote(j, part.at[rows_of(p.block(j, 1), rows)], theirs.at[j], p.sib) for j in range(4)
+        ]
+        self.da = remote(4, piece(3, 0), across.at[0], p.xn)
+        self.db = remote(5, piece(3, h), across.at[1], p.yn)
+        self.xa = remote(6, piece(1, 0), got.at[0, a], p.xn)
+        self.xb = remote(7, piece(1, h), got.at[0, b], p.xn)
+        self.ya = remote(8, piece(2, 0), got.at[1, a], p.yn)
+        self.yb = remote(9, piece(2, h), got.at[1, b], p.yn)
+
+    def add(self, j, lo, n, other, other_lo):
+        def body(i):
+            r = pl.ds(pl.multiple_of(self.base[j] + lo + i * CHUNK, CHUNK), CHUNK)
+            q = pl.ds(pl.multiple_of(other_lo + i * CHUNK, CHUNK), CHUNK)
+            self.part[r] = (self.part[r].astype(F32) + other[q].astype(F32)).astype(BF16)
+
+        loop(n // CHUNK, body)
+
+    def start(self):
+        for j in (3, 1, 2, 0):
+            self.swap[j].start()
+
+    def run(self):
+        rows, h = self.rows, self.half
+        for j, copies in ((3, (self.da, self.db)), (1, (self.xa,)), (2, (self.yb,))):
+            self.swap[j].wait_recv()
+            self.add(j, 0, rows, self.theirs.at[j], 0)
+            for copy in copies:
+                copy.start()
+        self.db.wait_recv()
+        self.add(1, h, h, self.across.at[1], 0)
+        self.xb.start()
+        self.da.wait_recv()
+        self.add(2, 0, h, self.across.at[0], 0)
+        self.ya.start()
+        self.swap[0].wait_recv()
+        for copy in (self.xa, self.yb, self.xb, self.ya):
+            copy.wait_recv()
+
+    def total(self, i):
+        r = pl.ds(pl.multiple_of(i * CHUNK, CHUNK), CHUNK)
+        mine = pl.ds(pl.multiple_of(self.base[0] + i * CHUNK, CHUNK), CHUNK)
+        pieces = (self.part[mine], self.theirs[0, r], self.got[0, r], self.got[1, r])
+        one, two, three, four = (piece.astype(F32) for piece in pieces)
+        return (one + two) + (three + four)
+
+
+def mega_kernel(names, count_in, count_out, *refs):
+    x_ref, cot_ref, gains_ref, cos_ref, sin_ref, rate_ref = refs[:6]
+    q_w, k_w, v_w, s_w, o_w, g_w, u_w, d_w = refs[6:count_in]
+    outs = refs[count_in : count_in + count_out]
+    final_out, delta_out, gains_out, q_g, k_g, v_g, s_g, o_g, g_g, u_g, d_g, stage, heard, added = outs
+    b = {name: ref for name, ref in zip(names, refs[count_in + count_out :], strict=True)}
+    w, xs, xt, st, part, turned = b["w"], b["xs"], b["xt"], b["st"], b["part"], b["turned"]
+    rows, hidden = x_ref.shape
+    width = hidden // 8
+
+    dp, tensor = lax.axis_index("dp"), lax.axis_index("tensor")
+    place = Place()
+    x, z = place.x, dp // 2
+    mid = (z == 1) | (z == 2)
+    end = (z == 0) | (z == 3)
+
+    barrier = pltpu.get_barrier_semaphore()
+    for i in range(1, 8):
+        other = (lax.rem(dp + i, 8), tensor)
+        pl.semaphore_signal(barrier, inc=1, device_id=other, device_id_type=MESH)
+    for i in range(1, 4):
+        other = (dp, lax.rem(tensor + i, 4))
+        pl.semaphore_signal(barrier, inc=1, device_id=other, device_id_type=MESH)
+    pl.semaphore_wait(barrier, 10)
+
+    def remote(source, target_ref, send, recv, target):
+        return pltpu.make_async_remote_copy(
+            src_ref=source,
+            dst_ref=target_ref,
+            send_sem=send,
+            recv_sem=recv,
+            device_id=target,
+            device_id_type=MESH,
+        )
+
+    def plane(step):
+        return ((z + step) * 2 + x, tensor)
+
+    def column_exchange(n, weight, k, lane, half):
+        where = w.at[k, pl.ds(pl.multiple_of(z * 512 + x * 256, 256), width), pl.ds(lane, half)]
+        keep = pltpu.make_async_copy(weight.at[:, at(x, half)], where, b["ex_l"].at[n])
+        give = remote(
+            weight.at[:, at(1 - x, half)], where, b["ex_s"].at[n], b["ex_r"].at[n], place.xn
+        )
+        return keep, give
+
+    def row_exchange(n, weight, k):
+        where = w.at[k, at(z, 512), at(x, width)]
+        keep = pltpu.make_async_copy(weight.at[at(x, 512)], where, b["ex_l"].at[n])
+        give = remote(weight.at[at(1 - x, 512)], where, b["ex_s"].at[n], b["ex_r"].at[n], place.xn)
+        return keep, give
+
+    exchanges = [
+        [column_exchange(0, q_w, QK, 0, 256), column_exchange(1, k_w, QK, 256, 256)],
+        [column_exchange(2, v_w, VALUE, 0, 512)],
+        [column_exchange(3, s_w, SWISH, 0, 512)],
+        [row_exchange(4, o_w, OUTPUT)],
+        [column_exchange(5, g_w, GATE, 0, 512)],
+        [column_exchange(6, u_w, UP, 0, 512)],
+        [row_exchange(7, d_w, DOWN)],
+    ]
+
+    def give(k):
+        for keep, send in exchanges[k]:
+            send.start()
+            keep.start()
+
+    steps = (2, -2, 1, -1)
+
+    def block_copy(k, block, step, slot):
+        ref = w.at[k, at(block, 512)]
+        return remote(ref, ref, b["zs"].at[k, slot], b["zr"].at[k, block], plane(step))
+
+    def reaches(step):
+        return (z + step >= 0) & (z + step < PLANES)
+
+    def spread(k):
+        for keep, send in exchanges[k]:
+            keep.wait()
+            send.wait_recv()
+        for slot, step in enumerate(steps):
+
+            @pl.when(reaches(step))
+            def _(slot=slot, step=step):
+                block_copy(k, z, step, slot).start()
+
+    far = jnp.where(z == 1, 3, 0)
+
+    def pass_on(k):
+        @pl.when(z == 1)
+        def _():
+            block_copy(k, 3, 1, 4).wait_recv()
+            block_copy(k, 3, -1, 4).start()
+
+        @pl.when(z == 2)
+        def _():
+            block_copy(k, 0, 1, 4).wait_recv()
+            block_copy(k, 0, 1, 4).start()
+
+    def arrive(k):
+        for block in range(PLANES):
+            skip = (z == block) | ((z == 1) & (block == 3)) | ((z == 2) & (block == 0))
+
+            @pl.when(jnp.logical_not(skip))
+            def _(block=block):
+                block_copy(k, block, 1, 4).wait_recv()
+
+    def weights_sent():
+        for k in range(7):
+            for _, send in exchanges[k]:
+                send.wait_send()
+            for slot, step in enumerate(steps):
+
+                @pl.when(reaches(step))
+                def _(k=k, slot=slot, step=step):
+                    block_copy(k, z, step, slot).wait_send()
+
+            @pl.when(mid)
+            def _(k=k):
+                block_copy(k, z, 1, 4).wait_send()
+
+    def direct(c, step, slot, to_added=False):
+        if to_added:
+            block = 3 - z
+            target, sem = added.at[c], b["ra"].at[c]
+        else:
+            block = z + step
+            target, sem = heard.at[c, z], b["rr"].at[c, z]
+        return remote(stage.at[c, block], target, b["rs"].at[c, slot], sem, plane(step))
+
+    def staged(c, block, slot):
+        return pltpu.make_async_copy(st.at[slot], stage.at[c, block], b["stl"].at[slot])
+
+    def send_gradient(c):
+        for block in range(PLANES):
+            staged(c, block, block).wait()
+        for here, step in ((0, 1), (3, -1)):
+
+            @pl.when(z == here)
+            def _(step=step):
+                direct(c, step, 0, True).start()
+                direct(c, 2 * step, 1).start()
+                direct(c, step, 2).start()
+
+        @pl.when(mid)
+        def _():
+            direct(c, 1, 1).start()
+            direct(c, -1, 2).start()
+
+    def rounds(count, body):
+        def step(i):
+            body(pl.ds(pl.multiple_of(i * 32, 32), 32))
+
+        loop(count // 32, step)
+
+    def combine(c):
+        for here, step in ((1, 2), (2, -2)):
+
+            @pl.when(z == here)
+            def _(here=here, step=step):
+                there = here + step
+                remote(
+                    stage.at[c, 0], added.at[c], b["rs"].at[c, 0], b["ra"].at[c], plane(step)
+                ).wait_recv()
+                one = pltpu.make_async_copy(added.at[c], st.at[0], b["fl"].at[0])
+                two = pltpu.make_async_copy(stage.at[c, there], st.at[1], b["fl"].at[1])
+                one.start()
+                two.start()
+                one.wait()
+                two.wait()
+
+                def body(r):
+                    st[2, r] = (st[0, r].astype(F32) + st[1, r].astype(F32)).astype(BF16)
+
+                rounds(WIDE, body)
+                three = pltpu.make_async_copy(st.at[2], stage.at[c, there], b["fl"].at[2])
+                three.start()
+                three.wait()
+                direct(c, step, 0).start()
+
+    col_homes = {VALUE: v_g, SWISH: s_g, GATE: g_g, UP: u_g}
+    row_homes = {OUTPUT: o_g, DOWN: d_g}
+
+    def homes(c):
+        if c == QK:
+            return [
+                ((at(x, 256), pl.ds(0, 256)), (at(1 - x, 256), pl.ds(0, 256)), q_g, 0),
+                ((at(x, 256), pl.ds(256, 256)), (at(1 - x, 256), pl.ds(256, 256)), k_g, 7),
+            ]
+        if c in col_homes:
+            every = pl.ds(0, 512)
+            return [((at(x, 256), every), (at(1 - x, 256), every), col_homes[c], c)]
+        every = pl.ds(0, 512)
+        return [((every, at(x, 256)), (every, at(1 - x, 256)), row_homes[c], c)]
+
+    def home_slot(c, home):
+        if c in row_homes:
+            return home.at[at(x, 512)]
+        half = home.shape[1] // 2
+        return home.at[:, at(x, half)]
+
+    def home_copies(c):
+        for kept, given, home, n in homes(c):
+            slot = home_slot(c, home)
+            yield (
+                pltpu.make_async_copy(st.at[0].at[kept], slot, b["fl"].at[1 if n == 7 else 0]),
+                remote(
+                    stage.at[c, z].at[given],
+                    slot,
+                    b["fe_s"].at[n],
+                    b["fe_r"].at[n],
+                    place.xn,
+                ),
+            )
+
+    def finish_gradient(c):
+        own = pltpu.make_async_copy(stage.at[c, z], st.at[0], b["fl"].at[0])
+        own.start()
+        for src in range(PLANES):
+            here = (jnp.abs(z - src) <= 2) & (z != src)
+
+            @pl.when(here)
+            def _(src=src):
+                remote(
+                    stage.at[c, 0], heard.at[c, src], b["rs"].at[c, 3], b["rr"].at[c, src], plane(1)
+                ).wait_recv()
+
+        def load(src, slot):
+            return pltpu.make_async_copy(heard.at[c, src], st.at[slot], b["fl"].at[slot])
+
+        sources = {0: (1, 2), 1: (0, 2, 3), 2: (0, 1, 3), 3: (1, 2)}
+        for here, srcs in sources.items():
+
+            @pl.when(z == here)
+            def _(srcs=srcs):
+                for slot, src in enumerate(srcs):
+                    load(src, slot + 1).start()
+                for slot, src in enumerate(srcs):
+                    load(src, slot + 1).wait()
+
+        own.wait()
+
+        @pl.when(end)
+        def _():
+            def body(r):
+                st[0, r] = (st[0, r].astype(F32) + (st[1, r].astype(F32) + st[2, r].astype(F32))).astype(BF16)
+
+            rounds(WIDE, body)
+
+        @pl.when(mid)
+        def _():
+            def body(r):
+                st[0, r] = (
+                    (st[0, r].astype(F32) + st[1, r].astype(F32))
+                    + (st[2, r].astype(F32) + st[3, r].astype(F32))
+                ).astype(BF16)
+
+            rounds(WIDE, body)
+
+        store = pltpu.make_async_copy(st.at[0], stage.at[c, z], b["fl"].at[2])
+        store.start()
+        copies = list(home_copies(c))
+        for keep, _ in copies:
+            keep.start()
+        store.wait()
+        for _, send in copies:
+            send.start()
+        for keep, _ in copies:
+            keep.wait()
+
+    def gradients_done():
+        for c in range(7):
+            for _, send in home_copies(c):
+                send.wait()
+            for here, step in ((0, 1), (3, -1)):
+
+                @pl.when(z == here)
+                def _(c=c, step=step):
+                    direct(c, step, 0, True).wait_send()
+                    direct(c, 2 * step, 1).wait_send()
+                    direct(c, step, 2).wait_send()
+
+            for here, step in ((1, 2), (2, -2)):
+
+                @pl.when(z == here)
+                def _(c=c, step=step):
+                    direct(c, step, 0).wait_send()
+                    direct(c, 1, 1).wait_send()
+                    direct(c, -1, 2).wait_send()
+
+    def gain_copy(i):
+        target = lax.rem(dp + i, 8)
+        return remote(
+            gains_ref, b["gparts"].at[dp], b["gg_s"].at[i], b["gg_r"].at[dp], (target, tensor)
+        )
+
+    def gain_arrival(i):
+        source = lax.rem(dp + i, 8)
+        return remote(
+            gains_ref, b["gparts"].at[source], b["gg_s"].at[i], b["gg_r"].at[source], (source, tensor)
+        )
+
+    gather_sems = (b["ga_s"], b["ga_r"])
+
+    def plane_sum(ref):
+        return PlaneSum(place, ref, b["theirs"], b["got"], b["across"], b["re_s"], b["re_r"])
+
+    give(QK)
+    for i in range(1, 8):
+        gain_copy(i).start()
+    give(VALUE)
+    mine = pltpu.make_async_copy(gains_ref, b["gparts"].at[dp], b["ol"].at[0])
+    mine.start()
+    rate = rate_ref[0:1, 0:1]
+
+    def body(i):
+        r = at(i, 64)
+        n = lax.broadcasted_iota(jnp.int32, (64, SEQ_LEN), 0) + i * 64
+        m = lax.broadcasted_iota(jnp.int32, (64, SEQ_LEN), 1)
+        gap = n - m
+        b["decay"][r] = jnp.where(gap >= 0, jnp.exp(jnp.maximum(gap, 0).astype(F32) * rate), 0.0)
+
+    loop(SEQ_LEN // 64, body)
+    spread(QK)
+    mine.wait()
+    for i in range(1, 8):
+        gain_arrival(i).wait_recv()
+    for i in range(8):
+        b["gain"][:, i * 256 : (i + 1) * 256] = b["gparts"][i]
+    gain = b["gain"]
+    low = b["low"]
+
+    def body(i):
+        r = at(i, CHUNK)
+        hat, _ = normalize(x_ref[r].astype(F32), EPSILON)
+        low[r] = (hat * gain[0:1, :] + gain[1:2, :]).astype(BF16)
+
+    loop(rows // CHUNK, body)
+    first = Gather(place, low, xs, *gather_sems)
+    first.start()
+    spread(VALUE)
+    first.forward()
+    for k in range(SWISH, DOWN + 1):
+        give(k)
+    cotangent = Gather(place, cot_ref, b["outs"], b["gc_s"], b["gc_r"])
+    cotangent.start()
+    first.finish()
+
+    def body(i):
+        xt[at(i, 256), :] = xs[:, at(i, 256)].T
+
+    loop(hidden // 256, body)
+
+    pass_on(QK)
+    spread(SWISH)
+    arrive(QK)
+
+    def turn(acc, tile, scale):
+        spot = at(lax.rem(tile, SEQ_LEN // TILE), TILE)
+        cos, sin = cos_ref[spot], sin_ref[spot]
+        one, two = acc[:, :128], acc[:, 128:]
+        return (((one * cos - two * sin) * scale).astype(BF16), ((two * cos + one * sin) * scale).astype(BF16))
+
+    def body(i):
+        r = at(i, TILE)
+        acc = matmul(xs[r], w[QK])
+        b["q"][r, :128], b["q"][r, 128:] = turn(acc[:, :KEY_DIM], i, 1.0)
+        b["k"][r, :128], b["k"][r, 128:] = turn(acc[:, KEY_DIM:], i, KEY_DIM ** (-0.5))
+
+    tiles = 8 * rows // TILE
+    per_slot = SEQ_LEN // TILE
+    loop(tiles, body)
+
+    def slot_rows(i):
+        return at(i // per_slot, SEQ_LEN)
+
+    def body(i):
+        r = at(i, TILE)
+        decay = b["decay"][at(lax.rem(i, per_slot), TILE)]
+        b["sc"][r] = (nt(b["q"][r], b["k"][slot_rows(i)]) * decay).astype(BF16)
+
+    loop(tiles, body)
+
+    pass_on(VALUE)
+    spread(OUTPUT)
+    arrive(VALUE)
+
+    def body(i):
+        r = at(i, TILE)
+        b["v"][r] = matmul(xs[r], w[VALUE]).astype(BF16)
+
+    loop(tiles, body)
+
+    def body(i):
+        r = at(i, TILE)
+        retained = matmul(b["sc"][r], b["v"][slot_rows(i)])
+        hat, inverse = normalize(retained, GROUP_EPSILON)
+        b["ghat"][r] = hat
+        b["ginv"][r] = jnp.broadcast_to(inverse, (TILE, 128))
+
+    loop(tiles, body)
+    cotangent.forward()
+    cotangent.finish()
+
+    pass_on(SWISH)
+    spread(GATE)
+    arrive(SWISH)
+
+    def body(i):
+        r = at(i, TILE)
+        swish = matmul(xs[r], w[SWISH])
+        b["swish"][r] = swish
+        b["gated"][r] = (swish * jax.nn.sigmoid(swish) * b["ghat"][r]).astype(BF16)
+
+    loop(tiles, body)
+
+    pass_on(OUTPUT)
+    spread(UP)
+    arrive(OUTPUT)
+
+    def grid_of(i):
+        return at(i // PLANES, TILE), at(lax.rem(i, PLANES), 512)
+
+    def body(i):
+        r, c = grid_of(i)
+        part[r, c] = matmul(b["gated"][r], w[OUTPUT, c]).astype(BF16)
+
+    loop(tiles * PLANES, body)
+    reduce = plane_sum(part)
+    reduce.start()
+    reduce.run()
+
+    def body(i):
+        r = at(i, CHUNK)
+        middle = x_ref[r].astype(F32) + reduce.total(i)
+        b["middle"][r] = middle
+        hat, _ = normalize(middle, EPSILON)
+        low[r] = (hat * gain[2:3, :] + gain[3:4, :]).astype(BF16)
+
+    loop(rows // CHUNK, body)
+    second = Gather(place, low, xs, *gather_sems)
+    second.start()
+    pass_on(GATE)
+    spread(DOWN)
+    second.forward()
+    second.finish()
+    reduce.finish()
+
+    arrive(GATE)
+
+    def body(i):
+        r = at(i, TILE)
+        b["gate"][r] = matmul(xs[r], w[GATE])
+
+    loop(tiles, body)
+    pass_on(UP)
+    arrive(UP)
+
+    def gelu_of(t):
+        inner = 0.7978845608028654 * (t + 0.044715 * t * t * t)
+        return 0.5 * (1.0 + jnp.tanh(inner)), jnp.tanh(inner)
+
+    def body(i):
+        r = at(i, TILE)
+        up = matmul(xs[r], w[UP])
+        b["up"][r] = up
+        gate = b["gate"][r]
+        share, _ = gelu_of(gate)
+        b["hid"][r] = (gate * share * up).astype(BF16)
+
+    loop(tiles, body)
+
+    def turned_of(ref):
+        def body(i):
+            turned[:, at(i, TILE)] = ref[at(i, TILE)].T
+
+        loop(tiles, body)
+
+    def stage_block(c, i, value):
+        st[i] = value.astype(BF16)
+        staged(c, i, i).start()
+
+    turned_of(b["hid"])
+
+    def body(i):
+        stage_block(DOWN, i, matmul(turned[...], b["outs"][:, at(i, 512)]))
+
+    loop(PLANES, body)
+    send_gradient(DOWN)
+    pass_on(DOWN)
+    arrive(DOWN)
+
+    def times_turned(left, r, k):
+        acc = nt(left[r, 0:512], w[k, 0:512])
+        for plane_at in range(1, PLANES):
+            lanes = slice(plane_at * 512, plane_at * 512 + 512)
+            acc = acc + nt(left[r, lanes], w[k, lanes])
+        return acc
+
+    def body(i):
+        r = at(i, TILE)
+        back = times_turned(b["outs"], r, DOWN)
+        gate, up = b["gate"][r], b["up"][r]
+        share, tanh = gelu_of(gate)
+        slope = 0.5 * gate * (1.0 - tanh * tanh) * (0.7978845608028654 * (1.0 + 0.134145 * gate * gate))
+        b["gb"][r] = (back * up * (share + slope)).astype(BF16)
+        b["ub"][r] = (back * gate * share).astype(BF16)
+
+    loop(tiles, body)
+
+    def body(i):
+        r, c = grid_of(i)
+        part[r, c] = (nt(b["gb"][r], w[GATE, c]) + nt(b["ub"][r], w[UP, c])).astype(BF16)
+
+    loop(tiles * PLANES, body)
+    reduce = plane_sum(part)
+    reduce.start()
+
+    def weight_gradient(c, right):
+        def body(i):
+            def body_turn(j):
+                turned[:, at(j, TILE)] = xs[at(j, TILE), at(i, 512)].T
+
+            loop(tiles, body_turn)
+            stage_block(c, i, matmul(turned[...], right[...]))
+
+        loop(PLANES, body)
+        send_gradient(c)
+
+    weight_gradient(GATE, b["gb"])
+    reduce.run()
+    b["pieces"][...] = jnp.zeros_like(b["pieces"])
+
+    def body(i):
+        r = at(i, CHUNK)
+        upstream = reduce.total(i)
+        hat, inverse = normalize(b["middle"][r], EPSILON)
+        scaled = upstream * hat
+        b["pieces"][2] += scaled[0:8] + scaled[8:16]
+        b["pieces"][3] += upstream[0:8] + upstream[8:16]
+        back = cot_ref[r].astype(F32) + normalize_back(upstream * gain[2:3, :], hat, inverse)
+        b["back"][r] = back
+        low[r] = back.astype(BF16)
+
+    loop(rows // CHUNK, body)
+    third = Gather(place, low, b["outs"], *gather_sems)
+    third.start()
+    weight_gradient(UP, b["ub"])
+    third.forward()
+    combine(DOWN)
+
+    def body(i):
+        r, c = grid_of(i)
+        xs[r, c] = matmul(b["hid"][r], w[DOWN, c]).astype(BF16)
+
+    loop(tiles * PLANES, body)
+    third.finish()
+    reduce.finish()
+
+    turned_of(b["gated"])
+
+    def body(i):
+        stage_block(OUTPUT, i, matmul(turned[...], b["outs"][:, at(i, 512)]))
+
+    loop(PLANES, body)
+    send_gradient(OUTPUT)
+    combine(GATE)
+    swb, rb, vlow = b["gb"], b["hid"], b["ub"]
+
+    def body(i):
+        r = at(i, TILE)
+        back = times_turned(b["outs"], r, OUTPUT)
+        swish, hat = b["swish"][r], b["ghat"][r]
+        gate = jax.nn.sigmoid(swish)
+        swb[r] = (back * hat * gate * (1.0 + swish * (1.0 - gate))).astype(BF16)
+        rb[r] = normalize_back(back * swish * gate, hat, b["ginv"][r, 0:1]).astype(BF16)
+
+    loop(tiles, body)
+
+    def projection_gradient(c, right):
+        def body(i):
+            stage_block(c, i, matmul(xt[at(i, 512)], right[...]))
+
+        loop(PLANES, body)
+        send_gradient(c)
+
+    projection_gradient(SWISH, swb)
+
+    def body(i):
+        r = at(i, TILE)
+        decay = b["decay"][at(lax.rem(i, per_slot), TILE)]
+        b["sb"][r] = (nt(rb[r], b["v"][slot_rows(i)]) * decay).astype(BF16)
+
+    loop(tiles, body)
+    turned_of(b["sc"])
+
+    def body(i):
+        vlow[at(i, TILE)] = matmul(
+            turned[at(lax.rem(i, per_slot), TILE), slot_rows(i)], rb[slot_rows(i)]
+        ).astype(BF16)
+
+    loop(tiles, body)
+    projection_gradient(VALUE, vlow)
+    combine(UP)
+    turned_of(b["sb"])
+
+    def turn_back(acc, tile, scale):
+        spot = at(lax.rem(tile, per_slot), TILE)
+        cos, sin = cos_ref[spot], sin_ref[spot]
+        one, two = acc[:, :128], acc[:, 128:]
+        return (((one * cos + two * sin) * scale).astype(BF16), ((two * cos - one * sin) * scale).astype(BF16))
+
+    def body(i):
+        r = at(i, TILE)
+        qkb = b["qkb"]
+        query = matmul(b["sb"][r], b["k"][slot_rows(i)])
+        qkb[r, 0:128], qkb[r, 128:256] = turn_back(query, i, 1.0)
+        key = matmul(turned[at(lax.rem(i, per_slot), TILE), slot_rows(i)], b["q"][slot_rows(i)])
+        qkb[r, 256:384], qkb[r, 384:512] = turn_back(key, i, KEY_DIM ** (-0.5))
+
+    loop(tiles, body)
+    projection_gradient(QK, b["qkb"])
+    combine(OUTPUT)
+
+    def body(i):
+        r, c = grid_of(i)
+        part[r, c] = (
+            nt(b["qkb"][r], w[QK, c]) + nt(vlow[r], w[VALUE, c]) + nt(swb[r], w[SWISH, c])
+        ).astype(BF16)
+
+    loop(tiles * PLANES, body)
+    finish_gradient(DOWN)
+    combine(SWISH)
+
+    reduce = plane_sum(xs)
+    reduce.start()
+    reduce.run()
+
+    def body(i):
+        b["middle"][at(i, CHUNK)] += reduce.total(i)
+
+    loop(rows // CHUNK, body)
+    reduce.finish()
+    for partner in (place.sib, place.xn, place.yn):
+        pl.semaphore_signal(b["free"], inc=1, device_id=partner, device_id_type=MESH)
+    final_copy = pltpu.make_async_copy(b["middle"], final_out, b["ol"].at[1])
+    final_copy.start()
+    finish_gradient(GATE)
+    combine(VALUE)
+    pl.semaphore_wait(b["free"], 3)
+    reduce = plane_sum(part)
+    reduce.start()
+    reduce.run()
+
+    def body(i):
+        r = at(i, CHUNK)
+        upstream = reduce.total(i)
+        hat, inverse = normalize(x_ref[r].astype(F32), EPSILON)
+        scaled = upstream * hat
+        b["pieces"][0] += scaled[0:8] + scaled[8:16]
+        b["pieces"][1] += upstream[0:8] + upstream[8:16]
+        b["back"][r] += normalize_back(upstream * gain[0:1, :], hat, inverse)
+
+    loop(rows // CHUNK, body)
+    reduce.finish()
+    delta_copy = pltpu.make_async_copy(b["back"], delta_out, b["ol"].at[2])
+    delta_copy.start()
+    combine(QK)
+
+    for i in range(1, 8):
+        gain_copy(i).wait_send()
+    gsend, gparts, gsum = b["gsend"], b["gparts"], b["gsum"]
+    for i in range(8):
+        for n in range(4):
+            lanes = slice(i * 256, i * 256 + 256)
+            gsend[i, n : n + 1, :] = jnp.sum(b["pieces"][n, :, lanes], axis=0, keepdims=True)
+            gsend[i, n + 4 : n + 5, :] = jnp.zeros((1, 256), F32)
+
+    def share_copy(i):
+        target = lax.rem(dp + i, 8)
+        return remote(
+            gsend.at[target], gparts.at[dp], b["gg_s"].at[i], b["gg_r"].at[dp], (target, tensor)
+        )
+
+    for i in range(1, 8):
+        share_copy(i).start()
+    acc = gsend[dp]
+    for i in range(1, 8):
+        gain_arrival(i).wait_recv()
+        acc = acc + gparts[lax.rem(dp + i, 8)]
+    gsum[tensor] = acc
+
+    def sum_copy(i, source):
+        target = lax.rem(tensor + i, 4)
+        return remote(
+            gsum.at[source], gsum.at[source], b["gt_s"].at[i], b["gt_r"].at[source], (dp, target)
+        )
+
+    for i in range(1, 4):
+        sum_copy(i, tensor).start()
+    for i in range(1, 4):
+        sum_copy(i, lax.rem(tensor + i, 4)).wait_recv()
+    for i in range(1, 4):
+        sum_copy(i, tensor).wait_send()
+    for i in range(1, 8):
+        share_copy(i).wait_send()
+    gains_out[...] = (gsum[0] + gsum[1]) + (gsum[2] + gsum[3])
+
+    finish_gradient(UP)
+    finish_gradient(OUTPUT)
+    finish_gradient(SWISH)
+    finish_gradient(VALUE)
+    finish_gradient(QK)
+    final_copy.wait()
+    delta_copy.wait()
+    weights_sent()
+    gradients_done()
+
+
+def whole_layer(
+    incoming_signals,
+    loss_sensitivity,
+    token_counts_per_slot,
+    leading_norm_multiplier,
+    leading_norm_offset,
+    question_projection,
+    lookup_projection,
+    content_projection,
+    silu_switch_projection,
+    retention_result_projection,
+    trailing_norm_multiplier,
+    trailing_norm_offset,
+    feedforward_switch_projection,
+    expanding_projection,
+    contracting_projection,
+):
+    rows, hidden = incoming_signals.shape
+    slots_here = token_counts_per_slot.shape[0]
+    dp_rank, tensor_rank = lax.axis_index("dp"), lax.axis_index("tensor")
+    row_ids = tensor_rank * rows + jnp.arange(rows, dtype=jnp.int32)
+    slot_match = (row_ids // SEQ_LEN)[:, None] == jnp.arange(slots_here, dtype=jnp.int32)[None, :]
+    row_lengths = jnp.sum(jnp.where(slot_match, token_counts_per_slot[None, :], 0), axis=1)
+    valid_rows = (row_ids % SEQ_LEN < row_lengths)[:, None]
+    gains = jnp.stack(
+        [leading_norm_multiplier, leading_norm_offset, trailing_norm_multiplier, trailing_norm_offset]
+    ).astype(F32)
+    gains = jnp.concatenate([gains, gains], axis=0)
+    places = np.arange(SEQ_LEN, dtype=np.float32)
+    spectrum = np.float32(10000.0) ** (-np.arange(KEY_DIM // 2, dtype=np.float32) / np.float32(KEY_DIM // 2))
+    angles = places[:, None] * spectrum[None, :]
+    head = tensor_rank * 2 + lax.rem(dp_rank, 2)
+    rate = jnp.log(1.0 - jnp.exp2(-5.0 - head.astype(F32)))
+    weights = (
+        question_projection,
+        lookup_projection,
+        content_projection,
+        silu_switch_projection,
+        retention_result_projection,
+        feedforward_switch_projection,
+        expanding_projection,
+        contracting_projection,
+    )
+    args = (
+        incoming_signals,
+        jnp.where(valid_rows, loss_sensitivity, 0),
+        gains,
+        jnp.asarray(np.cos(angles)),
+        jnp.asarray(np.sin(angles)),
+        jnp.full((8, 128), rate, F32),
+        *weights,
+    )
+    scratch = mega_scratch(rows, hidden)
+    shape = jax.ShapeDtypeStruct
+    outs = (
+        shape((rows, hidden), F32),
+        shape((rows, hidden), F32),
+        shape((8, 256), F32),
+        *(shape(weight.shape, BF16) for weight in weights),
+        shape((7, PLANES, WIDE, WIDE), BF16),
+        shape((7, PLANES, WIDE, WIDE), BF16),
+        shape((7, WIDE, WIDE), BF16),
+    )
+    results = pl.pallas_call(
+        functools.partial(mega_kernel, tuple(scratch), len(args), len(outs)),
+        out_shape=outs,
+        in_specs=[VM] * 6 + [ANY] * 8,
+        out_specs=tuple([ANY, ANY, VM] + [ANY] * 11),
+        scratch_shapes=list(scratch.values()),
+        compiler_params=pltpu.CompilerParams(
+            collective_id=0, has_side_effects=True, vmem_limit_bytes=67043328
+        ),
+        name="whole_layer",
+    )(*args)
+    final_rows, delta, gain_sums = results[:3]
+    grads = [grad.astype(F32) for grad in results[3:11]]
+    layer_output = jnp.where(valid_rows, final_rows, 0.0).astype(BF16)
+    query, key, value, swish, output, gate, up, down = grads
+    return (
+        layer_output,
+        delta,
+        gain_sums[0],
+        gain_sums[1],
+        query,
+        key,
+        value,
+        swish,
+        output,
+        gain_sums[2],
+        gain_sums[3],
+        gate,
+        up,
+        down,
+    )
+
+
 def solution(mesh):
     ranks = mesh.shape["dp"]
     groups = [[2 * k + side for k in range(ranks // 2)] for side in range(2)]
     swap = [(rank, rank + 1 - 2 * (rank % 2)) for rank in range(ranks)]
     rows, gain, column, row = P(("dp", "tensor"), None), P("dp"), P("dp", "tensor"), P("tensor", "dp")
     weights = (gain, gain, column, column, column, column, row, gain, gain, column, column, row)
+    one_kernel = ranks == 8 and mesh.shape["tensor"] == 4
     return jax.shard_map(
-        functools.partial(per_device, groups, swap),
+        whole_layer if one_kernel else functools.partial(per_device, groups, swap),
         mesh=mesh,
         in_specs=(rows, rows, P("dp"), *weights),
         out_specs=(rows, rows, *weights),

time: 704 us -> 570 us (0.81)
  Pallas kernels: 175 us -> 537 us
  waiting for transfers between devices: 231 us -> 0 us
  matrix products: 122 us -> 0 us
  blocking collectives: 68.6 us -> 0 us
  local copies, waits for them, and re-layouts: 31.1 us -> 6.98 us
  starting transfers between devices: 21.4 us -> 0 us
  between operations: 15.9 us -> 1.41 us
  other arithmetic: 31.8 us -> 21 us
    pallas_call x4 -> x1, Pallas kernels: 175 us -> 537 us  [whole_layer(): pl.pallas_call(functools.partial(mega_kernel, tuple(scratch), len(args),...]
    dot_general x27 -> x0, matrix products: 122 us -> none  [the longest x21 117 us: matmul(): return jnp.dot(left, right, preferred_element_type=jnp.float32)]
    all_gather x7 -> x0, waiting for transfers between devices: 118 us -> none  [spread(): lax.all_gather(block, 'dp', axis=axis, tiled=True, axis_index_groups=groups)]
    reduce_scatter x7 -> x0, waiting for transfers between devices: 74.1 us -> none  [collect(): lax.psum_scatter(gradient, 'dp', scatter_dimension=axis, tiled=True, axis...]
    psum x1 -> x0, blocking collectives: 43.3 us -> none  [per_device(): gain_sums = lax.psum(gain_pieces, ('dp', 'tensor'))]
    ppermute x16 -> x0, waiting for transfers between devices: 39 us -> none  [the longest x8 33.6 us: exchange(): take = lax.ppermute(give, 'dp', swap)]
    all_gather x1 -> x0, blocking collectives: 25.2 us -> none  [per_device(): gains = lax.all_gather(gains, 'dp', axis=1, tiled=True).astype(F32)]
    ppermute x16 -> x0, starting transfers between devices: 20.3 us -> none  [the longest x8 10.2 us: exchange(): take = lax.ppermute(give, 'dp', swap)]
  transfers between devices with their start and end apart: 30 -> 0, of which waited for: 15 -> 0; matrix products, arithmetic and copies ran while one was open for 22% -> 0% of each run, Pallas kernels for 25% -> 0%
where the time goes in v2:
time: 570 us; the launch traced here: 567 us
  Pallas kernels  537 us (94%)
  other arithmetic  21 us (4%)
  local copies, waits for them, and re-layouts  6.98 us (1%)
    pallas_call x1, Pallas kernels, whole_layer(): pl.pallas_call(functools.partial(mega_kernel, tuple(scratch), len(args),...  537 us
    convert_element_type x8, other arithmetic, whole_layer(): grads = [grad.astype(F32) for grad in results[3:11]]  16.3 us

profile of v2, /device:TPU:8, one launch (start us, length us, event | category | flops | bytes accessed | tf_op | source)
XLA Modules:
  0.0 566.7 jit_solution(10303563136441549895)
XLA Ops:
  1.4 0.0 copy-start
  1.4 0.7 stack.13
  2.1 0.7 stack.14
  2.7 0.7 stack.15
  3.4 0.7 stack.16
  4.1 0.6 broadcast_in_dim.44.refs_5_
  4.7 0.6 concatenate.7.refs_2_
  5.3 0.0 copy-done
  5.3 1.9 broadcast_select_fusion.refs_1_
  7.2 537.3 %whole_layer.1 = (f32[128,2048]{1,0:T(8,128)}, f32[128,2048]{1,0:T(8,128)}, f32[8,256]{1,0:T(8,128)}, bf16[256,512]{1,0:T(8,128)(2,1)}, bf16[256,512]{1,0:T(8,12...) custom-call(bf16[128,2048]{1,0:T(8,128)(2,1)} %refs_0_.1, ...), custom_call_target="tpu_custom_call" | custom-call | tf_op jit(solution)/shard_map/whole_layer/pallas_call | solution.py:1545
  544.5 2.1 select_convert_fusion
  546.7 1.4 fusion.1
  548.1 1.8 convert_element_type.35
  549.9 1.8 convert_element_type.36
  551.7 2.1 convert_element_type.37
  553.8 2.1 convert_element_type.38
  556.0 2.1 convert_element_type.39
  558.1 2.1 convert_element_type.40
  560.2 2.1 convert_element_type.41
  562.3 2.1 convert_element_type.42
  564.4 2.3 copy.33
  (2 shorter events, 0.0 us)
Async XLA Ops:
  1.4 3.9 copy-start

commit v3 on v2

--- a/solution.py
+++ b/solution.py
@@ -606,6 +606,8 @@
 PLANES = 4
 QK, VALUE, SWISH, OUTPUT, GATE, UP, DOWN = range(7)
 WIDE = 512
+QUERY, KEY = 7, 8
+GRADIENTS = (DOWN, GATE, UP, OUTPUT, SWISH, VALUE, QUERY, KEY)
 TILE = 256
 
 
@@ -663,14 +665,17 @@
         gain=pltpu.VMEM((8, hidden), F32),
         gsend=pltpu.VMEM((8, 8, 256), F32),
         gsum=pltpu.VMEM((4, 8, 256), F32),
+        xr=pltpu.VMEM((rows, hidden), BF16),
+        cr=pltpu.VMEM((rows, hidden), BF16),
+        gown=pltpu.VMEM((8, 256), F32),
         ex_s=dma((8,)),
         ex_r=dma((8,)),
         ex_l=dma((8,)),
-        zs=dma((7, 5)),
-        zr=dma((7, 4)),
-        rs=dma((7, 4)),
-        rr=dma((7, 4)),
-        ra=dma((7,)),
+        zs=dma((7, 2, 4)),
+        zr=dma((7, 2, 4)),
+        rs=dma((8, 3)),
+        rr=dma((8, 4)),
+        ra=dma((8, 2)),
         stl=dma((4,)),
         fl=dma((4,)),
         fe_s=dma((8,)),
@@ -685,7 +690,7 @@
         gc_r=dma((13,)),
         re_s=dma((10,)),
         re_r=dma((10,)),
-        ol=dma((4,)),
+        ol=dma((6,)),
         free=pltpu.SemaphoreType.REGULAR,
     )
 
@@ -761,20 +766,22 @@
 
 
 def mega_kernel(names, count_in, count_out, *refs):
-    x_ref, cot_ref, gains_ref, cos_ref, sin_ref, rate_ref = refs[:6]
-    q_w, k_w, v_w, s_w, o_w, g_w, u_w, d_w = refs[6:count_in]
+    x_hbm, cot_hbm, counts_ref, cos_ref, sin_ref = refs[:5]
+    gain_refs = refs[5:9]
+    q_w, k_w, v_w, s_w, o_w, g_w, u_w, d_w = refs[9:count_in]
     outs = refs[count_in : count_in + count_out]
     final_out, delta_out, gains_out, q_g, k_g, v_g, s_g, o_g, g_g, u_g, d_g, stage, heard, added = outs
     b = {name: ref for name, ref in zip(names, refs[count_in + count_out :], strict=True)}
     w, xs, xt, st, part, turned = b["w"], b["xs"], b["xt"], b["st"], b["part"], b["turned"]
+    x_ref, cot_ref = b["xr"], b["cr"]
     rows, hidden = x_ref.shape
     width = hidden // 8
 
     dp, tensor = lax.axis_index("dp"), lax.axis_index("tensor")
     place = Place()
     x, z = place.x, dp // 2
-    mid = (z == 1) | (z == 2)
-    end = (z == 0) | (z == 3)
+    first_plane, inner = z == 0, (z == 1) | (z == 2)
+    outer = jnp.logical_not(inner)
 
     barrier = pltpu.get_barrier_semaphore()
     for i in range(1, 8):
@@ -783,7 +790,6 @@
     for i in range(1, 4):
         other = (dp, lax.rem(tensor + i, 4))
         pl.semaphore_signal(barrier, inc=1, device_id=other, device_id_type=MESH)
-    pl.semaphore_wait(barrier, 10)
 
     def remote(source, target_ref, send, recv, target):
         return pltpu.make_async_remote_copy(
@@ -822,244 +828,249 @@
         [row_exchange(7, d_w, DOWN)],
     ]
 
+    def keep(k):
+        for local, _ in exchanges[k]:
+            local.start()
+
     def give(k):
-        for keep, send in exchanges[k]:
+        for _, send in exchanges[k]:
             send.start()
-            keep.start()
-
-    steps = (2, -2, 1, -1)
-
-    def block_copy(k, block, step, slot):
-        ref = w.at[k, at(block, 512)]
-        return remote(ref, ref, b["zs"].at[k, slot], b["zr"].at[k, block], plane(step))
-
-    def reaches(step):
-        return (z + step >= 0) & (z + step < PLANES)
+
+    towards = jnp.where(z == 1, -1, 1)
+    near, far = jnp.where(z == 1, 2, 1), jnp.where(z == 1, 3, 0)
+    own_steps = (
+        jnp.where(first_plane, 2, jnp.where(inner, 1, -2)),
+        jnp.where(first_plane, 1, -1),
+    )
+    beside = place.xn
+
+    def parts(k):
+        return (0, 1) if k == QK else (0,)
+
+    def block_copy(k, block, half, slot, target):
+        if k == QK:
+            side = x if half == 0 else 1 - x
+            ref = w.at[k, pl.ds(pl.multiple_of(block * 512 + side * 256, 256), 256)]
+        else:
+            ref = w.at[k, at(block, 512)]
+        return remote(ref, ref, b["zs"].at[k, half, slot], b["zr"].at[k, half, block], target)
+
+    def kept(k):
+        for local, _ in exchanges[k]:
+            local.wait()
+
+    def swapped(k):
+        for _, send in exchanges[k]:
+            send.wait_recv()
+
+    def spread_half(k, half):
+        for slot, step in enumerate(own_steps):
+            block_copy(k, z, half, slot, plane(step)).start()
 
     def spread(k):
-        for keep, send in exchanges[k]:
-            keep.wait()
-            send.wait_recv()
-        for slot, step in enumerate(steps):
-
-            @pl.when(reaches(step))
-            def _(slot=slot, step=step):
-                block_copy(k, z, step, slot).start()
-
-    far = jnp.where(z == 1, 3, 0)
+        kept(k)
+        swapped(k)
+        spread_half(k, 0)
 
     def pass_on(k):
-        @pl.when(z == 1)
+        @pl.when(inner)
         def _():
-            block_copy(k, 3, 1, 4).wait_recv()
-            block_copy(k, 3, -1, 4).start()
-
-        @pl.when(z == 2)
-        def _():
-            block_copy(k, 0, 1, 4).wait_recv()
-            block_copy(k, 0, 1, 4).start()
+            for half in parts(k):
+                for slot, block in ((2, near), (3, far)):
+                    copy = block_copy(k, block, half, slot, plane(towards))
+                    copy.wait_recv()
+                    copy.start()
 
     def arrive(k):
-        for block in range(PLANES):
-            skip = (z == block) | ((z == 1) & (block == 3)) | ((z == 2) & (block == 0))
-
-            @pl.when(jnp.logical_not(skip))
-            def _(block=block):
-                block_copy(k, block, 1, 4).wait_recv()
+        for half in parts(k):
+
+            @pl.when(inner)
+            def _(half=half):
+                block_copy(k, jnp.where(z == 1, 0, 3), half, 0, beside).wait_recv()
+
+            @pl.when(outer)
+            def _(half=half):
+                for i in range(3):
+                    block = jnp.where(first_plane, i + 1, i)
+                    block_copy(k, block, half, 0, beside).wait_recv()
 
     def weights_sent():
         for k in range(7):
             for _, send in exchanges[k]:
                 send.wait_send()
-            for slot, step in enumerate(steps):
-
-                @pl.when(reaches(step))
-                def _(k=k, slot=slot, step=step):
-                    block_copy(k, z, step, slot).wait_send()
-
-            @pl.when(mid)
-            def _(k=k):
-                block_copy(k, z, 1, 4).wait_send()
-
-    def direct(c, step, slot, to_added=False):
-        if to_added:
-            block = 3 - z
-            target, sem = added.at[c], b["ra"].at[c]
-        else:
-            block = z + step
-            target, sem = heard.at[c, z], b["rr"].at[c, z]
-        return remote(stage.at[c, block], target, b["rs"].at[c, slot], sem, plane(step))
+            for half in parts(k):
+                for slot in range(2):
+                    block_copy(k, z, half, slot, beside).wait_send()
+
+                @pl.when(inner)
+                def _(k=k, half=half):
+                    for slot in (2, 3):
+                        block_copy(k, z, half, slot, beside).wait_send()
+
+    def lanes_of(c):
+        if c in (QUERY, KEY):
+            return QK, pl.ds(256 * (c - QUERY), 256)
+        return c, pl.ds(0, 512)
+
+    def share(ref, c, *index):
+        chunk, lanes = lanes_of(c)
+        return ref.at[(chunk, *index, slice(None), lanes)]
+
+    def slot_of(c, slot):
+        return st.at[slot, :, pl.ds(0, 256 if c in (QUERY, KEY) else 512)]
+
+    def number(c):
+        return c if c < QUERY else c - QUERY + (0 if c == QUERY else 6)
 
     def staged(c, block, slot):
-        return pltpu.make_async_copy(st.at[slot], stage.at[c, block], b["stl"].at[slot])
+        return pltpu.make_async_copy(slot_of(c, slot), share(stage, c, block), b["stl"].at[slot])
+
+    def to_added(c, block, which, target):
+        n = number(c)
+        return remote(
+            share(stage, c, block),
+            share(added, c, which),
+            b["rs"].at[n, which],
+            b["ra"].at[n, which],
+            target,
+        )
+
+    def to_heard(c, block, slot, target):
+        n = number(c)
+        return remote(
+            share(stage, c, block), share(heard, c, z), b["rs"].at[n, slot], b["rr"].at[n, z], target
+        )
 
     def send_gradient(c):
         for block in range(PLANES):
             staged(c, block, block).wait()
-        for here, step in ((0, 1), (3, -1)):
-
-            @pl.when(z == here)
-            def _(step=step):
-                direct(c, step, 0, True).start()
-                direct(c, 2 * step, 1).start()
-                direct(c, step, 2).start()
-
-        @pl.when(mid)
+        step = jnp.where(first_plane, 1, -1)
+
+        @pl.when(outer)
         def _():
-            direct(c, 1, 1).start()
-            direct(c, -1, 2).start()
-
-    def rounds(count, body):
+            to_added(c, 3 - z, 0, plane(step)).start()
+            to_added(c, z + 2 * step, 1, plane(step)).start()
+            to_heard(c, z + step, 2, plane(step)).start()
+
+        @pl.when(inner)
+        def _():
+            to_heard(c, z + towards, 2, plane(towards)).start()
+
+    def rounds(c, body):
+        lanes = 256 if c in (QUERY, KEY) else 512
+
         def step(i):
-            body(pl.ds(pl.multiple_of(i * 32, 32), 32))
-
-        loop(count // 32, step)
+            body(pl.ds(pl.multiple_of(i * 32, 32), 32), pl.ds(0, lanes))
+
+        loop(WIDE // 32, step)
+
+    def local(source, target, n):
+        return pltpu.make_async_copy(source, target, b["fl"].at[n])
 
     def combine(c):
-        for here, step in ((1, 2), (2, -2)):
-
-            @pl.when(z == here)
-            def _(here=here, step=step):
-                there = here + step
+        @pl.when(inner)
+        def _():
+            blocks = (far, near)
+            mine = [local(share(stage, c, blocks[i]), slot_of(c, i), i) for i in range(2)]
+            for copy in mine:
+                copy.start()
+            theirs = [local(share(added, c, i), slot_of(c, 2 + i), 2 + i) for i in range(2)]
+            for i in range(2):
+                to_added(c, blocks[i], i, beside).wait_recv()
+                theirs[i].start()
+            for i in range(2):
+                mine[i].wait()
+                theirs[i].wait()
+
+                def body(r, lanes, i=i):
+                    st[i, r, lanes] = (
+                        st[i, r, lanes].astype(F32) + st[2 + i, r, lanes].astype(F32)
+                    ).astype(BF16)
+
+                rounds(c, body)
+                back = local(slot_of(c, i), share(stage, c, blocks[i]), i)
+                back.start()
+            for i, step in enumerate((-2 * towards, -towards)):
+                local(slot_of(c, i), share(stage, c, blocks[i]), i).wait()
+                to_heard(c, blocks[i], i, plane(step)).start()
+
+    homes = {
+        QUERY: q_g, KEY: k_g, VALUE: v_g, SWISH: s_g, OUTPUT: o_g, GATE: g_g, UP: u_g, DOWN: d_g
+    }
+
+    def home_copies(c, source):
+        home, (_, lanes) = homes[c], lanes_of(c)
+        if c in (OUTPUT, DOWN):
+            kept_half, given_half = (slice(None), at(x, 256)), (slice(None), at(1 - x, 256))
+            slot = home.at[at(x, 512)]
+        else:
+            kept_half, given_half = (at(x, 256),), (at(1 - x, 256),)
+            slot = home.at[:, at(x, home.shape[1] // 2)]
+        n = number(c)
+        return (
+            local(slot_of(c, 0).at[kept_half], slot, 3),
+            remote(source.at[given_half], slot, b["fe_s"].at[n], b["fe_r"].at[n], beside),
+        )
+
+    sources = (jnp.where(z == 1, 0, 1), jnp.where(z == 2, 3, 2))
+
+    def finish_gradient(c, last=False):
+        n = number(c)
+        own = local(share(stage, c, z), slot_of(c, 0), 0)
+        own.start()
+        loads = []
+        for i, source in enumerate(sources):
+            remote(
+                share(stage, c, 0), share(heard, c, source), b["rs"].at[n, 2], b["rr"].at[n, source], beside
+            ).wait_recv()
+            loads.append(local(share(heard, c, source), slot_of(c, 1 + i), 1 + i))
+            loads[-1].start()
+        own.wait()
+        for load in loads:
+            load.wait()
+
+        def body(r, lanes):
+            st[0, r, lanes] = (
+                st[0, r, lanes].astype(F32)
+                + (st[1, r, lanes].astype(F32) + st[2, r, lanes].astype(F32))
+            ).astype(BF16)
+
+        rounds(c, body)
+        source = slot_of(c, 0) if last else share(stage, c, z)
+        stay, send = home_copies(c, source)
+        if not last:
+            store = local(slot_of(c, 0), share(stage, c, z), 0)
+            store.start()
+            stay.start()
+            store.wait()
+            send.start()
+            stay.wait()
+        else:
+            send.start()
+            stay.start()
+            stay.wait()
+
+    def gradients_done():
+        for c in GRADIENTS:
+            n = number(c)
+            source = slot_of(c, 0) if c == KEY else share(stage, c, z)
+            _, send = home_copies(c, source)
+            send.wait()
+            for slot in range(3):
                 remote(
-                    stage.at[c, 0], added.at[c], b["rs"].at[c, 0], b["ra"].at[c], plane(step)
-                ).wait_recv()
-                one = pltpu.make_async_copy(added.at[c], st.at[0], b["fl"].at[0])
-                two = pltpu.make_async_copy(stage.at[c, there], st.at[1], b["fl"].at[1])
-                one.start()
-                two.start()
-                one.wait()
-                two.wait()
-
-                def body(r):
-                    st[2, r] = (st[0, r].astype(F32) + st[1, r].astype(F32)).astype(BF16)
-
-                rounds(WIDE, body)
-                three = pltpu.make_async_copy(st.at[2], stage.at[c, there], b["fl"].at[2])
-                three.start()
-                three.wait()
-                direct(c, step, 0).start()
-
-    col_homes = {VALUE: v_g, SWISH: s_g, GATE: g_g, UP: u_g}
-    row_homes = {OUTPUT: o_g, DOWN: d_g}
-
-    def homes(c):
-        if c == QK:
-            return [
-                ((at(x, 256), pl.ds(0, 256)), (at(1 - x, 256), pl.ds(0, 256)), q_g, 0),
-                ((at(x, 256), pl.ds(256, 256)), (at(1 - x, 256), pl.ds(256, 256)), k_g, 7),
-            ]
-        if c in col_homes:
-            every = pl.ds(0, 512)
-            return [((at(x, 256), every), (at(1 - x, 256), every), col_homes[c], c)]
-        every = pl.ds(0, 512)
-        return [((every, at(x, 256)), (every, at(1 - x, 256)), row_homes[c], c)]
-
-    def home_slot(c, home):
-        if c in row_homes:
-            return home.at[at(x, 512)]
-        half = home.shape[1] // 2
-        return home.at[:, at(x, half)]
-
-    def home_copies(c):
-        for kept, given, home, n in homes(c):
-            slot = home_slot(c, home)
-            yield (
-                pltpu.make_async_copy(st.at[0].at[kept], slot, b["fl"].at[1 if n == 7 else 0]),
-                remote(
-                    stage.at[c, z].at[given],
-                    slot,
-                    b["fe_s"].at[n],
-                    b["fe_r"].at[n],
-                    place.xn,
-                ),
-            )
-
-    def finish_gradient(c):
-        own = pltpu.make_async_copy(stage.at[c, z], st.at[0], b["fl"].at[0])
-        own.start()
-        for src in range(PLANES):
-            here = (jnp.abs(z - src) <= 2) & (z != src)
-
-            @pl.when(here)
-            def _(src=src):
-                remote(
-                    stage.at[c, 0], heard.at[c, src], b["rs"].at[c, 3], b["rr"].at[c, src], plane(1)
-                ).wait_recv()
-
-        def load(src, slot):
-            return pltpu.make_async_copy(heard.at[c, src], st.at[slot], b["fl"].at[slot])
-
-        sources = {0: (1, 2), 1: (0, 2, 3), 2: (0, 1, 3), 3: (1, 2)}
-        for here, srcs in sources.items():
-
-            @pl.when(z == here)
-            def _(srcs=srcs):
-                for slot, src in enumerate(srcs):
-                    load(src, slot + 1).start()
-                for slot, src in enumerate(srcs):
-                    load(src, slot + 1).wait()
-
-        own.wait()
-
-        @pl.when(end)
-        def _():
-            def body(r):
-                st[0, r] = (st[0, r].astype(F32) + (st[1, r].astype(F32) + st[2, r].astype(F32))).astype(BF16)
-
-            rounds(WIDE, body)
-
-        @pl.when(mid)
-        def _():
-            def body(r):
-                st[0, r] = (
-                    (st[0, r].astype(F32) + st[1, r].astype(F32))
-                    + (st[2, r].astype(F32) + st[3, r].astype(F32))
-                ).astype(BF16)
-
-            rounds(WIDE, body)
-
-        store = pltpu.make_async_copy(st.at[0], stage.at[c, z], b["fl"].at[2])
-        store.start()
-        copies = list(home_copies(c))
-        for keep, _ in copies:
-            keep.start()
-        store.wait()
-        for _, send in copies:
-            send.start()
-        for keep, _ in copies:
-            keep.wait()
-
-    def gradients_done():
-        for c in range(7):
-            for _, send in home_copies(c):
-                send.wait()
-            for here, step in ((0, 1), (3, -1)):
-
-                @pl.when(z == here)
-                def _(c=c, step=step):
-                    direct(c, step, 0, True).wait_send()
-                    direct(c, 2 * step, 1).wait_send()
-                    direct(c, step, 2).wait_send()
-
-            for here, step in ((1, 2), (2, -2)):
-
-                @pl.when(z == here)
-                def _(c=c, step=step):
-                    direct(c, step, 0).wait_send()
-                    direct(c, 1, 1).wait_send()
-                    direct(c, -1, 2).wait_send()
+                    share(stage, c, 0), share(heard, c, 0), b["rs"].at[n, slot], b["rr"].at[n, 0], beside
+                ).wait_send()
 
     def gain_copy(i):
         target = lax.rem(dp + i, 8)
         return remote(
-            gains_ref, b["gparts"].at[dp], b["gg_s"].at[i], b["gg_r"].at[dp], (target, tensor)
+            b["gown"], b["gparts"].at[dp], b["gg_s"].at[i], b["gg_r"].at[dp], (target, tensor)
         )
 
     def gain_arrival(i):
         source = lax.rem(dp + i, 8)
         return remote(
-            gains_ref, b["gparts"].at[source], b["gg_s"].at[i], b["gg_r"].at[source], (source, tensor)
+            b["gown"], b["gparts"].at[source], b["gg_s"].at[i], b["gg_r"].at[source], (source, tensor)
         )
 
     gather_sems = (b["ga_s"], b["ga_r"])
@@ -1067,13 +1078,26 @@
     def plane_sum(ref):
         return PlaneSum(place, ref, b["theirs"], b["got"], b["across"], b["re_s"], b["re_r"])
 
-    give(QK)
+    for k in range(7):
+        keep(k)
+    gown = b["gown"]
+    for n in range(8):
+        gown[n : n + 1, :] = gain_refs[n % 4][...].astype(F32).reshape(1, 256)
+    load_x = pltpu.make_async_copy(x_hbm, x_ref, b["ol"].at[3])
+    load_cot = pltpu.make_async_copy(cot_hbm, cot_ref, b["ol"].at[4])
+    load_x.start()
+    load_cot.start()
+    mine = pltpu.make_async_copy(gown, b["gparts"].at[dp], b["ol"].at[0])
+    mine.start()
+    kept(QK)
+    pl.semaphore_wait(barrier, 10)
     for i in range(1, 8):
         gain_copy(i).start()
+    give(QK)
+    spread_half(QK, 0)
     give(VALUE)
-    mine = pltpu.make_async_copy(gains_ref, b["gparts"].at[dp], b["ol"].at[0])
-    mine.start()
-    rate = rate_ref[0:1, 0:1]
+    head = (tensor * 2 + x).astype(F32)
+    rate = jnp.log(1.0 - jnp.exp2(-5.0 - jnp.full((8, SEQ_LEN), head, F32)))[0:1]
 
     def body(i):
         r = at(i, 64)
@@ -1083,7 +1107,9 @@
         b["decay"][r] = jnp.where(gap >= 0, jnp.exp(jnp.maximum(gap, 0).astype(F32) * rate), 0.0)
 
     loop(SEQ_LEN // 64, body)
-    spread(QK)
+    load_x.wait()
+    swapped(QK)
+    spread_half(QK, 1)
     mine.wait()
     for i in range(1, 8):
         gain_arrival(i).wait_recv()
@@ -1101,20 +1127,29 @@
     first = Gather(place, low, xs, *gather_sems)
     first.start()
     spread(VALUE)
+    load_cot.wait()
+    count = counts_ref[0]
+
+    def body(i):
+        r = at(i, CHUNK)
+        row = lax.broadcasted_iota(jnp.int32, (CHUNK, hidden), 0) + (tensor * rows + i * CHUNK)
+        cot_ref[r] = jnp.where(row < count, cot_ref[r].astype(F32), 0.0).astype(BF16)
+
+    loop(rows // CHUNK, body)
     first.forward()
     for k in range(SWISH, DOWN + 1):
         give(k)
     cotangent = Gather(place, cot_ref, b["outs"], b["gc_s"], b["gc_r"])
     cotangent.start()
-    first.finish()
-
-    def body(i):
-        xt[at(i, 256), :] = xs[:, at(i, 256)].T
-
-    loop(hidden // 256, body)
-
     pass_on(QK)
     spread(SWISH)
+    first.finish()
+
+    def body(i):
+        xt[at(i, 256), :] = xs[:, at(i, 256)].T
+
+    loop(hidden // 256, body)
+
     arrive(QK)
 
     def turn(acc, tile, scale):
@@ -1178,6 +1213,7 @@
 
     pass_on(OUTPUT)
     spread(UP)
+    pl.when(outer)(lambda: spread(DOWN))
     arrive(OUTPUT)
 
     def grid_of(i):
@@ -1191,6 +1227,7 @@
     reduce = plane_sum(part)
     reduce.start()
     reduce.run()
+    pass_on(GATE)
 
     def body(i):
         r = at(i, CHUNK)
@@ -1202,12 +1239,12 @@
     loop(rows // CHUNK, body)
     second = Gather(place, low, xs, *gather_sems)
     second.start()
-    pass_on(GATE)
-    spread(DOWN)
     second.forward()
     second.finish()
     reduce.finish()
 
+    pass_on(UP)
+    pl.when(inner)(lambda: spread(DOWN))
     arrive(GATE)
 
     def body(i):
@@ -1215,7 +1252,6 @@
         b["gate"][r] = matmul(xs[r], w[GATE])
 
     loop(tiles, body)
-    pass_on(UP)
     arrive(UP)
 
     def gelu_of(t):
@@ -1242,6 +1278,7 @@
         st[i] = value.astype(BF16)
         staged(c, i, i).start()
 
+    pass_on(DOWN)
     turned_of(b["hid"])
 
     def body(i):
@@ -1249,7 +1286,6 @@
 
     loop(PLANES, body)
     send_gradient(DOWN)
-    pass_on(DOWN)
     arrive(DOWN)
 
     def times_turned(left, r, k):
@@ -1270,14 +1306,6 @@
 
     loop(tiles, body)
 
-    def body(i):
-        r, c = grid_of(i)
-        part[r, c] = (nt(b["gb"][r], w[GATE, c]) + nt(b["ub"][r], w[UP, c])).astype(BF16)
-
-    loop(tiles * PLANES, body)
-    reduce = plane_sum(part)
-    reduce.start()
-
     def weight_gradient(c, right):
         def body(i):
             def body_turn(j):
@@ -1290,6 +1318,15 @@
         send_gradient(c)
 
     weight_gradient(GATE, b["gb"])
+
+    def body(i):
+        r, c = grid_of(i)
+        part[r, c] = (nt(b["gb"][r], w[GATE, c]) + nt(b["ub"][r], w[UP, c])).astype(BF16)
+
+    loop(tiles * PLANES, body)
+    reduce = plane_sum(part)
+    reduce.start()
+    weight_gradient(UP, b["ub"])
     reduce.run()
     b["pieces"][...] = jnp.zeros_like(b["pieces"])
 
@@ -1307,9 +1344,7 @@
     loop(rows // CHUNK, body)
     third = Gather(place, low, b["outs"], *gather_sems)
     third.start()
-    weight_gradient(UP, b["ub"])
     third.forward()
-    combine(DOWN)
 
     def body(i):
         r, c = grid_of(i)
@@ -1326,7 +1361,6 @@
 
     loop(PLANES, body)
     send_gradient(OUTPUT)
-    combine(GATE)
     swb, rb, vlow = b["gb"], b["hid"], b["ub"]
 
     def body(i):
@@ -1339,14 +1373,17 @@
 
     loop(tiles, body)
 
-    def projection_gradient(c, right):
+    def projection_gradient(c, right, lanes=slice(None)):
         def body(i):
-            stage_block(c, i, matmul(xt[at(i, 512)], right[...]))
+            value = matmul(xt[at(i, 512)], right[:, lanes]).astype(BF16)
+            st[i, :, 0 : value.shape[1]] = value
+            staged(c, i, i).start()
 
         loop(PLANES, body)
         send_gradient(c)
 
     projection_gradient(SWISH, swb)
+    combine(DOWN)
 
     def body(i):
         r = at(i, TILE)
@@ -1363,7 +1400,6 @@
 
     loop(tiles, body)
     projection_gradient(VALUE, vlow)
-    combine(UP)
     turned_of(b["sb"])
 
     def turn_back(acc, tile, scale):
@@ -1381,8 +1417,9 @@
         qkb[r, 256:384], qkb[r, 384:512] = turn_back(key, i, KEY_DIM ** (-0.5))
 
     loop(tiles, body)
-    projection_gradient(QK, b["qkb"])
-    combine(OUTPUT)
+    projection_gradient(QUERY, b["qkb"], slice(0, 256))
+    projection_gradient(KEY, b["qkb"], slice(256, 512))
+    combine(GATE)
 
     def body(i):
         r, c = grid_of(i)
@@ -1391,9 +1428,6 @@
         ).astype(BF16)
 
     loop(tiles * PLANES, body)
-    finish_gradient(DOWN)
-    combine(SWISH)
-
     reduce = plane_sum(xs)
     reduce.start()
     reduce.run()
@@ -1407,8 +1441,8 @@
         pl.semaphore_signal(b["free"], inc=1, device_id=partner, device_id_type=MESH)
     final_copy = pltpu.make_async_copy(b["middle"], final_out, b["ol"].at[1])
     final_copy.start()
-    finish_gradient(GATE)
-    combine(VALUE)
+    combine(UP)
+    finish_gradient(DOWN)
     pl.semaphore_wait(b["free"], 3)
     reduce = plane_sum(part)
     reduce.start()
@@ -1427,7 +1461,8 @@
     reduce.finish()
     delta_copy = pltpu.make_async_copy(b["back"], delta_out, b["ol"].at[2])
     delta_copy.start()
-    combine(QK)
+    combine(OUTPUT)
+    finish_gradient(GATE)
 
     for i in range(1, 8):
         gain_copy(i).wait_send()
@@ -1446,6 +1481,15 @@
 
     for i in range(1, 8):
         share_copy(i).start()
+    combine(SWISH)
+    finish_gradient(UP)
+    combine(VALUE)
+    finish_gradient(OUTPUT)
+    combine(QUERY)
+    finish_gradient(SWISH)
+    combine(KEY)
+    finish_gradient(VALUE)
+    finish_gradient(QUERY)
     acc = gsend[dp]
     for i in range(1, 8):
         gain_arrival(i).wait_recv()
@@ -1460,6 +1504,7 @@
 
     for i in range(1, 4):
         sum_copy(i, tensor).start()
+    finish_gradient(KEY, last=True)
     for i in range(1, 4):
         sum_copy(i, lax.rem(tensor + i, 4)).wait_recv()
     for i in range(1, 4):
@@ -1467,12 +1512,6 @@
     for i in range(1, 8):
         share_copy(i).wait_send()
     gains_out[...] = (gsum[0] + gsum[1]) + (gsum[2] + gsum[3])
-
-    finish_gradient(UP)
-    finish_gradient(OUTPUT)
-    finish_gradient(SWISH)
-    finish_gradient(VALUE)
-    finish_gradient(QK)
     final_copy.wait()
     delta_copy.wait()
     weights_sent()
@@ -1497,21 +1536,10 @@
     contracting_projection,
 ):
     rows, hidden = incoming_signals.shape
-    slots_here = token_counts_per_slot.shape[0]
-    dp_rank, tensor_rank = lax.axis_index("dp"), lax.axis_index("tensor")
-    row_ids = tensor_rank * rows + jnp.arange(rows, dtype=jnp.int32)
-    slot_match = (row_ids // SEQ_LEN)[:, None] == jnp.arange(slots_here, dtype=jnp.int32)[None, :]
-    row_lengths = jnp.sum(jnp.where(slot_match, token_counts_per_slot[None, :], 0), axis=1)
-    valid_rows = (row_ids % SEQ_LEN < row_lengths)[:, None]
-    gains = jnp.stack(
-        [leading_norm_multiplier, leading_norm_offset, trailing_norm_multiplier, trailing_norm_offset]
-    ).astype(F32)
-    gains = jnp.concatenate([gains, gains], axis=0)
     places = np.arange(SEQ_LEN, dtype=np.float32)
-    spectrum = np.float32(10000.0) ** (-np.arange(KEY_DIM // 2, dtype=np.float32) / np.float32(KEY_DIM // 2))
+    middle = KEY_DIM // 2
+    spectrum = np.float32(10000.0) ** (-np.arange(middle, dtype=np.float32) / np.float32(middle))
     angles = places[:, None] * spectrum[None, :]
-    head = tensor_rank * 2 + lax.rem(dp_rank, 2)
-    rate = jnp.log(1.0 - jnp.exp2(-5.0 - head.astype(F32)))
     weights = (
         question_projection,
         lookup_projection,
@@ -1522,15 +1550,11 @@
         expanding_projection,
         contracting_projection,
     )
-    args = (
-        incoming_signals,
-        jnp.where(valid_rows, loss_sensitivity, 0),
-        gains,
-        jnp.asarray(np.cos(angles)),
-        jnp.asarray(np.sin(angles)),
-        jnp.full((8, 128), rate, F32),
-        *weights,
-    )
+    gains = (
+        leading_norm_multiplier, leading_norm_offset, trailing_norm_multiplier, trailing_norm_offset
+    )
+    tables = (jnp.asarray(np.cos(angles)), jnp.asarray(np.sin(angles)))
+    args = (incoming_signals, loss_sensitivity, token_counts_per_slot, *tables, *gains, *weights)
     scratch = mega_scratch(rows, hidden)
     shape = jax.ShapeDtypeStruct
     outs = (
@@ -1540,12 +1564,13 @@
         *(shape(weight.shape, BF16) for weight in weights),
         shape((7, PLANES, WIDE, WIDE), BF16),
         shape((7, PLANES, WIDE, WIDE), BF16),
-        shape((7, WIDE, WIDE), BF16),
-    )
+        shape((7, 2, WIDE, WIDE), BF16),
+    )
+    scalar = pl.BlockSpec(memory_space=pltpu.SMEM)
     results = pl.pallas_call(
         functools.partial(mega_kernel, tuple(scratch), len(args), len(outs)),
         out_shape=outs,
-        in_specs=[VM] * 6 + [ANY] * 8,
+        in_specs=[ANY, ANY, scalar] + [VM] * 6 + [ANY] * 8,
         out_specs=tuple([ANY, ANY, VM] + [ANY] * 11),
         scratch_shapes=list(scratch.values()),
         compiler_params=pltpu.CompilerParams(
@@ -1554,12 +1579,32 @@
         name="whole_layer",
     )(*args)
     final_rows, delta, gain_sums = results[:3]
-    grads = [grad.astype(F32) for grad in results[3:11]]
-    layer_output = jnp.where(valid_rows, final_rows, 0.0).astype(BF16)
-    query, key, value, swish, output, gate, up, down = grads
+    owned = results[3:11]
+    wide = pl.pallas_call(
+        widen_kernel,
+        out_shape=(
+            shape((rows, hidden), BF16),
+            shape((rows, hidden), F32),
+            *(shape(weight.shape, F32) for weight in weights),
+        ),
+        in_specs=[scalar] + [ANY] * 10,
+        out_specs=(ANY,) * 10,
+        scratch_shapes=[
+            pltpu.VMEM((rows, hidden), F32),
+            pltpu.VMEM((rows, hidden), F32),
+            pltpu.VMEM((rows, hidden), BF16),
+            *(pltpu.VMEM(weight.shape, BF16) for weight in weights),
+            *(pltpu.VMEM(weight.shape, F32) for weight in weights),
+            pltpu.SemaphoreType.DMA((10,)),
+            pltpu.SemaphoreType.DMA((10,)),
+        ],
+        compiler_params=pltpu.CompilerParams(vmem_limit_bytes=67043328),
+        name="widen",
+    )(token_counts_per_slot, final_rows, delta, *owned)
+    query, key, value, swish, output, gate, up, down = wide[2:]
     return (
-        layer_output,
-        delta,
+        wide[0],
+        wide[1],
         gain_sums[0],
         gain_sums[1],
         query,
@@ -1573,6 +1618,47 @@
         up,
         down,
     )
+
+
+def widen_kernel(counts_ref, *refs):
+    sources, targets, scratch = refs[:10], refs[10:20], refs[20:]
+    final, delta, low = scratch[:3]
+    narrow, wide, (came, went) = scratch[3:11], scratch[11:19], scratch[19:]
+    buffers = (final, delta, *narrow)
+    loads = [
+        pltpu.make_async_copy(source, buffer, came.at[i])
+        for i, (source, buffer) in enumerate(zip(sources, buffers, strict=True))
+    ]
+    stores = [
+        pltpu.make_async_copy(buffer, target, went.at[i])
+        for i, (buffer, target) in enumerate(zip((low, delta, *wide), targets, strict=True))
+    ]
+    for load in loads:
+        load.start()
+    rows, hidden = final.shape
+    tensor, count = lax.axis_index("tensor"), counts_ref[0]
+    loads[0].wait()
+
+    def body(i):
+        r = at(i, CHUNK)
+        row = lax.broadcasted_iota(jnp.int32, (CHUNK, hidden), 0) + (tensor * rows + i * CHUNK)
+        low[r] = jnp.where(row < count, final[r], 0.0).astype(BF16)
+
+    loop(rows // CHUNK, body)
+    stores[0].start()
+    loads[1].wait()
+    stores[1].start()
+    for n in range(8):
+        loads[n + 2].wait()
+
+        def body(i, n=n):
+            r = at(i, 32)
+            wide[n][r] = narrow[n][r].astype(F32)
+
+        loop(narrow[n].shape[0] // 32, body)
+        stores[n + 2].start()
+    for store in stores:
+        store.wait()
 
 
 def solution(mesh):

time: 570 us -> 480 us (0.84)
  Pallas kernels: 537 us -> 476 us
  other arithmetic: 21 us -> 0 us
    pallas_call x1, Pallas kernels: 537 us -> 471 us  [whole_layer(): pl.pallas_call(functools.partial(mega_kernel, tuple(scratch), len(args),...]
    convert_element_type x9 -> x0, other arithmetic: 18.4 us -> none  [the longest x8 16.3 us: whole_layer(): grads = [grad.astype(F32) for grad in results[3:11]]]
where the time goes in v3:
time: 480 us; the launch traced here: 479 us
  Pallas kernels  476 us (99%)
    pallas_call x1, Pallas kernels, whole_layer(): pl.pallas_call(functools.partial(mega_kernel, tuple(scratch), len(args),...  471 us

profile of v3, /device:TPU:8, one launch (start us, length us, event | category | flops | bytes accessed | tf_op | source)
XLA Modules:
  0.0 479.0 jit_solution(8193986189987089416)
XLA Ops:
  1.3 471.2 %whole_layer.1 = (f32[128,2048]{1,0:T(8,128)}, f32[128,2048]{1,0:T(8,128)}, f32[8,256]{1,0:T(8,128)}, bf16[256,512]{1,0:T(8,128)(2,1)}, bf16[256,512]{1,0:T(8,12...) custom-call(bf16[128,2048]{1,0:T(8,128)(2,1)} %refs_0_.1, ...), custom_call_target="tpu_custom_call" | custom-call | tf_op jit(solution)/shard_map/whole_layer/pallas_call | solution.py:1570
  472.5 1.4 fusion
  474.0 5.0 %widen.1 = (bf16[128,2048]{1,0:T(8,128)(2,1)}, f32[128,2048]{1,0:T(8,128)}, f32[256,512]{1,0:T(8,128)}, f32[256,512]{1,0:T(8,128)}, f32[256,1024]{1,0:T(8,128)},...) custom-call(s32[1]{0:T(128)S(6)} %copy.31.refs_2_.counts_ref, ...), custom_call_target="tpu_custom_call" | custom-call | tf_op jit(solution)/shard_map/widen/pallas_call | solution.py:1583

commit v4 on v3

--- a/solution.py
+++ b/solution.py
@@ -131,6 +131,14 @@
 
     def start(self):
         for copy in (self.xa, self.yb, self.xb, self.ya, self.s0, self.local):
+            copy.start()
+
+    def start_first_half(self):
+        self.xa.start()
+        self.ya.start()
+
+    def start_second_half(self):
+        for copy in (self.yb, self.xb, self.s0, self.local):
             copy.start()
 
     def forward(self):
@@ -607,7 +615,8 @@
 QK, VALUE, SWISH, OUTPUT, GATE, UP, DOWN = range(7)
 WIDE = 512
 QUERY, KEY = 7, 8
-GRADIENTS = (DOWN, GATE, UP, OUTPUT, SWISH, VALUE, QUERY, KEY)
+FEED_FORWARD = (DOWN, GATE, UP)
+GRADIENTS = (*FEED_FORWARD, OUTPUT, SWISH, VALUE, QUERY, KEY)
 TILE = 256
 
 
@@ -667,6 +676,13 @@
         gsum=pltpu.VMEM((4, 8, 256), F32),
         xr=pltpu.VMEM((rows, hidden), BF16),
         cr=pltpu.VMEM((rows, hidden), BF16),
+        rows2=pltpu.VMEM((rows, hidden), BF16),
+        cot2=pltpu.VMEM((rows, hidden), BF16),
+        ub2=pltpu.VMEM((total, WIDE), BF16),
+        hop_s=dma((6,)),
+        hop_r=dma((6,)),
+        gd_s=dma((13,)),
+        gd_r=dma((13,)),
         gown=pltpu.VMEM((8, 256), F32),
         ex_s=dma((8,)),
         ex_r=dma((8,)),
@@ -717,6 +733,7 @@
         def piece(j, lo):
             return part.at[pl.ds(pl.multiple_of(self.base[j] + lo, 8), h)]
 
+        self.place, self.remote = p, remote
         a, b = pl.ds(0, h), pl.ds(h, h)
         self.swap = [
             remote(j, part.at[rows_of(p.block(j, 1), rows)], theirs.at[j], p.sib) for j in range(4)
@@ -740,22 +757,51 @@
         for j in (3, 1, 2, 0):
             self.swap[j].start()
 
-    def run(self):
-        rows, h = self.rows, self.half
+    def fill(self, tile_value):
+        p, tile = self.place, 2 * self.rows
+
+        def body(i):
+            j = jnp.where(i == 0, 3, jnp.where(i == 3, 0, i))
+            chip_x = jnp.where(lax.rem(j, 2) == 1, 1 - p.x, p.x)
+            chip_y = jnp.where(j >= 2, 1 - p.y, p.y)
+            chip = chip_x * 2 + chip_y
+            r = at(chip, tile)
+
+            def inner(n):
+                c = at(n, WIDE)
+                self.part[r, c] = tile_value(r, c).astype(BF16)
+
+            loop(self.part.shape[1] // WIDE, inner)
+            source = self.part.at[rows_of(chip * 2 + 1 - p.c, self.rows)]
+            self.remote(j, source, self.theirs.at[j], p.sib).start()
+
+        loop(4, body)
+
+    def run1(self):
         for j, copies in ((3, (self.da, self.db)), (1, (self.xa,)), (2, (self.yb,))):
             self.swap[j].wait_recv()
-            self.add(j, 0, rows, self.theirs.at[j], 0)
+            self.add(j, 0, self.rows, self.theirs.at[j], 0)
             for copy in copies:
                 copy.start()
+
+    def run2(self):
+        h = self.half
         self.db.wait_recv()
         self.add(1, h, h, self.across.at[1], 0)
         self.xb.start()
         self.da.wait_recv()
         self.add(2, 0, h, self.across.at[0], 0)
         self.ya.start()
+
+    def run3(self):
         self.swap[0].wait_recv()
         for copy in (self.xa, self.yb, self.xb, self.ya):
             copy.wait_recv()
+
+    def run(self):
+        self.run1()
+        self.run2()
+        self.run3()
 
     def total(self, i):
         r = pl.ds(pl.multiple_of(i * CHUNK, CHUNK), CHUNK)
@@ -864,8 +910,15 @@
             send.wait_recv()
 
     def spread_half(k, half):
-        for slot, step in enumerate(own_steps):
-            block_copy(k, z, half, slot, plane(step)).start()
+        def both():
+            for slot, step in enumerate(own_steps):
+                block_copy(k, z, half, slot, plane(step)).start()
+
+        if k in FEED_FORWARD:
+            pl.when(outer)(both)
+            pl.when(inner)(lambda: block_copy(k, z, half, 0, plane(-towards)).start())
+        else:
+            both()
 
     def spread(k):
         kept(k)
@@ -894,18 +947,26 @@
                     block = jnp.where(first_plane, i + 1, i)
                     block_copy(k, block, half, 0, beside).wait_recv()
 
+    def arrive_inner(k):
+        for i in range(3):
+            block = jnp.where(z == 1, (0, 2, 3)[i], (0, 1, 3)[i])
+            block_copy(k, block, 0, 0, beside).wait_recv()
+
     def weights_sent():
         for k in range(7):
             for _, send in exchanges[k]:
                 send.wait_send()
             for half in parts(k):
-                for slot in range(2):
-                    block_copy(k, z, half, slot, beside).wait_send()
-
-                @pl.when(inner)
-                def _(k=k, half=half):
-                    for slot in (2, 3):
-                        block_copy(k, z, half, slot, beside).wait_send()
+                block_copy(k, z, half, 0, beside).wait_send()
+                if k in FEED_FORWARD:
+                    pl.when(outer)(lambda k=k, half=half: block_copy(k, z, half, 1, beside).wait_send())
+                else:
+                    block_copy(k, z, half, 1, beside).wait_send()
+
+                    @pl.when(inner)
+                    def _(k=k, half=half):
+                        for slot in (2, 3):
+                            block_copy(k, z, half, slot, beside).wait_send()
 
     def lanes_of(c):
         if c in (QUERY, KEY):
@@ -941,9 +1002,12 @@
             share(stage, c, block), share(heard, c, z), b["rs"].at[n, slot], b["rr"].at[n, z], target
         )
 
-    def send_gradient(c):
+    def all_staged(c):
         for block in range(PLANES):
             staged(c, block, block).wait()
+
+    def send_gradient(c):
+        all_staged(c)
         step = jnp.where(first_plane, 1, -1)
 
         @pl.when(outer)
@@ -955,6 +1019,10 @@
         @pl.when(inner)
         def _():
             to_heard(c, z + towards, 2, plane(towards)).start()
+
+    def send_inner(c):
+        to_added(c, far, 0, plane(-towards)).start()
+        to_heard(c, near, 1, plane(-towards)).start()
 
     def rounds(c, body):
         lanes = 256 if c in (QUERY, KEY) else 512
@@ -994,6 +1062,27 @@
                 local(slot_of(c, i), share(stage, c, blocks[i]), i).wait()
                 to_heard(c, blocks[i], i, plane(step)).start()
 
+    def combine_inner(c):
+        block = z + towards
+        mine = local(share(stage, c, block), slot_of(c, 0), 0)
+        theirs = local(share(added, c, 0), slot_of(c, 1), 1)
+        mine.start()
+        to_added(c, block, 0, beside).wait_recv()
+        theirs.start()
+        mine.wait()
+        theirs.wait()
+
+        def body(r, lanes):
+            st[0, r, lanes] = (
+                st[0, r, lanes].astype(F32) + st[1, r, lanes].astype(F32)
+            ).astype(BF16)
+
+        rounds(c, body)
+        back = local(slot_of(c, 0), share(stage, c, block), 0)
+        back.start()
+        back.wait()
+        to_heard(c, block, 2, plane(towards)).start()
+
     homes = {
         QUERY: q_g, KEY: k_g, VALUE: v_g, SWISH: s_g, OUTPUT: o_g, GATE: g_g, UP: u_g, DOWN: d_g
     }
@@ -1016,26 +1105,53 @@
 
     def finish_gradient(c, last=False):
         n = number(c)
-        own = local(share(stage, c, z), slot_of(c, 0), 0)
-        own.start()
-        loads = []
-        for i, source in enumerate(sources):
+
+        def own_load():
+            return local(share(stage, c, z), slot_of(c, 0), 0)
+
+        def arrival(i, source):
             remote(
                 share(stage, c, 0), share(heard, c, source), b["rs"].at[n, 2], b["rr"].at[n, source], beside
             ).wait_recv()
-            loads.append(local(share(heard, c, source), slot_of(c, 1 + i), 1 + i))
-            loads[-1].start()
-        own.wait()
-        for load in loads:
-            load.wait()
-
-        def body(r, lanes):
-            st[0, r, lanes] = (
-                st[0, r, lanes].astype(F32)
-                + (st[1, r, lanes].astype(F32) + st[2, r, lanes].astype(F32))
-            ).astype(BF16)
-
-        rounds(c, body)
+            load = local(share(heard, c, source), slot_of(c, i), i)
+            load.start()
+            return load
+
+        if c in FEED_FORWARD:
+            source = jnp.where((z == 0) | (z == 2), 1, 2)
+
+            @pl.when(outer)
+            def _():
+                arrival(0, source).wait()
+
+            @pl.when(inner)
+            def _():
+                own_load().start()
+                arrival(1, source).wait()
+                own_load().wait()
+
+                def body(r, lanes):
+                    st[0, r, lanes] = (
+                        st[0, r, lanes].astype(F32) + st[1, r, lanes].astype(F32)
+                    ).astype(BF16)
+
+                rounds(c, body)
+
+        else:
+            own_load().start()
+            loads = [arrival(1 + i, source) for i, source in enumerate(sources)]
+            own_load().wait()
+            for load in loads:
+                load.wait()
+
+            def body(r, lanes):
+                st[0, r, lanes] = (
+                    st[0, r, lanes].astype(F32)
+                    + (st[1, r, lanes].astype(F32) + st[2, r, lanes].astype(F32))
+                ).astype(BF16)
+
+            rounds(c, body)
+
         source = slot_of(c, 0) if last else share(stage, c, z)
         stay, send = home_copies(c, source)
         if not last:
@@ -1056,10 +1172,33 @@
             source = slot_of(c, 0) if c == KEY else share(stage, c, z)
             _, send = home_copies(c, source)
             send.wait()
-            for slot in range(3):
-                remote(
-                    share(stage, c, 0), share(heard, c, 0), b["rs"].at[n, slot], b["rr"].at[n, 0], beside
-                ).wait_send()
+
+            def sent(c=c, n=n):
+                for slot in range(3):
+                    remote(
+                        share(stage, c, 0), share(heard, c, 0), b["rs"].at[n, slot], b["rr"].at[n, 0], beside
+                    ).wait_send()
+
+            if c in FEED_FORWARD:
+                pl.when(inner)(sent)
+            else:
+                sent()
+
+    across_step = jnp.where(outer, jnp.where(first_plane, 1, -1), towards)
+
+    def hop(n, source, target, part_of=slice(None)):
+        return remote(
+            source.at[part_of], target.at[part_of], b["hop_s"].at[n], b["hop_r"].at[n], plane(across_step)
+        )
+
+    halves = (pl.ds(0, rows // 2), pl.ds(rows // 2, rows // 2))
+
+    def neighbours_may_write():
+        for partner in (place.sib, place.xn, place.yn):
+            pl.semaphore_signal(b["free"], inc=1, device_id=partner, device_id_type=MESH)
+
+    def may_write():
+        pl.semaphore_wait(b["free"], 3)
 
     def gain_copy(i):
         target = lax.rem(dp + i, 8)
@@ -1136,11 +1275,12 @@
         cot_ref[r] = jnp.where(row < count, cot_ref[r].astype(F32), 0.0).astype(BF16)
 
     loop(rows // CHUNK, body)
+    pl.when(outer)(lambda: hop(2, cot_ref, b["cot2"]).start())
     first.forward()
     for k in range(SWISH, DOWN + 1):
         give(k)
     cotangent = Gather(place, cot_ref, b["outs"], b["gc_s"], b["gc_r"])
-    cotangent.start()
+    pl.when(inner)(cotangent.start)
     pass_on(QK)
     spread(SWISH)
     first.finish()
@@ -1149,6 +1289,7 @@
         xt[at(i, 256), :] = xs[:, at(i, 256)].T
 
     loop(hidden // 256, body)
+    spread(OUTPUT)
 
     arrive(QK)
 
@@ -1178,8 +1319,9 @@
 
     loop(tiles, body)
 
+    for k in (GATE, UP, DOWN):
+        spread(k)
     pass_on(VALUE)
-    spread(OUTPUT)
     arrive(VALUE)
 
     def body(i):
@@ -1196,11 +1338,12 @@
         b["ginv"][r] = jnp.broadcast_to(inverse, (TILE, 128))
 
     loop(tiles, body)
-    cotangent.forward()
-    cotangent.finish()
+    @pl.when(inner)
+    def _():
+        cotangent.forward()
+        cotangent.finish()
 
     pass_on(SWISH)
-    spread(GATE)
     arrive(SWISH)
 
     def body(i):
@@ -1212,23 +1355,14 @@
     loop(tiles, body)
 
     pass_on(OUTPUT)
-    spread(UP)
-    pl.when(outer)(lambda: spread(DOWN))
     arrive(OUTPUT)
 
     def grid_of(i):
         return at(i // PLANES, TILE), at(lax.rem(i, PLANES), 512)
 
-    def body(i):
-        r, c = grid_of(i)
-        part[r, c] = matmul(b["gated"][r], w[OUTPUT, c]).astype(BF16)
-
-    loop(tiles * PLANES, body)
     reduce = plane_sum(part)
-    reduce.start()
+    reduce.fill(lambda r, c: matmul(b["gated"][r], w[OUTPUT, c]))
     reduce.run()
-    pass_on(GATE)
-
     def body(i):
         r = at(i, CHUNK)
         middle = x_ref[r].astype(F32) + reduce.total(i)
@@ -1237,36 +1371,16 @@
         low[r] = (hat * gain[2:3, :] + gain[3:4, :]).astype(BF16)
 
     loop(rows // CHUNK, body)
-    second = Gather(place, low, xs, *gather_sems)
-    second.start()
-    second.forward()
-    second.finish()
-    reduce.finish()
-
-    pass_on(UP)
-    pl.when(inner)(lambda: spread(DOWN))
-    arrive(GATE)
-
-    def body(i):
-        r = at(i, TILE)
-        b["gate"][r] = matmul(xs[r], w[GATE])
-
-    loop(tiles, body)
-    arrive(UP)
+
+    @pl.when(outer)
+    def _():
+        for n in range(2):
+            hop(n, low, b["rows2"], halves[n]).start()
 
     def gelu_of(t):
-        inner = 0.7978845608028654 * (t + 0.044715 * t * t * t)
-        return 0.5 * (1.0 + jnp.tanh(inner)), jnp.tanh(inner)
-
-    def body(i):
-        r = at(i, TILE)
-        up = matmul(xs[r], w[UP])
-        b["up"][r] = up
-        gate = b["gate"][r]
-        share, _ = gelu_of(gate)
-        b["hid"][r] = (gate * share * up).astype(BF16)
-
-    loop(tiles, body)
+        inner_value = 0.7978845608028654 * (t + 0.044715 * t * t * t)
+        tanh = jnp.tanh(inner_value)
+        return 0.5 * (1.0 + tanh), tanh
 
     def turned_of(ref):
         def body(i):
@@ -1277,16 +1391,6 @@
     def stage_block(c, i, value):
         st[i] = value.astype(BF16)
         staged(c, i, i).start()
-
-    pass_on(DOWN)
-    turned_of(b["hid"])
-
-    def body(i):
-        stage_block(DOWN, i, matmul(turned[...], b["outs"][:, at(i, 512)]))
-
-    loop(PLANES, body)
-    send_gradient(DOWN)
-    arrive(DOWN)
 
     def times_turned(left, r, k):
         acc = nt(left[r, 0:512], w[k, 0:512])
@@ -1295,44 +1399,84 @@
             acc = acc + nt(left[r, lanes], w[k, lanes])
         return acc
 
-    def body(i):
-        r = at(i, TILE)
-        back = times_turned(b["outs"], r, DOWN)
-        gate, up = b["gate"][r], b["up"][r]
-        share, tanh = gelu_of(gate)
-        slope = 0.5 * gate * (1.0 - tanh * tanh) * (0.7978845608028654 * (1.0 + 0.134145 * gate * gate))
-        b["gb"][r] = (back * up * (share + slope)).astype(BF16)
-        b["ub"][r] = (back * gate * share).astype(BF16)
-
-    loop(tiles, body)
-
-    def weight_gradient(c, right):
+    def gate_projection(mixer):
+        def body(i):
+            r = at(i, TILE)
+            b["gate"][r] = matmul(mixer[r], w[GATE])
+
+        loop(tiles, body)
+
+    def up_projection(mixer, hid):
+        def body(i):
+            r = at(i, TILE)
+            up = matmul(mixer[r], w[UP])
+            b["up"][r] = up
+            gate = b["gate"][r]
+            share_of, _ = gelu_of(gate)
+            hid[r] = (gate * share_of * up).astype(BF16)
+
+        loop(tiles, body)
+
+    def hidden_backward(cots, gb, ub):
+        def body(i):
+            r = at(i, TILE)
+            back = times_turned(cots, r, DOWN)
+            gate, up = b["gate"][r], b["up"][r]
+            share_of, tanh = gelu_of(gate)
+            slope = 0.5 * gate * (1.0 - tanh * tanh) * (0.7978845608028654 * (1.0 + 0.134145 * gate * gate))
+            gb[r] = (back * up * (share_of + slope)).astype(BF16)
+            ub[r] = (back * gate * share_of).astype(BF16)
+
+        loop(tiles, body)
+
+    def refill(c):
+        copies = [pltpu.make_async_copy(stage.at[c, i], st.at[i], b["fl"].at[i]) for i in range(PLANES)]
+        for copy in copies:
+            copy.start()
+        for copy in copies:
+            copy.wait()
+
+    def product_of(c, i, value, more):
+        stage_block(c, i, value + st[i].astype(F32) if more else value)
+
+    def down_gradient(hid, cots, more):
+        if more:
+            refill(DOWN)
+        turned_of(hid)
+
+        def body(i):
+            product_of(DOWN, i, matmul(turned[...], cots[:, at(i, 512)]), more)
+
+        loop(PLANES, body)
+        all_staged(DOWN)
+
+    def weight_gradient(c, mixer, right, more):
+        if more:
+            refill(c)
+
         def body(i):
             def body_turn(j):
-                turned[:, at(j, TILE)] = xs[at(j, TILE), at(i, 512)].T
+                turned[:, at(j, TILE)] = mixer[at(j, TILE), at(i, 512)].T
 
             loop(tiles, body_turn)
-            stage_block(c, i, matmul(turned[...], right[...]))
+            product_of(c, i, matmul(turned[...], right[...]), more)
 
         loop(PLANES, body)
-        send_gradient(c)
-
-    weight_gradient(GATE, b["gb"])
-
-    def body(i):
-        r, c = grid_of(i)
-        part[r, c] = (nt(b["gb"][r], w[GATE, c]) + nt(b["ub"][r], w[UP, c])).astype(BF16)
-
-    loop(tiles * PLANES, body)
-    reduce = plane_sum(part)
-    reduce.start()
-    weight_gradient(UP, b["ub"])
-    reduce.run()
+        all_staged(c)
+
+    def mixer_input(gb, ub):
+        return lambda r, c: nt(gb[r], w[GATE, c]) + nt(ub[r], w[UP, c])
+
+    def mixer_output(hid, target):
+        def body(i):
+            r, c = grid_of(i)
+            target[r, c] = matmul(hid[r], w[DOWN, c]).astype(BF16)
+
+        loop(tiles * PLANES, body)
+
     b["pieces"][...] = jnp.zeros_like(b["pieces"])
 
-    def body(i):
-        r = at(i, CHUNK)
-        upstream = reduce.total(i)
+    def second_norm_backward(r, upstream):
         hat, inverse = normalize(b["middle"][r], EPSILON)
         scaled = upstream * hat
         b["pieces"][2] += scaled[0:8] + scaled[8:16]
@@ -1341,18 +1485,110 @@
         b["back"][r] = back
         low[r] = back.astype(BF16)
 
-    loop(rows // CHUNK, body)
-    third = Gather(place, low, b["outs"], *gather_sems)
-    third.start()
+    hid2, gb2, ub2 = b["sb"], b["qkb"], b["ub2"]
+    outs_ref = b["outs"]
+
+    @pl.when(inner)
+    def _():
+        second = Gather(place, low, xs, *gather_sems)
+        second.start()
+        hop(2, cot_ref, b["cot2"]).wait_recv()
+        second.forward()
+        other_cot = Gather(place, b["cot2"], part, b["gc_s"], b["gc_r"])
+        reduce.finish()
+        neighbours_may_write()
+        may_write()
+        other_cot.start()
+        second.finish()
+        arrive_inner(GATE)
+        gate_projection(xs)
+        arrive_inner(UP)
+        up_projection(xs, b["hid"])
+        other_cot.forward()
+        arrive_inner(DOWN)
+        hidden_backward(outs_ref, b["gb"], b["ub"])
+        down_gradient(b["hid"], outs_ref, False)
+        neighbours_may_write()
+        other_cot.finish()
+        other = Gather(place, b["rows2"], outs_ref, b["gd_s"], b["gd_r"])
+        may_write()
+        hop(0, low, b["rows2"], halves[0]).wait_recv()
+        other.start_first_half()
+        hop(1, low, b["rows2"], halves[1]).wait_recv()
+        other.start_second_half()
+        weight_gradient(GATE, xs, b["gb"], False)
+        other.forward()
+        weight_gradient(UP, xs, b["ub"], False)
+        other.finish()
+        gate_projection(outs_ref)
+        up_projection(outs_ref, hid2)
+        hidden_backward(part, gb2, ub2)
+        reduce2 = plane_sum(xs)
+        reduce2.fill(mixer_input(gb2, ub2))
+        reduce2.run1()
+        down_gradient(hid2, part, True)
+        send_inner(DOWN)
+        reduce2.run2()
+        reduce2.run3()
+
+        for n in range(2):
+
+            def body(i, n=n):
+                i = n * (rows // 2 // CHUNK) + i
+                b["rows2"][at(i, CHUNK)] = reduce2.total(i).astype(BF16)
+
+            loop(rows // 2 // CHUNK, body)
+            hop(3 + n, b["rows2"], b["rows2"], halves[n]).start()
+        reduce2.finish()
+        neighbours_may_write()
+        may_write()
+        reduce3 = plane_sum(part)
+        reduce3.fill(mixer_input(b["gb"], b["ub"]))
+        reduce3.run1()
+        weight_gradient(GATE, outs_ref, gb2, True)
+        send_inner(GATE)
+        reduce3.run2()
+        combine_inner(DOWN)
+        weight_gradient(UP, outs_ref, ub2, True)
+        send_inner(UP)
+        neighbours_may_write()
+        reduce3.run3()
+
+        def body(i):
+            second_norm_backward(at(i, CHUNK), reduce3.total(i))
+
+        loop(rows // CHUNK, body)
+        reduce3.finish()
+        may_write()
+
+    third = Gather(place, low, outs_ref, *gather_sems)
+
+    @pl.when(outer)
+    def _():
+        reduce.finish()
+        for n in range(2):
+            hop(n, low, b["rows2"], halves[n]).wait_send()
+        for n in range(2):
+            hop(3 + n, b["rows2"], b["rows2"], halves[n]).wait_recv()
+
+            def body(i, n=n):
+                r = pl.ds(pl.multiple_of(n * (rows // 2) + i * CHUNK, CHUNK), CHUNK)
+                second_norm_backward(r, b["rows2"][r].astype(F32))
+
+            loop(rows // 2 // CHUNK, body)
+            if n == 0:
+                third.start_first_half()
+            else:
+                third.start_second_half()
+
+    pl.when(inner)(third.start)
     third.forward()
-
-    def body(i):
-        r, c = grid_of(i)
-        xs[r, c] = matmul(b["hid"][r], w[DOWN, c]).astype(BF16)
-
-    loop(tiles * PLANES, body)
+    pl.when(inner)(lambda: combine_inner(GATE))
+    pl.when(inner)(lambda: mixer_output(hid2, xs))
     third.finish()
-    reduce.finish()
+    reduce5 = plane_sum(xs)
+    pl.when(inner)(reduce5.start)
+    pl.when(inner)(lambda: combine_inner(UP))
 
     turned_of(b["gated"])
 
@@ -1361,7 +1597,8 @@
 
     loop(PLANES, body)
     send_gradient(OUTPUT)
-    swb, rb, vlow = b["gb"], b["hid"], b["ub"]
+    pl.when(inner)(reduce5.run1)
+    swb, rb, vlow = b["gb"], b["ub2"], b["ub"]
 
     def body(i):
         r = at(i, TILE)
@@ -1382,9 +1619,27 @@
         loop(PLANES, body)
         send_gradient(c)
 
+    pl.when(inner)(reduce5.run2)
     projection_gradient(SWISH, swb)
-    combine(DOWN)
-
+
+    @pl.when(inner)
+    def _():
+        reduce5.run3()
+
+        def body(i):
+            b["cot2"][at(i, CHUNK)] = reduce5.total(i).astype(BF16)
+
+        loop(rows // CHUNK, body)
+        hop(5, b["cot2"], b["cot2"]).start()
+        reduce5.finish()
+        neighbours_may_write()
+        mixer_output(b["hid"], xs)
+        may_write()
+        plane_sum(xs).start()
+
+    reduce6 = plane_sum(xs)
+    combine(OUTPUT)
+    pl.when(inner)(reduce6.run1)
     def body(i):
         r = at(i, TILE)
         decay = b["decay"][at(lax.rem(i, per_slot), TILE)]
@@ -1399,6 +1654,7 @@
         ).astype(BF16)
 
     loop(tiles, body)
+    pl.when(inner)(reduce6.run2)
     projection_gradient(VALUE, vlow)
     turned_of(b["sb"])
 
@@ -1419,34 +1675,30 @@
     loop(tiles, body)
     projection_gradient(QUERY, b["qkb"], slice(0, 256))
     projection_gradient(KEY, b["qkb"], slice(256, 512))
-    combine(GATE)
-
-    def body(i):
-        r, c = grid_of(i)
-        part[r, c] = (
-            nt(b["qkb"][r], w[QK, c]) + nt(vlow[r], w[VALUE, c]) + nt(swb[r], w[SWISH, c])
-        ).astype(BF16)
-
-    loop(tiles * PLANES, body)
-    reduce = plane_sum(xs)
-    reduce.start()
-    reduce.run()
-
-    def body(i):
-        b["middle"][at(i, CHUNK)] += reduce.total(i)
-
-    loop(rows // CHUNK, body)
-    reduce.finish()
-    for partner in (place.sib, place.xn, place.yn):
-        pl.semaphore_signal(b["free"], inc=1, device_id=partner, device_id_type=MESH)
-    final_copy = pltpu.make_async_copy(b["middle"], final_out, b["ol"].at[1])
-    final_copy.start()
-    combine(UP)
+    combine(SWISH)
+
+    @pl.when(inner)
+    def _():
+        reduce6.run3()
+
+        def body(i):
+            b["middle"][at(i, CHUNK)] += reduce6.total(i)
+
+        loop(rows // CHUNK, body)
+        reduce6.finish()
+        neighbours_may_write()
+        may_write()
+
+    reduce = plane_sum(part)
+    reduce.fill(
+        lambda r, c: nt(b["qkb"][r], w[QK, c]) + nt(vlow[r], w[VALUE, c]) + nt(swb[r], w[SWISH, c])
+    )
+    reduce.run1()
     finish_gradient(DOWN)
-    pl.semaphore_wait(b["free"], 3)
-    reduce = plane_sum(part)
-    reduce.start()
-    reduce.run()
+    reduce.run2()
+    combine(VALUE)
+    finish_gradient(GATE)
+    reduce.run3()
 
     def body(i):
         r = at(i, CHUNK)
@@ -1461,8 +1713,6 @@
     reduce.finish()
     delta_copy = pltpu.make_async_copy(b["back"], delta_out, b["ol"].at[2])
     delta_copy.start()
-    combine(OUTPUT)
-    finish_gradient(GATE)
 
     for i in range(1, 8):
         gain_copy(i).wait_send()
@@ -1481,13 +1731,24 @@
 
     for i in range(1, 8):
         share_copy(i).start()
-    combine(SWISH)
     finish_gradient(UP)
-    combine(VALUE)
+    combine(QUERY)
+    @pl.when(outer)
+    def _():
+        hop(2, cot_ref, b["cot2"]).wait_send()
+        hop(5, b["cot2"], b["cot2"]).wait_recv()
+
+        def body(i):
+            r = at(i, CHUNK)
+            b["middle"][r] += b["cot2"][r].astype(F32)
+
+        loop(rows // CHUNK, body)
+
+    final_copy = pltpu.make_async_copy(b["middle"], final_out, b["ol"].at[1])
+    final_copy.start()
     finish_gradient(OUTPUT)
-    combine(QUERY)
+    combine(KEY)
     finish_gradient(SWISH)
-    combine(KEY)
     finish_gradient(VALUE)
     finish_gradient(QUERY)
     acc = gsend[dp]
@@ -1515,6 +1776,13 @@
     final_copy.wait()
     delta_copy.wait()
     weights_sent()
+
+    @pl.when(inner)
+    def _():
+        for n in range(2):
+            hop(3 + n, b["rows2"], b["rows2"], halves[n]).wait_send()
+        hop(5, b["cot2"], b["cot2"]).wait_send()
+
     gradients_done()
 
 

time: 480 us -> 447 us (0.931)
  Pallas kernels: 476 us -> 443 us
    pallas_call x1, Pallas kernels: 471 us -> 438 us  [whole_layer(): pl.pallas_call(functools.partial(mega_kernel, tuple(scratch), len(args),...]
where the time goes in v4:
time: 447 us; the launch traced here: 446 us
  Pallas kernels  443 us (99%)
    pallas_call x1, Pallas kernels, whole_layer(): pl.pallas_call(functools.partial(mega_kernel, tuple(scratch), len(args),...  438 us

profile of v4, /device:TPU:8, one launch (start us, length us, event | category | flops | bytes accessed | tf_op | source)
XLA Modules:
  0.0 445.8 jit_solution(6120906640598637737)
XLA Ops:
  1.3 437.9 %whole_layer.1 = (f32[128,2048]{1,0:T(8,128)}, f32[128,2048]{1,0:T(8,128)}, f32[8,256]{1,0:T(8,128)}, bf16[256,512]{1,0:T(8,128)(2,1)}, bf16[256,512]{1,0:T(8,12...) custom-call(bf16[128,2048]{1,0:T(8,128)(2,1)} %refs_0_.1, ...), custom_call_target="tpu_custom_call" | custom-call | tf_op jit(solution)/shard_map/whole_layer/pallas_call | solution.py:1838
  439.2 1.4 fusion
  440.7 5.0 %widen.1 = (bf16[128,2048]{1,0:T(8,128)(2,1)}, f32[128,2048]{1,0:T(8,128)}, f32[256,512]{1,0:T(8,128)}, f32[256,512]{1,0:T(8,128)}, f32[256,1024]{1,0:T(8,128)},...) custom-call(s32[1]{0:T(128)S(6)} %copy.31.refs_2_.counts_ref, ...), custom_call_target="tpu_custom_call" | custom-call | tf_op jit(solution)/shard_map/widen/pallas_call | solution.py:1851

commit v5 on v4

--- a/solution.py
+++ b/solution.py
@@ -142,14 +142,38 @@
             copy.start()
 
     def forward(self):
+        self.forward_across()
+        self.forward_beside()
+
+    def forward_across(self):
         self.xa.wait_recv()
         self.da.start()
         self.yb.wait_recv()
         self.db.start()
+
+    def forward_beside(self):
         self.xb.wait_recv()
         self.s1.start()
         self.ya.wait_recv()
         self.s2.start()
+
+    def own_arrived(self):
+        self.local.wait()
+        self.s0.wait_recv()
+
+    def across_arrived(self):
+        self.da.wait_recv()
+        self.s3a.start()
+        self.db.wait_recv()
+        self.s3b.start()
+        self.s3a.wait_recv()
+        self.s3b.wait_recv()
+
+    def drain(self):
+        for copy in (self.s0, self.s1, self.s2, self.s3a, self.s3b):
+            copy.wait_send()
+        for copy in (self.xa, self.xb, self.ya, self.yb, self.da, self.db):
+            copy.wait_send()
 
     def finish(self):
         self.da.wait_recv()
@@ -616,6 +640,7 @@
 WIDE = 512
 QUERY, KEY = 7, 8
 FEED_FORWARD = (DOWN, GATE, UP)
+INNER_SUMS = (*FEED_FORWARD, OUTPUT)
 GRADIENTS = (*FEED_FORWARD, OUTPUT, SWISH, VALUE, QUERY, KEY)
 TILE = 256
 
@@ -630,6 +655,11 @@
         return carry
 
     lax.fori_loop(0, count, step, 0)
+
+
+def together(*steps):
+    for step in steps:
+        step()
 
 
 def at(index, size):
@@ -642,7 +672,7 @@
     return dict(
         w=pltpu.VMEM((7, hidden, WIDE), BF16),
         xs=pltpu.VMEM((total, hidden), BF16),
-        xt=pltpu.VMEM((hidden, total), BF16),
+        xt=pltpu.VMEM((total, hidden), BF16),
         outs=pltpu.VMEM((total, hidden), BF16),
         part=pltpu.VMEM((total, hidden), BF16),
         theirs=pltpu.VMEM((4, rows, hidden), BF16),
@@ -657,8 +687,8 @@
         ginv=pltpu.VMEM((total, 128), F32),
         gated=pltpu.VMEM((total, VAL_DIM), BF16),
         hid=pltpu.VMEM((total, WIDE), BF16),
-        gate=pltpu.VMEM((total, WIDE), F32),
-        up=pltpu.VMEM((total, WIDE), F32),
+        gate=pltpu.VMEM((TILE, WIDE), F32),
+        up=pltpu.VMEM((TILE, WIDE), F32),
         gb=pltpu.VMEM((total, WIDE), BF16),
         ub=pltpu.VMEM((total, WIDE), BF16),
         sb=pltpu.VMEM((total, SEQ_LEN), BF16),
@@ -679,8 +709,9 @@
         rows2=pltpu.VMEM((rows, hidden), BF16),
         cot2=pltpu.VMEM((rows, hidden), BF16),
         ub2=pltpu.VMEM((total, WIDE), BF16),
-        hop_s=dma((6,)),
-        hop_r=dma((6,)),
+        gated2=pltpu.VMEM((total, VAL_DIM), BF16),
+        hop_s=dma((9,)),
+        hop_r=dma((9,)),
         gd_s=dma((13,)),
         gd_r=dma((13,)),
         gown=pltpu.VMEM((8, 256), F32),
@@ -691,7 +722,7 @@
         zr=dma((7, 2, 4)),
         rs=dma((8, 3)),
         rr=dma((8, 4)),
-        ra=dma((8, 2)),
+        ra=dma((8, 3)),
         stl=dma((4,)),
         fl=dma((4,)),
         fe_s=dma((8,)),
@@ -757,32 +788,44 @@
         for j in (3, 1, 2, 0):
             self.swap[j].start()
 
-    def fill(self, tile_value):
-        p, tile = self.place, 2 * self.rows
-
+    def fill(self, tile_value, sending=None):
         def body(i):
-            j = jnp.where(i == 0, 3, jnp.where(i == 3, 0, i))
-            chip_x = jnp.where(lax.rem(j, 2) == 1, 1 - p.x, p.x)
-            chip_y = jnp.where(j >= 2, 1 - p.y, p.y)
-            chip = chip_x * 2 + chip_y
-            r = at(chip, tile)
-
-            def inner(n):
-                c = at(n, WIDE)
-                self.part[r, c] = tile_value(r, c).astype(BF16)
-
-            loop(self.part.shape[1] // WIDE, inner)
-            source = self.part.at[rows_of(chip * 2 + 1 - p.c, self.rows)]
-            self.remote(j, source, self.theirs.at[j], p.sib).start()
+            self.fill_chip(jnp.where(i == 0, 3, jnp.where(i == 3, 0, i)), tile_value, sending)
 
         loop(4, body)
 
+    def chip(self, j):
+        p = self.place
+        chip_x = jnp.where(lax.rem(j, 2) == 1, 1 - p.x, p.x)
+        chip_y = jnp.where(j >= 2, 1 - p.y, p.y)
+        return chip_x * 2 + chip_y
+
+    def fill_chip(self, j, tile_value, sending=None):
+        chip = self.chip(j)
+        r = at(chip, 2 * self.rows)
+
+        def inner(n):
+            c = at(n, WIDE)
+            self.part[r, c] = tile_value(r, c).astype(BF16)
+
+        loop(self.part.shape[1] // WIDE, inner)
+        source = self.part.at[rows_of(chip * 2 + 1 - self.place.c, self.rows)]
+        send = self.remote(j, source, self.theirs.at[j], self.place.sib)
+        if sending is None:
+            send.start()
+        else:
+            pl.when(sending)(send.start)
+
+    def take(self, j):
+        copies = {3: (self.da, self.db), 1: (self.xa,), 2: (self.yb,)}[j]
+        self.swap[j].wait_recv()
+        self.add(j, 0, self.rows, self.theirs.at[j], 0)
+        for copy in copies:
+            copy.start()
+
     def run1(self):
-        for j, copies in ((3, (self.da, self.db)), (1, (self.xa,)), (2, (self.yb,))):
-            self.swap[j].wait_recv()
-            self.add(j, 0, self.rows, self.theirs.at[j], 0)
-            for copy in copies:
-                copy.start()
+        for j in (3, 1, 2):
+            self.take(j)
 
     def run2(self):
         h = self.half
@@ -816,7 +859,7 @@
     gain_refs = refs[5:9]
     q_w, k_w, v_w, s_w, o_w, g_w, u_w, d_w = refs[9:count_in]
     outs = refs[count_in : count_in + count_out]
-    final_out, delta_out, gains_out, q_g, k_g, v_g, s_g, o_g, g_g, u_g, d_g, stage, heard, added = outs
+    final_out, delta_out, gains_out, q_g, k_g, v_g, s_g, o_g, g_g, u_g, d_g, stage, heard, added, parked = outs
     b = {name: ref for name, ref in zip(names, refs[count_in + count_out :], strict=True)}
     w, xs, xt, st, part, turned = b["w"], b["xs"], b["xt"], b["st"], b["part"], b["turned"]
     x_ref, cot_ref = b["xr"], b["cr"]
@@ -915,8 +958,8 @@
                 block_copy(k, z, half, slot, plane(step)).start()
 
         if k in FEED_FORWARD:
-            pl.when(outer)(both)
-            pl.when(inner)(lambda: block_copy(k, z, half, 0, plane(-towards)).start())
+            step = jnp.where(outer, jnp.where(first_plane, 1, -1), -towards)
+            block_copy(k, z, half, 0, plane(step)).start()
         else:
             both()
 
@@ -947,9 +990,13 @@
                     block = jnp.where(first_plane, i + 1, i)
                     block_copy(k, block, half, 0, beside).wait_recv()
 
+    def pass_inner(k):
+        copy = block_copy(k, jnp.where(z == 1, 0, 3), 0, 1, plane(-towards))
+        copy.wait_recv()
+        copy.start()
+
     def arrive_inner(k):
-        for i in range(3):
-            block = jnp.where(z == 1, (0, 2, 3)[i], (0, 1, 3)[i])
+        for block in (near, far):
             block_copy(k, block, 0, 0, beside).wait_recv()
 
     def weights_sent():
@@ -959,7 +1006,7 @@
             for half in parts(k):
                 block_copy(k, z, half, 0, beside).wait_send()
                 if k in FEED_FORWARD:
-                    pl.when(outer)(lambda k=k, half=half: block_copy(k, z, half, 1, beside).wait_send())
+                    pl.when(inner)(lambda k=k, half=half: block_copy(k, z, half, 1, beside).wait_send())
                 else:
                     block_copy(k, z, half, 1, beside).wait_send()
 
@@ -986,12 +1033,12 @@
     def staged(c, block, slot):
         return pltpu.make_async_copy(slot_of(c, slot), share(stage, c, block), b["stl"].at[slot])
 
-    def to_added(c, block, which, target):
+    def to_added(c, block, which, target, slot=None):
         n = number(c)
         return remote(
             share(stage, c, block),
             share(added, c, which),
-            b["rs"].at[n, which],
+            b["rs"].at[n, which if slot is None else slot],
             b["ra"].at[n, which],
             target,
         )
@@ -1016,12 +1063,8 @@
             to_added(c, z + 2 * step, 1, plane(step)).start()
             to_heard(c, z + step, 2, plane(step)).start()
 
-        @pl.when(inner)
-        def _():
-            to_heard(c, z + towards, 2, plane(towards)).start()
-
     def send_inner(c):
-        to_added(c, far, 0, plane(-towards)).start()
+        to_added(c, far, 2, plane(-towards), 0).start()
         to_heard(c, near, 1, plane(-towards)).start()
 
     def rounds(c, body):
@@ -1058,16 +1101,16 @@
                 rounds(c, body)
                 back = local(slot_of(c, i), share(stage, c, blocks[i]), i)
                 back.start()
-            for i, step in enumerate((-2 * towards, -towards)):
+            for i in range(2):
                 local(slot_of(c, i), share(stage, c, blocks[i]), i).wait()
-                to_heard(c, blocks[i], i, plane(step)).start()
+            send_inner(c)
 
     def combine_inner(c):
         block = z + towards
         mine = local(share(stage, c, block), slot_of(c, 0), 0)
-        theirs = local(share(added, c, 0), slot_of(c, 1), 1)
+        theirs = local(share(added, c, 2), slot_of(c, 1), 1)
         mine.start()
-        to_added(c, block, 0, beside).wait_recv()
+        to_added(c, block, 2, beside, 0).wait_recv()
         theirs.start()
         mine.wait()
         theirs.wait()
@@ -1101,8 +1144,6 @@
             remote(source.at[given_half], slot, b["fe_s"].at[n], b["fe_r"].at[n], beside),
         )
 
-    sources = (jnp.where(z == 1, 0, 1), jnp.where(z == 2, 3, 2))
-
     def finish_gradient(c, last=False):
         n = number(c)
 
@@ -1117,14 +1158,16 @@
             load.start()
             return load
 
-        if c in FEED_FORWARD:
-            source = jnp.where((z == 0) | (z == 2), 1, 2)
+        source = jnp.where((z == 0) | (z == 2), 1, 2)
+        if c in INNER_SUMS:
 
             @pl.when(outer)
             def _():
                 arrival(0, source).wait()
 
-            @pl.when(inner)
+        else:
+
+            @pl.when(outer)
             def _():
                 own_load().start()
                 arrival(1, source).wait()
@@ -1137,18 +1180,21 @@
 
                 rounds(c, body)
 
-        else:
+        @pl.when(inner)
+        def _():
             own_load().start()
-            loads = [arrival(1 + i, source) for i, source in enumerate(sources)]
+            loads = [arrival(1, source)]
+            if c not in INNER_SUMS:
+                loads.append(arrival(2, jnp.where(z == 1, 0, 3)))
             own_load().wait()
             for load in loads:
                 load.wait()
 
             def body(r, lanes):
-                st[0, r, lanes] = (
-                    st[0, r, lanes].astype(F32)
-                    + (st[1, r, lanes].astype(F32) + st[2, r, lanes].astype(F32))
-                ).astype(BF16)
+                acc = st[0, r, lanes].astype(F32) + st[1, r, lanes].astype(F32)
+                if c not in INNER_SUMS:
+                    acc = acc + st[2, r, lanes].astype(F32)
+                st[0, r, lanes] = acc.astype(BF16)
 
             rounds(c, body)
 
@@ -1179,7 +1225,7 @@
                         share(stage, c, 0), share(heard, c, 0), b["rs"].at[n, slot], b["rr"].at[n, 0], beside
                     ).wait_send()
 
-            if c in FEED_FORWARD:
+            if c in INNER_SUMS:
                 pl.when(inner)(sent)
             else:
                 sent()
@@ -1285,10 +1331,18 @@
     spread(SWISH)
     first.finish()
 
+    def turned_rows(i):
+        return at(i // 2, 512), at(lax.rem(i, 2), 8 * rows)
+
     def body(i):
-        xt[at(i, 256), :] = xs[:, at(i, 256)].T
+        r, lanes = turned_rows(i // 2)
+        r = pl.ds(pl.multiple_of((i // 4) * 512 + lax.rem(i, 2) * 256, 256), 256)
+        xt[r, lanes] = xs[:, at(i, 256)].T
 
     loop(hidden // 256, body)
+    park = pltpu.make_async_copy(xt, parked, b["ol"].at[5])
+    unpark = pltpu.make_async_copy(parked, xt, b["ol"].at[0])
+    pl.when(inner)(park.start)
     spread(OUTPUT)
 
     arrive(QK)
@@ -1376,6 +1430,9 @@
     def _():
         for n in range(2):
             hop(n, low, b["rows2"], halves[n]).start()
+        hop(6, b["gated"], b["gated2"]).start()
+
+    pl.when(inner)(lambda: pass_inner(GATE))
 
     def gelu_of(t):
         inner_value = 0.7978845608028654 * (t + 0.044715 * t * t * t)
@@ -1399,35 +1456,22 @@
             acc = acc + nt(left[r, lanes], w[k, lanes])
         return acc
 
-    def gate_projection(mixer):
-        def body(i):
-            r = at(i, TILE)
-            b["gate"][r] = matmul(mixer[r], w[GATE])
-
-        loop(tiles, body)
-
-    def up_projection(mixer, hid):
-        def body(i):
-            r = at(i, TILE)
-            up = matmul(mixer[r], w[UP])
-            b["up"][r] = up
-            gate = b["gate"][r]
-            share_of, _ = gelu_of(gate)
-            hid[r] = (gate * share_of * up).astype(BF16)
-
-        loop(tiles, body)
-
-    def hidden_backward(cots, gb, ub):
-        def body(i):
-            r = at(i, TILE)
-            back = times_turned(cots, r, DOWN)
-            gate, up = b["gate"][r], b["up"][r]
-            share_of, tanh = gelu_of(gate)
-            slope = 0.5 * gate * (1.0 - tanh * tanh) * (0.7978845608028654 * (1.0 + 0.134145 * gate * gate))
-            gb[r] = (back * up * (share_of + slope)).astype(BF16)
-            ub[r] = (back * gate * share_of).astype(BF16)
-
-        loop(tiles, body)
+    def hidden_tile(mixer, hid, r):
+        gate = matmul(mixer[r], w[GATE])
+        b["gate"][...] = gate
+        up = matmul(mixer[r], w[UP])
+        b["up"][...] = up
+        gate = b["gate"][...]
+        share_of, _ = gelu_of(gate)
+        hid[r] = (gate * share_of * up).astype(BF16)
+
+    def back_tile(cots, gb, ub, r):
+        back = times_turned(cots, r, DOWN)
+        gate, up = b["gate"][...], b["up"][...]
+        share_of, tanh = gelu_of(gate)
+        slope = 0.5 * gate * (1.0 - tanh * tanh) * (0.7978845608028654 * (1.0 + 0.134145 * gate * gate))
+        gb[r] = (back * up * (share_of + slope)).astype(BF16)
+        ub[r] = (back * gate * share_of).astype(BF16)
 
     def refill(c):
         copies = [pltpu.make_async_copy(stage.at[c, i], st.at[i], b["fl"].at[i]) for i in range(PLANES)]
@@ -1494,19 +1538,25 @@
         second.start()
         hop(2, cot_ref, b["cot2"]).wait_recv()
         second.forward()
+        pass_inner(UP)
         other_cot = Gather(place, b["cot2"], part, b["gc_s"], b["gc_r"])
         reduce.finish()
         neighbours_may_write()
         may_write()
         other_cot.start()
+        pass_inner(DOWN)
         second.finish()
         arrive_inner(GATE)
-        gate_projection(xs)
         arrive_inner(UP)
-        up_projection(xs, b["hid"])
         other_cot.forward()
         arrive_inner(DOWN)
-        hidden_backward(outs_ref, b["gb"], b["ub"])
+
+        def body(i):
+            r = at(i, TILE)
+            hidden_tile(xs, b["hid"], r)
+            back_tile(outs_ref, b["gb"], b["ub"], r)
+
+        loop(tiles, body)
         down_gradient(b["hid"], outs_ref, False)
         neighbours_may_write()
         other_cot.finish()
@@ -1517,29 +1567,40 @@
         hop(1, low, b["rows2"], halves[1]).wait_recv()
         other.start_second_half()
         weight_gradient(GATE, xs, b["gb"], False)
-        other.forward()
+        other.forward_across()
+        other.own_arrived()
+        park.wait()
+        reduce2 = plane_sum(xt)
+
+        def body(i):
+            pl.when(i == 1)(lambda: together(other.forward_beside, other.s1.wait_recv))
+            pl.when(i == 2)(other.s2.wait_recv)
+            pl.when(i == 3)(other.across_arrived)
+            r = at(reduce2.chip(i), TILE)
+            hidden_tile(outs_ref, hid2, r)
+            back_tile(part, gb2, ub2, r)
+            reduce2.fill_chip(i, mixer_input(gb2, ub2))
+            pl.when(i == 2)(lambda: reduce2.take(1))
+            pl.when(i == 3)(lambda: reduce2.take(2))
+
+        loop(PLANES, body)
+        reduce2.take(3)
         weight_gradient(UP, xs, b["ub"], False)
-        other.finish()
-        gate_projection(outs_ref)
-        up_projection(outs_ref, hid2)
-        hidden_backward(part, gb2, ub2)
-        reduce2 = plane_sum(xs)
-        reduce2.fill(mixer_input(gb2, ub2))
-        reduce2.run1()
+        reduce2.run2()
         down_gradient(hid2, part, True)
         send_inner(DOWN)
-        reduce2.run2()
         reduce2.run3()
-
         for n in range(2):
 
             def body(i, n=n):
                 i = n * (rows // 2 // CHUNK) + i
                 b["rows2"][at(i, CHUNK)] = reduce2.total(i).astype(BF16)
 
+            other.drain() if n == 0 else None
             loop(rows // 2 // CHUNK, body)
             hop(3 + n, b["rows2"], b["rows2"], halves[n]).start()
         reduce2.finish()
+        unpark.start()
         neighbours_may_write()
         may_write()
         reduce3 = plane_sum(part)
@@ -1548,10 +1609,9 @@
         weight_gradient(GATE, outs_ref, gb2, True)
         send_inner(GATE)
         reduce3.run2()
-        combine_inner(DOWN)
         weight_gradient(UP, outs_ref, ub2, True)
         send_inner(UP)
-        neighbours_may_write()
+        combine_inner(DOWN)
         reduce3.run3()
 
         def body(i):
@@ -1559,9 +1619,13 @@
 
         loop(rows // CHUNK, body)
         reduce3.finish()
+        neighbours_may_write()
         may_write()
-
-    third = Gather(place, low, outs_ref, *gather_sems)
+        hop(7, low, b["cot2"]).wait_recv()
+
+    third = Gather(place, low, xs, *gather_sems)
+    other_middle = Gather(place, b["cot2"], part, b["gd_s"], b["gd_r"])
+    outs_ref = b["outs"]
 
     @pl.when(outer)
     def _():
@@ -1580,29 +1644,40 @@
                 third.start_first_half()
             else:
                 third.start_second_half()
-
-    pl.when(inner)(third.start)
-    third.forward()
-    pl.when(inner)(lambda: combine_inner(GATE))
-    pl.when(inner)(lambda: mixer_output(hid2, xs))
-    third.finish()
-    reduce5 = plane_sum(xs)
-    pl.when(inner)(reduce5.start)
-    pl.when(inner)(lambda: combine_inner(UP))
-
-    turned_of(b["gated"])
-
-    def body(i):
-        stage_block(OUTPUT, i, matmul(turned[...], b["outs"][:, at(i, 512)]))
-
-    loop(PLANES, body)
-    send_gradient(OUTPUT)
-    pl.when(inner)(reduce5.run1)
+                hop(7, low, b["cot2"]).start()
+        third.forward()
+        third.finish()
+
+    def output_gradient(rows_ref, cots, more):
+        if more:
+            refill(OUTPUT)
+        turned_of(rows_ref)
+
+        def body(i):
+            product_of(OUTPUT, i, matmul(turned[...], cots[:, at(i, 512)]), more)
+
+        loop(PLANES, body)
+        all_staged(OUTPUT)
+
+    reduce5 = plane_sum(outs_ref)
+
+    @pl.when(inner)
+    def _():
+        third.start()
+        mixer_output(hid2, outs_ref)
+        third.forward_across()
+        other_middle.start()
+        finish_gradient(DOWN)
+        combine_inner(GATE)
+        third.forward_beside()
+        third.finish()
+        other_middle.forward_across()
+
     swb, rb, vlow = b["gb"], b["ub2"], b["ub"]
 
     def body(i):
         r = at(i, TILE)
-        back = times_turned(b["outs"], r, OUTPUT)
+        back = times_turned(xs, r, OUTPUT)
         swish, hat = b["swish"][r], b["ghat"][r]
         gate = jax.nn.sigmoid(swish)
         swb[r] = (back * hat * gate * (1.0 + swish * (1.0 - gate))).astype(BF16)
@@ -1612,34 +1687,32 @@
 
     def projection_gradient(c, right, lanes=slice(None)):
         def body(i):
-            value = matmul(xt[at(i, 512)], right[:, lanes]).astype(BF16)
+            value = matmul(xt[turned_rows(i)], right[:, lanes]).astype(BF16)
             st[i, :, 0 : value.shape[1]] = value
             staged(c, i, i).start()
 
         loop(PLANES, body)
         send_gradient(c)
 
-    pl.when(inner)(reduce5.run2)
+    pl.when(inner)(lambda: together(other_middle.forward_beside, unpark.wait))
     projection_gradient(SWISH, swb)
 
     @pl.when(inner)
     def _():
-        reduce5.run3()
-
-        def body(i):
-            b["cot2"][at(i, CHUNK)] = reduce5.total(i).astype(BF16)
-
-        loop(rows // CHUNK, body)
-        hop(5, b["cot2"], b["cot2"]).start()
-        reduce5.finish()
-        neighbours_may_write()
-        mixer_output(b["hid"], xs)
-        may_write()
-        plane_sum(xs).start()
-
-    reduce6 = plane_sum(xs)
-    combine(OUTPUT)
-    pl.when(inner)(reduce6.run1)
+        output_gradient(b["gated"], xs, False)
+
+    combine(SWISH)
+
+    @pl.when(inner)
+    def _():
+        other_middle.finish()
+        reduce5.start()
+        hop(6, b["gated"], b["gated2"]).wait_recv()
+        output_gradient(b["gated2"], part, True)
+        send_inner(OUTPUT)
+        combine_inner(UP)
+        reduce5.run1()
+
     def body(i):
         r = at(i, TILE)
         decay = b["decay"][at(lax.rem(i, per_slot), TILE)]
@@ -1654,8 +1727,9 @@
         ).astype(BF16)
 
     loop(tiles, body)
-    pl.when(inner)(reduce6.run2)
     projection_gradient(VALUE, vlow)
+    pl.when(inner)(reduce5.run2)
+    pl.when(inner)(lambda: combine_inner(SWISH))
     turned_of(b["sb"])
 
     def turn_back(acc, tile, scale):
@@ -1675,7 +1749,39 @@
     loop(tiles, body)
     projection_gradient(QUERY, b["qkb"], slice(0, 256))
     projection_gradient(KEY, b["qkb"], slice(256, 512))
-    combine(SWISH)
+    reduce6 = plane_sum(outs_ref)
+
+    @pl.when(inner)
+    def _():
+        reduce5.run3()
+
+        def body(i):
+            b["cot2"][at(i, CHUNK)] = reduce5.total(i).astype(BF16)
+
+        loop(rows // CHUNK, body)
+        hop(5, b["cot2"], b["cot2"]).start()
+        reduce5.finish()
+        neighbours_may_write()
+
+    combine(VALUE)
+
+    @pl.when(inner)
+    def _():
+        finish_gradient(GATE)
+        may_write()
+        reduce6.fill(lambda r, c: matmul(b["hid"][r], w[DOWN, c]))
+        combine_inner(OUTPUT)
+        reduce6.run1()
+
+    reduce = plane_sum(part)
+    reduce.fill(
+        lambda r, c: nt(b["qkb"][r], w[QK, c]) + nt(vlow[r], w[VALUE, c]) + nt(swb[r], w[SWISH, c]),
+        sending=outer,
+    )
+    pl.when(inner)(reduce6.run2)
+    combine(QUERY)
+    pl.when(inner)(lambda: combine_inner(VALUE))
+    pl.when(outer)(lambda: finish_gradient(DOWN))
 
     @pl.when(inner)
     def _():
@@ -1688,16 +1794,16 @@
         reduce6.finish()
         neighbours_may_write()
         may_write()
-
-    reduce = plane_sum(part)
-    reduce.fill(
-        lambda r, c: nt(b["qkb"][r], w[QK, c]) + nt(vlow[r], w[VALUE, c]) + nt(swb[r], w[SWISH, c])
-    )
+        reduce.start()
+
+    pl.when(outer)(lambda: finish_gradient(GATE))
     reduce.run1()
-    finish_gradient(DOWN)
+    combine(KEY)
+    pl.when(inner)(lambda: combine_inner(QUERY))
     reduce.run2()
-    combine(VALUE)
-    finish_gradient(GATE)
+    finish_gradient(UP)
+    pl.when(inner)(lambda: combine_inner(KEY))
+    finish_gradient(SWISH)
     reduce.run3()
 
     def body(i):
@@ -1731,8 +1837,6 @@
 
     for i in range(1, 8):
         share_copy(i).start()
-    finish_gradient(UP)
-    combine(QUERY)
     @pl.when(outer)
     def _():
         hop(2, cot_ref, b["cot2"]).wait_send()
@@ -1747,8 +1851,6 @@
     final_copy = pltpu.make_async_copy(b["middle"], final_out, b["ol"].at[1])
     final_copy.start()
     finish_gradient(OUTPUT)
-    combine(KEY)
-    finish_gradient(SWISH)
     finish_gradient(VALUE)
     finish_gradient(QUERY)
     acc = gsend[dp]
@@ -1782,6 +1884,11 @@
         for n in range(2):
             hop(3 + n, b["rows2"], b["rows2"], halves[n]).wait_send()
         hop(5, b["cot2"], b["cot2"]).wait_send()
+
+    @pl.when(outer)
+    def _():
+        hop(6, b["gated"], b["gated2"]).wait_send()
+        hop(7, low, b["cot2"]).wait_send()
 
     gradients_done()
 
@@ -1832,14 +1939,15 @@
         *(shape(weight.shape, BF16) for weight in weights),
         shape((7, PLANES, WIDE, WIDE), BF16),
         shape((7, PLANES, WIDE, WIDE), BF16),
-        shape((7, 2, WIDE, WIDE), BF16),
+        shape((7, 3, WIDE, WIDE), BF16),
+        shape((8 * rows, hidden), BF16),
     )
     scalar = pl.BlockSpec(memory_space=pltpu.SMEM)
     results = pl.pallas_call(
         functools.partial(mega_kernel, tuple(scratch), len(args), len(outs)),
         out_shape=outs,
         in_specs=[ANY, ANY, scalar] + [VM] * 6 + [ANY] * 8,
-        out_specs=tuple([ANY, ANY, VM] + [ANY] * 11),
+        out_specs=tuple([ANY, ANY, VM] + [ANY] * 12),
         scratch_shapes=list(scratch.values()),
         compiler_params=pltpu.CompilerParams(
             collective_id=0, has_side_effects=True, vmem_limit_bytes=67043328

time: 447 us -> 433 us (0.969)
  Pallas kernels: 443 us -> 429 us
    pallas_call x1, Pallas kernels: 438 us -> 424 us  [whole_layer(): pl.pallas_call(functools.partial(mega_kernel, tuple(scratch), len(args),...]
where the time goes in v5:
time: 433 us; the launch traced here: 432 us
  Pallas kernels  429 us (99%)
    pallas_call x1, Pallas kernels, whole_layer(): pl.pallas_call(functools.partial(mega_kernel, tuple(scratch), len(args),...  424 us

profile of v5, /device:TPU:8, one launch (start us, length us, event | category | flops | bytes accessed | tf_op | source)
XLA Modules:
  0.0 432.0 jit_solution(993736631738193103)
XLA Ops:
  1.3 424.1 %whole_layer.1 = (f32[128,2048]{1,0:T(8,128)}, f32[128,2048]{1,0:T(8,128)}, f32[8,256]{1,0:T(8,128)}, bf16[256,512]{1,0:T(8,128)(2,1)}, bf16[256,512]{1,0:T(8,12...) custom-call(bf16[128,2048]{1,0:T(8,128)(2,1)} %refs_0_.1, ...), custom_call_target="tpu_custom_call" | custom-call | tf_op jit(solution)/shard_map/whole_layer/pallas_call | solution.py:1946
  425.4 1.4 fusion
  426.8 5.0 %widen.1 = (bf16[128,2048]{1,0:T(8,128)(2,1)}, f32[128,2048]{1,0:T(8,128)}, f32[256,512]{1,0:T(8,128)}, f32[256,512]{1,0:T(8,128)}, f32[256,1024]{1,0:T(8,128)},...) custom-call(s32[1]{0:T(128)S(6)} %copy.31.refs_2_.counts_ref, ...), custom_call_target="tpu_custom_call" | custom-call | tf_op jit(solution)/shard_map/widen/pallas_call | solution.py:1959

commit v6 on v5

--- a/solution.py
+++ b/solution.py
@@ -675,9 +675,7 @@
         xt=pltpu.VMEM((total, hidden), BF16),
         outs=pltpu.VMEM((total, hidden), BF16),
         part=pltpu.VMEM((total, hidden), BF16),
-        theirs=pltpu.VMEM((4, rows, hidden), BF16),
-        got=pltpu.VMEM((2, rows, hidden), BF16),
-        across=pltpu.VMEM((2, rows // 2, hidden), BF16),
+        room=pltpu.VMEM((7 * rows, hidden), BF16),
         q=pltpu.VMEM((total, KEY_DIM), BF16),
         k=pltpu.VMEM((total, KEY_DIM), BF16),
         v=pltpu.VMEM((total, VAL_DIM), BF16),
@@ -737,18 +735,18 @@
         gc_r=dma((13,)),
         re_s=dma((10,)),
         re_r=dma((10,)),
+        rf_s=dma((10,)),
+        rf_r=dma((10,)),
         ol=dma((6,)),
         free=pltpu.SemaphoreType.REGULAR,
     )
 
 
 class PlaneSum(Reduce):
-    def __init__(self, place, part, theirs, got, across, send, recv):
+    def __init__(self, place, part, room, rows, send, recv, y_first=False):
         p = place
-        rows = theirs.shape[1]
         h = rows // 2
-        self.rows, self.half, self.part = rows, h, part
-        self.theirs, self.got, self.across = theirs, got, across
+        self.rows, self.half, self.part, self.room, self.y_first = rows, h, part, room, y_first
         self.base = [p.block(j) * rows for j in range(4)]
 
         def remote(k, source, target_ref, target):
@@ -764,23 +762,31 @@
         def piece(j, lo):
             return part.at[pl.ds(pl.multiple_of(self.base[j] + lo, 8), h)]
 
+        def got(k, lo):
+            return room.at[pl.ds((4 + k) * rows + lo, h)]
+
+        def across(k):
+            return room.at[pl.ds(6 * rows + k * h, h)]
+
         self.place, self.remote = p, remote
-        a, b = pl.ds(0, h), pl.ds(h, h)
         self.swap = [
-            remote(j, part.at[rows_of(p.block(j, 1), rows)], theirs.at[j], p.sib) for j in range(4)
+            remote(j, part.at[rows_of(p.block(j, 1), rows)], self.theirs(j), p.sib) for j in range(4)
         ]
-        self.da = remote(4, piece(3, 0), across.at[0], p.xn)
-        self.db = remote(5, piece(3, h), across.at[1], p.yn)
-        self.xa = remote(6, piece(1, 0), got.at[0, a], p.xn)
-        self.xb = remote(7, piece(1, h), got.at[0, b], p.xn)
-        self.ya = remote(8, piece(2, 0), got.at[1, a], p.yn)
-        self.yb = remote(9, piece(2, h), got.at[1, b], p.yn)
-
-    def add(self, j, lo, n, other, other_lo):
+        self.da = remote(4, piece(3, 0), across(0), p.yn if y_first else p.xn)
+        self.db = remote(5, piece(3, h), across(1), p.yn)
+        self.xa = remote(6, piece(1, 0), got(0, 0), p.xn)
+        self.xb = remote(7, piece(1, h), got(0, h), p.xn)
+        self.ya = remote(8, piece(2, 0), got(1, 0), p.yn)
+        self.yb = remote(9, piece(2, h), got(1, h), p.yn)
+
+    def theirs(self, j):
+        return self.room.at[rows_of(j, self.rows)]
+
+    def add(self, j, lo, n, first):
         def body(i):
             r = pl.ds(pl.multiple_of(self.base[j] + lo + i * CHUNK, CHUNK), CHUNK)
-            q = pl.ds(pl.multiple_of(other_lo + i * CHUNK, CHUNK), CHUNK)
-            self.part[r] = (self.part[r].astype(F32) + other[q].astype(F32)).astype(BF16)
+            q = pl.ds(pl.multiple_of(first + i * CHUNK, CHUNK), CHUNK)
+            self.part[r] = (self.part[r].astype(F32) + self.room[q].astype(F32)).astype(BF16)
 
         loop(n // CHUNK, body)
 
@@ -810,16 +816,19 @@
 
         loop(self.part.shape[1] // WIDE, inner)
         source = self.part.at[rows_of(chip * 2 + 1 - self.place.c, self.rows)]
-        send = self.remote(j, source, self.theirs.at[j], self.place.sib)
+        send = self.remote(j, source, self.theirs(j), self.place.sib)
         if sending is None:
             send.start()
         else:
             pl.when(sending)(send.start)
 
     def take(self, j):
-        copies = {3: (self.da, self.db), 1: (self.xa,), 2: (self.yb,)}[j]
+        if self.y_first:
+            copies = {3: (self.da, self.db), 1: (), 2: (self.ya, self.yb)}[j]
+        else:
+            copies = {3: (self.da, self.db), 1: (self.xa,), 2: (self.yb,)}[j]
         self.swap[j].wait_recv()
-        self.add(j, 0, self.rows, self.theirs.at[j], 0)
+        self.add(j, 0, self.rows, j * self.rows)
         for copy in copies:
             copy.start()
 
@@ -828,12 +837,20 @@
             self.take(j)
 
     def run2(self):
-        h = self.half
+        h, across = self.half, 6 * self.rows
+        if self.y_first:
+            self.da.wait_recv()
+            self.add(1, 0, h, across)
+            self.xa.start()
+            self.db.wait_recv()
+            self.add(1, h, h, across + h)
+            self.xb.start()
+            return
         self.db.wait_recv()
-        self.add(1, h, h, self.across.at[1], 0)
+        self.add(1, h, h, across + h)
         self.xb.start()
         self.da.wait_recv()
-        self.add(2, 0, h, self.across.at[0], 0)
+        self.add(2, 0, h, across)
         self.ya.start()
 
     def run3(self):
@@ -847,9 +864,11 @@
         self.run3()
 
     def total(self, i):
-        r = pl.ds(pl.multiple_of(i * CHUNK, CHUNK), CHUNK)
-        mine = pl.ds(pl.multiple_of(self.base[0] + i * CHUNK, CHUNK), CHUNK)
-        pieces = (self.part[mine], self.theirs[0, r], self.got[0, r], self.got[1, r])
+        def at_row(first):
+            return pl.ds(pl.multiple_of(first + i * CHUNK, CHUNK), CHUNK)
+
+        n = self.rows
+        pieces = (self.part[at_row(self.base[0])], *(self.room[at_row(k * n)] for k in (0, 4, 5)))
         one, two, three, four = (piece.astype(F32) for piece in pieces)
         return (one + two) + (three + four)
 
@@ -1260,8 +1279,8 @@
 
     gather_sems = (b["ga_s"], b["ga_r"])
 
-    def plane_sum(ref):
-        return PlaneSum(place, ref, b["theirs"], b["got"], b["across"], b["re_s"], b["re_r"])
+    def plane_sum(ref, y_first=False):
+        return PlaneSum(place, ref, b["room"], rows, b["re_s"], b["re_r"], y_first)
 
     for k in range(7):
         keep(k)
@@ -1562,10 +1581,9 @@
         other_cot.finish()
         other = Gather(place, b["rows2"], outs_ref, b["gd_s"], b["gd_r"])
         may_write()
-        hop(0, low, b["rows2"], halves[0]).wait_recv()
-        other.start_first_half()
-        hop(1, low, b["rows2"], halves[1]).wait_recv()
-        other.start_second_half()
+        for n in range(2):
+            hop(n, low, b["rows2"], halves[n]).wait_recv()
+        other.start()
         weight_gradient(GATE, xs, b["gb"], False)
         other.forward_across()
         other.own_arrived()
@@ -1585,10 +1603,12 @@
 
         loop(PLANES, body)
         reduce2.take(3)
+        down_gradient(hid2, part, True)
+        send_inner(DOWN)
         weight_gradient(UP, xs, b["ub"], False)
         reduce2.run2()
-        down_gradient(hid2, part, True)
-        send_inner(DOWN)
+        weight_gradient(GATE, outs_ref, gb2, True)
+        send_inner(GATE)
         reduce2.run3()
         for n in range(2):
 
@@ -1606,11 +1626,9 @@
         reduce3 = plane_sum(part)
         reduce3.fill(mixer_input(b["gb"], b["ub"]))
         reduce3.run1()
-        weight_gradient(GATE, outs_ref, gb2, True)
-        send_inner(GATE)
-        reduce3.run2()
         weight_gradient(UP, outs_ref, ub2, True)
         send_inner(UP)
+        reduce3.run2()
         combine_inner(DOWN)
         reduce3.run3()
 
@@ -1659,19 +1677,17 @@
         loop(PLANES, body)
         all_staged(OUTPUT)
 
-    reduce5 = plane_sum(outs_ref)
+    reduce5 = plane_sum(outs_ref, y_first=True)
 
     @pl.when(inner)
     def _():
         third.start()
         mixer_output(hid2, outs_ref)
         third.forward_across()
-        other_middle.start()
-        finish_gradient(DOWN)
         combine_inner(GATE)
         third.forward_beside()
         third.finish()
-        other_middle.forward_across()
+        other_middle.start()
 
     swb, rb, vlow = b["gb"], b["ub2"], b["ub"]
 
@@ -1694,17 +1710,17 @@
         loop(PLANES, body)
         send_gradient(c)
 
-    pl.when(inner)(lambda: together(other_middle.forward_beside, unpark.wait))
+    pl.when(inner)(unpark.wait)
     projection_gradient(SWISH, swb)
+    pl.when(inner)(other_middle.forward_across)
+    combine(SWISH)
 
     @pl.when(inner)
     def _():
+        other_middle.forward_beside()
+        finish_gradient(DOWN)
+        finish_gradient(GATE)
         output_gradient(b["gated"], xs, False)
-
-    combine(SWISH)
-
-    @pl.when(inner)
-    def _():
         other_middle.finish()
         reduce5.start()
         hop(6, b["gated"], b["gated2"]).wait_recv()
@@ -1728,7 +1744,6 @@
 
     loop(tiles, body)
     projection_gradient(VALUE, vlow)
-    pl.when(inner)(reduce5.run2)
     pl.when(inner)(lambda: combine_inner(SWISH))
     turned_of(b["sb"])
 
@@ -1749,85 +1764,55 @@
     loop(tiles, body)
     projection_gradient(QUERY, b["qkb"], slice(0, 256))
     projection_gradient(KEY, b["qkb"], slice(256, 512))
-    reduce6 = plane_sum(outs_ref)
-
-    @pl.when(inner)
-    def _():
-        reduce5.run3()
-
-        def body(i):
-            b["cot2"][at(i, CHUNK)] = reduce5.total(i).astype(BF16)
-
-        loop(rows // CHUNK, body)
-        hop(5, b["cot2"], b["cot2"]).start()
-        reduce5.finish()
-        neighbours_may_write()
-
+    pl.when(inner)(reduce5.run2)
     combine(VALUE)
-
-    @pl.when(inner)
-    def _():
-        finish_gradient(GATE)
-        may_write()
-        reduce6.fill(lambda r, c: matmul(b["hid"][r], w[DOWN, c]))
-        combine_inner(OUTPUT)
-        reduce6.run1()
+    reduce6 = PlaneSum(place, outs_ref, xt, rows, b["rf_s"], b["rf_r"], y_first=True)
+    pl.when(inner)(lambda: finish_gradient(UP))
 
     reduce = plane_sum(part)
     reduce.fill(
         lambda r, c: nt(b["qkb"][r], w[QK, c]) + nt(vlow[r], w[VALUE, c]) + nt(swb[r], w[SWISH, c]),
         sending=outer,
     )
-    pl.when(inner)(reduce6.run2)
-    combine(QUERY)
-    pl.when(inner)(lambda: combine_inner(VALUE))
-    pl.when(outer)(lambda: finish_gradient(DOWN))
 
     @pl.when(inner)
     def _():
-        reduce6.run3()
+        reduce5.run3()
 
         def body(i):
-            b["middle"][at(i, CHUNK)] += reduce6.total(i)
+            b["cot2"][at(i, CHUNK)] = reduce5.total(i).astype(BF16)
 
         loop(rows // CHUNK, body)
-        reduce6.finish()
+        hop(5, b["cot2"], b["cot2"]).start()
+        reduce5.finish()
         neighbours_may_write()
         may_write()
         reduce.start()
 
-    pl.when(outer)(lambda: finish_gradient(GATE))
-    reduce.run1()
-    combine(KEY)
-    pl.when(inner)(lambda: combine_inner(QUERY))
-    reduce.run2()
-    finish_gradient(UP)
-    pl.when(inner)(lambda: combine_inner(KEY))
-    finish_gradient(SWISH)
-    reduce.run3()
-
-    def body(i):
-        r = at(i, CHUNK)
-        upstream = reduce.total(i)
-        hat, inverse = normalize(x_ref[r].astype(F32), EPSILON)
-        scaled = upstream * hat
-        b["pieces"][0] += scaled[0:8] + scaled[8:16]
-        b["pieces"][1] += upstream[0:8] + upstream[8:16]
-        b["back"][r] += normalize_back(upstream * gain[0:1, :], hat, inverse)
-
-    loop(rows // CHUNK, body)
-    reduce.finish()
-    delta_copy = pltpu.make_async_copy(b["back"], delta_out, b["ol"].at[2])
-    delta_copy.start()
-
-    for i in range(1, 8):
-        gain_copy(i).wait_send()
+    def delta_rows():
+        reduce.run3()
+
+        def body(i):
+            r = at(i, CHUNK)
+            upstream = reduce.total(i)
+            hat, inverse = normalize(x_ref[r].astype(F32), EPSILON)
+            scaled = upstream * hat
+            b["pieces"][0] += scaled[0:8] + scaled[8:16]
+            b["pieces"][1] += upstream[0:8] + upstream[8:16]
+            b["back"][r] += normalize_back(upstream * gain[0:1, :], hat, inverse)
+
+        loop(rows // CHUNK, body)
+        reduce.finish()
+        delta_copy().start()
+        share_gains()
+
+    def delta_copy():
+        return pltpu.make_async_copy(b["back"], delta_out, b["ol"].at[2])
+
+    def final_copy():
+        return pltpu.make_async_copy(b["middle"], final_out, b["ol"].at[1])
+
     gsend, gparts, gsum = b["gsend"], b["gparts"], b["gsum"]
-    for i in range(8):
-        for n in range(4):
-            lanes = slice(i * 256, i * 256 + 256)
-            gsend[i, n : n + 1, :] = jnp.sum(b["pieces"][n, :, lanes], axis=0, keepdims=True)
-            gsend[i, n + 4 : n + 5, :] = jnp.zeros((1, 256), F32)
 
     def share_copy(i):
         target = lax.rem(dp + i, 8)
@@ -1835,10 +1820,26 @@
             gsend.at[target], gparts.at[dp], b["gg_s"].at[i], b["gg_r"].at[dp], (target, tensor)
         )
 
-    for i in range(1, 8):
-        share_copy(i).start()
+    def share_gains():
+        for i in range(1, 8):
+            gain_copy(i).wait_send()
+        for i in range(8):
+            for n in range(4):
+                lanes = slice(i * 256, i * 256 + 256)
+                gsend[i, n : n + 1, :] = jnp.sum(b["pieces"][n, :, lanes], axis=0, keepdims=True)
+                gsend[i, n + 4 : n + 5, :] = jnp.zeros((1, 256), F32)
+        for i in range(1, 8):
+            share_copy(i).start()
+
     @pl.when(outer)
     def _():
+        finish_gradient(DOWN)
+        reduce.run1()
+        finish_gradient(GATE)
+        reduce.run2()
+        delta_rows()
+        finish_gradient(UP)
+        finish_gradient(SWISH)
         hop(2, cot_ref, b["cot2"]).wait_send()
         hop(5, b["cot2"], b["cot2"]).wait_recv()
 
@@ -1847,11 +1848,36 @@
             b["middle"][r] += b["cot2"][r].astype(F32)
 
         loop(rows // CHUNK, body)
-
-    final_copy = pltpu.make_async_copy(b["middle"], final_out, b["ol"].at[1])
-    final_copy.start()
-    finish_gradient(OUTPUT)
-    finish_gradient(VALUE)
+        final_copy().start()
+        finish_gradient(OUTPUT)
+        finish_gradient(VALUE)
+
+    @pl.when(inner)
+    def _():
+        combine_inner(OUTPUT)
+        reduce.run1()
+        combine(QUERY)
+        reduce6.fill(lambda r, c: matmul(b["hid"][r], w[DOWN, c]))
+        reduce.run2()
+        reduce6.run1()
+        combine_inner(VALUE)
+        finish_gradient(SWISH)
+        combine(KEY)
+        delta_rows()
+        reduce6.run2()
+        combine_inner(QUERY)
+        finish_gradient(OUTPUT)
+        combine_inner(KEY)
+        finish_gradient(VALUE)
+        reduce6.run3()
+
+        def body(i):
+            b["middle"][at(i, CHUNK)] += reduce6.total(i)
+
+        loop(rows // CHUNK, body)
+        reduce6.finish()
+        final_copy().start()
+
     finish_gradient(QUERY)
     acc = gsend[dp]
     for i in range(1, 8):
@@ -1875,8 +1901,8 @@
     for i in range(1, 8):
         share_copy(i).wait_send()
     gains_out[...] = (gsum[0] + gsum[1]) + (gsum[2] + gsum[3])
-    final_copy.wait()
-    delta_copy.wait()
+    final_copy().wait()
+    delta_copy().wait()
     weights_sent()
 
     @pl.when(inner)

time: 433 us -> 417 us (0.963)
  Pallas kernels: 429 us -> 414 us
    pallas_call x1, Pallas kernels: 424 us -> 409 us  [whole_layer(): pl.pallas_call(functools.partial(mega_kernel, tuple(scratch), len(args),...]
where the time goes in v6:
time: 417 us; the launch traced here: 416 us
  Pallas kernels  414 us (99%)
    pallas_call x1, Pallas kernels, whole_layer(): pl.pallas_call(functools.partial(mega_kernel, tuple(scratch), len(args),...  409 us

profile of v6, /device:TPU:8, one launch (start us, length us, event | category | flops | bytes accessed | tf_op | source)
XLA Modules:
  0.0 416.4 jit_solution(1573741448291652680)
XLA Ops:
  1.3 408.5 %whole_layer.1 = (f32[128,2048]{1,0:T(8,128)}, f32[128,2048]{1,0:T(8,128)}, f32[8,256]{1,0:T(8,128)}, bf16[256,512]{1,0:T(8,128)(2,1)}, bf16[256,512]{1,0:T(8,12...) custom-call(bf16[128,2048]{1,0:T(8,128)(2,1)} %refs_0_.1, ...), custom_call_target="tpu_custom_call" | custom-call | tf_op jit(solution)/shard_map/whole_layer/pallas_call | solution.py:1972
  409.8 1.4 fusion
  411.3 5.0 %widen.1 = (bf16[128,2048]{1,0:T(8,128)(2,1)}, f32[128,2048]{1,0:T(8,128)}, f32[256,512]{1,0:T(8,128)}, f32[256,512]{1,0:T(8,128)}, f32[256,1024]{1,0:T(8,128)},...) custom-call(s32[1]{0:T(128)S(6)} %copy.31.refs_2_.counts_ref, ...), custom_call_target="tpu_custom_call" | custom-call | tf_op jit(solution)/shard_map/widen/pallas_call | solution.py:1985

commit v7 on v6

--- a/solution.py
+++ b/solution.py
@@ -1605,10 +1605,8 @@
         reduce2.take(3)
         down_gradient(hid2, part, True)
         send_inner(DOWN)
+        reduce2.run2()
         weight_gradient(UP, xs, b["ub"], False)
-        reduce2.run2()
-        weight_gradient(GATE, outs_ref, gb2, True)
-        send_inner(GATE)
         reduce2.run3()
         for n in range(2):
 
@@ -1626,9 +1624,11 @@
         reduce3 = plane_sum(part)
         reduce3.fill(mixer_input(b["gb"], b["ub"]))
         reduce3.run1()
+        weight_gradient(GATE, outs_ref, gb2, True)
+        send_inner(GATE)
+        reduce3.run2()
         weight_gradient(UP, outs_ref, ub2, True)
         send_inner(UP)
-        reduce3.run2()
         combine_inner(DOWN)
         reduce3.run3()
 
@@ -1864,8 +1864,8 @@
         finish_gradient(SWISH)
         combine(KEY)
         delta_rows()
+        combine_inner(QUERY)
         reduce6.run2()
-        combine_inner(QUERY)
         finish_gradient(OUTPUT)
         combine_inner(KEY)
         finish_gradient(VALUE)
@@ -1981,6 +1981,7 @@
         name="whole_layer",
     )(*args)
     final_rows, delta, gain_sums = results[:3]
+    gain = shape((256,), F32)
     owned = results[3:11]
     wide = pl.pallas_call(
         widen_kernel,
@@ -1988,9 +1989,10 @@
             shape((rows, hidden), BF16),
             shape((rows, hidden), F32),
             *(shape(weight.shape, F32) for weight in weights),
+            *[gain] * 4,
         ),
-        in_specs=[scalar] + [ANY] * 10,
-        out_specs=(ANY,) * 10,
+        in_specs=[scalar, VM] + [ANY] * 10,
+        out_specs=(ANY,) * 10 + (VM,) * 4,
         scratch_shapes=[
             pltpu.VMEM((rows, hidden), F32),
             pltpu.VMEM((rows, hidden), F32),
@@ -2002,8 +2004,9 @@
         ],
         compiler_params=pltpu.CompilerParams(vmem_limit_bytes=67043328),
         name="widen",
-    )(token_counts_per_slot, final_rows, delta, *owned)
-    query, key, value, swish, output, gate, up, down = wide[2:]
+    )(token_counts_per_slot, gain_sums, final_rows, delta, *owned)
+    query, key, value, swish, output, gate, up, down = wide[2:10]
+    gain_sums = wide[10:]
     return (
         wide[0],
         wide[1],
@@ -2022,8 +2025,10 @@
     )
 
 
-def widen_kernel(counts_ref, *refs):
-    sources, targets, scratch = refs[:10], refs[10:20], refs[20:]
+def widen_kernel(counts_ref, gains_ref, *refs):
+    sources, targets, gain_refs, scratch = refs[:10], refs[10:20], refs[20:24], refs[24:]
+    for n, gain_ref in enumerate(gain_refs):
+        gain_ref[...] = gains_ref[n, :]
     final, delta, low = scratch[:3]
     narrow, wide, (came, went) = scratch[3:11], scratch[11:19], scratch[19:]
     buffers = (final, delta, *narrow)

time: 417 us -> 413 us (level)
    pallas_call x1, Pallas kernels: 409 us -> 404 us  [whole_layer(): pl.pallas_call(functools.partial(mega_kernel, tuple(scratch), len(args),...]
where the time goes in v7:
time: 413 us; the launch traced here: 412 us
  Pallas kernels  411 us (100%)
    pallas_call x1, Pallas kernels, whole_layer(): pl.pallas_call(functools.partial(mega_kernel, tuple(scratch), len(args),...  404 us

profile of v7, /device:TPU:8, one launch (start us, length us, event | category | flops | bytes accessed | tf_op | source)
XLA Modules:
  0.0 412.1 jit_solution(7465508301101883018)
XLA Ops:
  1.3 404.3 %whole_layer.1 = (f32[128,2048]{1,0:T(8,128)}, f32[128,2048]{1,0:T(8,128)}, f32[8,256]{1,0:T(8,128)}, bf16[256,512]{1,0:T(8,128)(2,1)}, bf16[256,512]{1,0:T(8,12...) custom-call(bf16[128,2048]{1,0:T(8,128)(2,1)} %refs_0_.1, ...), custom_call_target="tpu_custom_call" | custom-call | tf_op jit(solution)/shard_map/whole_layer/pallas_call | solution.py:1972
  405.6 6.3 %widen.1 = (bf16[128,2048]{1,0:T(8,128)(2,1)}, f32[128,2048]{1,0:T(8,128)}, f32[256,512]{1,0:T(8,128)}, f32[256,512]{1,0:T(8,128)}, f32[256,1024]{1,0:T(8,128)},...) custom-call(s32[1]{0:T(128)S(6)} %copy.31.refs_2_.counts_ref, ...), custom_call_target="tpu_custom_call" | custom-call | tf_op jit(solution)/shard_map/widen/pallas_call | solution.py:1986
